TPU v7x, 128 devices: a whole 4x4x4 slice. The times are simulated.
128 devices in a mesh: gx: 32 (over y, z, core), gy: 4 (over x).
Axes of the slice: x: 4, y: 4, z: 4, core: 2. Of those that a mesh axis runs over, the one named last changes fastest.
Arguments:
- emb_table: float32 [262144, 128], P(('gx', 'gy')), may hold values from -0.6 to 0.6
- row_state: float32 [262144], P(('gx', 'gy')), may hold values from 1e-05 to 0.001
- pair_mask: int32 [32], P('gx'), may hold values from 0 to 3
- look_rows: int32 [786432], P(('gx', 'gy')), may hold values from 0 to 2047
- bag_sizes: int32 [128, 2048], P(('gx', 'gy')), may hold values from 1 to 12, 6144 in all within a row
- bag_owner: int32 [262144, 1], P(('gx', 'gy')), may hold values from 0 to 127, as said below
- bag_slot: int32 [262144], P(('gx', 'gy')), may hold values from 0 to 2047, as said below
- dense_vectors: float32 [16384, 128], P(('gx', 'gy')), may hold values from -3 to 3
- labels: float32 [16384], P(('gx', 'gy')), may hold values from 0 to 1
- top_weight: float32 [264, 1024], replicated, may hold values from -0.375 to 0.375
- out_weight: float32 [1024], replicated, may hold values from -0.1875 to 0.1875
Outputs:
- moved_table: float32 [262144, 128], P(('gx', 'gy'))
- moved_state: float32 [262144], P(('gx', 'gy'))
- top_grad: float32 [264, 1024], replicated
- out_grad: float32 [1024], replicated
Inputs may be any that keep to these rules, and one draw needn't show every extreme that they name: Device (g, y) trades with device (g, y xor pair_mask[g]); 0 keeps the block. `look_rows`: a row of the block that the device holds after the trade. `bag_sizes`: each device's sizes sum to 6144. `bag_owner`: among one device's 2048 bags every owner is named either never or exactly 32 times; each owner is named so by exactly half of the devices. `bag_slot`: sample times 16 plus feature; the bags that reach one owner name every one of its slots exactly once.
All inputs are finite; a program needn't handle non-finite values.
Results may differ from a plain program's by a relative error of at most 0.0003.
Values sent between devices are 32-bit elements; how exact they have to be, the bound alone decides.
A program may use at most 64 MiB of HBM per device.

v0:
```python
from functools import partial

import jax
import jax.numpy as jnp
import numpy as np
from jax import lax
from jax.sharding import PartitionSpec as P

E = 128
F = 16
B_DEV = 128


learn_rate = 0.05
epsilon = 1e-08


def from_partner(block, axis, apart):
    count = lax.axis_size(axis)
    route = []
    for low in range(count):
        high = low | 1 << apart
        if high != low and high < count:
            route += [(low, high), (high, low)]
    return lax.ppermute(block, axis, route)


def cut_along(x, dim, count):
    before, after = (x.shape[:dim], x.shape[dim + 1 :])
    return jnp.moveaxis(x.reshape(*before, count, -1, *after), dim, 0)


def in_order(pieces, dim):
    pieces = jnp.moveaxis(pieces, 0, dim)
    shape = pieces.shape
    return pieces.reshape(*shape[:dim], shape[dim] * shape[dim + 1], *shape[dim + 2 :])


def exchange_both(x, axis, axes, splits, concats):
    sizes = [lax.axis_size(a) for a in axes]
    pieces = cut_along(x, splits[0], sizes[0])
    pieces = jnp.moveaxis(cut_along(pieces, splits[1] + 1, sizes[1]), 0, 1)
    inside = pieces.shape[2:]
    pieces = pieces.reshape(-1, *inside)
    pieces = lax.all_to_all(pieces, axis, split_axis=0, concat_axis=0, tiled=True)
    pieces = in_order(pieces.reshape(*sizes, *inside), concats[0] + 1)
    return in_order(pieces, concats[1])


def pair_terms(vectors):
    gram_all = jnp.einsum("bie,bje->bij", vectors, vectors, precision=lax.Precision.HIGHEST)
    upper_row, upper_col = np.triu_indices(F + 1, 1)
    return gram_all[:, upper_row, upper_col]


def sample_loss(pooled, dense_vectors, labels, top_weight, out_weight):
    sample_count = dense_vectors.shape[0]
    vectors = jnp.concatenate(
        [dense_vectors[:, None, :], pooled.reshape(sample_count, F, E)], axis=1
    )
    interact = jnp.concatenate([dense_vectors, pair_terms(vectors)], axis=1)
    hidden = jax.nn.silu(jnp.dot(interact, top_weight, precision=lax.Precision.HIGHEST))
    logits = jnp.dot(hidden, out_weight, precision=lax.Precision.HIGHEST)
    return jnp.sum(jax.nn.softplus(logits) - labels * logits)


def bag_index(sizes_row, lookup_count):
    ending = jnp.cumsum(sizes_row)
    positions = jnp.arange(lookup_count, dtype=jnp.int32)
    return jnp.searchsorted(ending, positions, side="right")


def trade_blocks(values, pair_value):
    result = values
    for bit_number in range(lax.axis_size("gy").bit_length() - 1):
        partner_copy = from_partner(result, "gy", bit_number)
        flipped = jnp.bitwise_and(jnp.right_shift(pair_value, bit_number), 1) == 1
        result = jax.tree.map(partial(jnp.where, flipped), partner_copy, result)
    return result


def embed_step(
    held_table,
    held_state,
    look_rows,
    bag_sizes,
    bag_owner,
    bag_slot,
    dense_vectors,
    labels,
    top_weight,
    out_weight,
):
    groups_x = lax.axis_size("gx")
    groups_y = lax.axis_size("gy")
    devices = groups_x * groups_y
    bag_count = bag_slot.shape[0]
    capacity = 2 * bag_count // devices
    bag_of = bag_index(bag_sizes[0], look_rows.shape[0])
    partial_bags = jax.ops.segment_sum(held_table[look_rows], bag_of, num_segments=bag_count)
    owners = bag_owner[:, 0]
    onehot = (owners[:, None] == jnp.arange(devices, dtype=jnp.int32)[None, :]).astype(jnp.int32)
    placed_at = jnp.sum((jnp.cumsum(onehot, axis=0) - onehot) * onehot, axis=1)
    where_to = owners * capacity + placed_at
    unused_slot = B_DEV * F
    send_rows = jnp.zeros((devices * capacity, E), jnp.float32).at[where_to].set(partial_bags)
    send_slots = jnp.full((devices * capacity,), unused_slot, jnp.int32).at[where_to].set(bag_slot)
    got_rows, got_slots = (
        exchange_both(
            send_rows.reshape(groups_x, groups_y, capacity, E),
            ("gx", "gy"),
            ("gx", "gy"),
            (0, 1),
            (0, 1),
        ),
        exchange_both(
            send_slots.reshape(groups_x, groups_y, capacity),
            ("gx", "gy"),
            ("gx", "gy"),
            (0, 1),
            (0, 1),
        ),
    )
    got_rows = got_rows.reshape(devices * capacity, E)
    got_slots = got_slots.reshape(devices * capacity)
    pooled = jax.ops.segment_sum(got_rows, got_slots, num_segments=unused_slot + 1)[:unused_slot]
    d_pooled, top_local, out_local = jax.grad(sample_loss, argnums=(0, 3, 4))(
        pooled, dense_vectors, labels, top_weight, out_weight
    )
    padded_grads = jnp.concatenate([d_pooled, jnp.zeros((1, E), jnp.float32)], axis=0)
    back_rows = padded_grads[got_slots]
    came_back = exchange_both(
        back_rows.reshape(groups_x, groups_y, capacity, E),
        ("gx", "gy"),
        ("gx", "gy"),
        (0, 1),
        (0, 1),
    )
    bag_grads = came_back.reshape(devices * capacity, E)[where_to]
    row_grad = jax.ops.segment_sum(bag_grads[bag_of], look_rows, num_segments=held_table.shape[0])
    new_state = held_state + jnp.mean(row_grad * row_grad, axis=1)
    new_table = held_table - learn_rate * row_grad / (jnp.sqrt(new_state)[:, None] + epsilon)
    top_grad, out_grad = lax.psum((top_local, out_local), ("gx", "gy"))
    return (new_table, new_state, top_grad, out_grad)


def on_device(
    emb_table,
    row_state,
    pair_mask,
    look_rows,
    bag_sizes,
    bag_owner,
    bag_slot,
    dense_vectors,
    labels,
    top_weight,
    out_weight,
):
    pair_value = pair_mask[0]
    held_table, held_state = trade_blocks((emb_table, row_state), pair_value)
    return embed_step(
        held_table,
        held_state,
        look_rows,
        bag_sizes,
        bag_owner,
        bag_slot,
        dense_vectors,
        labels,
        top_weight,
        out_weight,
    )


def solution(mesh):
    in_specs = (
        P(("gx", "gy"), None),
        P(("gx", "gy")),
        P("gx"),
        P(("gx", "gy")),
        P(("gx", "gy"), None),
        P(("gx", "gy"), None),
        P(("gx", "gy")),
        P(("gx", "gy"), None),
        P(("gx", "gy")),
        P(),
        P(),
    )
    out_specs = (P(("gx", "gy"), None), P(("gx", "gy")), P(), P())
    return jax.shard_map(
        on_device, mesh=mesh, in_specs=in_specs, out_specs=out_specs, check_vma=False
    )
```

profile of v0, /device:TPU:1, one launch (start us, length us, event | category | flops | bytes accessed | tf_op | source)
XLA Modules:
  0.0 805.5 jit_solution(9462092261142050727)
XLA Ops:
  11.9 8.2 %scatter_custom_fusion = s32[4096]{0:T(1024)S(1)} fusion(s32[2048]{0:T(1024)S(1)} %bitcast.91, s32[2048]{0:T(1024)} %param.23, s32[]{:T(128)} %constant.81.clone.1), kind=kCustom, calls=%fused_computation.72 | custom fusion | bytes 16896 | tf_op jit(solution)/shard_map/scatter | solution.py:107
  20.9 10.7 %all-to-all-start = ((s32[128,1,1,32]{3,2,1,0:T(1,128)}), s32[128,1,1,32]{3,2,1,0:T(1,128)S(1)}, u32[]{:S(2)}, u32[]{:S(2)}) async-start(s32[128,1,1,32]{3,2,1,0:T(1,128)} %bitcast.10), calls=%async_computation | async-start | bytes 131072 | tf_op jit(solution)/shard_map/all_to_all | solution.py:45
  32.9 2.9 collective-permute-start.1
  35.8 412.6 %while.24 = (s32[]{:T(128)}, u32[6144]{0:T(1024)S(1)}, u32[6144]{0:T(1024)S(1)}, s32[2048]{0:T(1024)S(1)}, s32[]{:T(128)}, /*index=5*/s32[]{:T(128)}, s32[]{}) while((s32[]{:T(128)}, u32[6144]{0:T(1024)S(1)}, u32[6144]{0:T(1024)S(1)}, s32[2048]{0:T(1024)S(1)}, s32[]{:T(128)}, /*index=5*/s32[]{:T(128)}, s32[]{}) %tuple.40), condition=%wide.region_7.8_spmd.clone, body=%wide.region_6.7_spmd.clone.sunk | while | flops 116740 | bytes 381029 | solution.py:70
  35.9 34.3 %gather_fusion = s32[6144]{0:T(1024)S(1)} fusion(s32[2048]{0:T(1024)S(1)} %get-tuple-element.145, u32[6144]{0:T(1024)S(1)} %broadcast_clamp_fusion.4), kind=kCustom, calls=%fused_computation.clone.clone.1 | custom fusion | bytes 73728 | tf_op jit(solution)/shard_map/jit(searchsorted)/jit(_searchsorted_scan_impl)/vmap(jit(_searchsorted_scan_impl))/while/body/eval_jaxpr/gather | solution.py:70
  70.2 34.3 %gather_fusion = s32[6144]{0:T(1024)S(1)} fusion(s32[2048]{0:T(1024)S(1)} %get-tuple-element.145, u32[6144]{0:T(1024)S(1)} %broadcast_clamp_fusion.4), kind=kCustom, calls=%fused_computation.clone.clone.1 | custom fusion | bytes 73728 | tf_op jit(solution)/shard_map/jit(searchsorted)/jit(_searchsorted_scan_impl)/vmap(jit(_searchsorted_scan_impl))/while/body/eval_jaxpr/gather | solution.py:70
  104.6 34.3 %gather_fusion = s32[6144]{0:T(1024)S(1)} fusion(s32[2048]{0:T(1024)S(1)} %get-tuple-element.145, u32[6144]{0:T(1024)S(1)} %broadcast_clamp_fusion.4), kind=kCustom, calls=%fused_computation.clone.clone.1 | custom fusion | bytes 73728 | tf_op jit(solution)/shard_map/jit(searchsorted)/jit(_searchsorted_scan_impl)/vmap(jit(_searchsorted_scan_impl))/while/body/eval_jaxpr/gather | solution.py:70
  139.0 34.3 %gather_fusion = s32[6144]{0:T(1024)S(1)} fusion(s32[2048]{0:T(1024)S(1)} %get-tuple-element.145, u32[6144]{0:T(1024)S(1)} %broadcast_clamp_fusion.4), kind=kCustom, calls=%fused_computation.clone.clone.1 | custom fusion | bytes 73728 | tf_op jit(solution)/shard_map/jit(searchsorted)/jit(_searchsorted_scan_impl)/vmap(jit(_searchsorted_scan_impl))/while/body/eval_jaxpr/gather | solution.py:70
  173.4 34.3 %gather_fusion = s32[6144]{0:T(1024)S(1)} fusion(s32[2048]{0:T(1024)S(1)} %get-tuple-element.145, u32[6144]{0:T(1024)S(1)} %broadcast_clamp_fusion.4), kind=kCustom, calls=%fused_computation.clone.clone.1 | custom fusion | bytes 73728 | tf_op jit(solution)/shard_map/jit(searchsorted)/jit(_searchsorted_scan_impl)/vmap(jit(_searchsorted_scan_impl))/while/body/eval_jaxpr/gather | solution.py:70
  207.8 34.3 %gather_fusion = s32[6144]{0:T(1024)S(1)} fusion(s32[2048]{0:T(1024)S(1)} %get-tuple-element.145, u32[6144]{0:T(1024)S(1)} %broadcast_clamp_fusion.4), kind=kCustom, calls=%fused_computation.clone.clone.1 | custom fusion | bytes 73728 | tf_op jit(solution)/shard_map/jit(searchsorted)/jit(_searchsorted_scan_impl)/vmap(jit(_searchsorted_scan_impl))/while/body/eval_jaxpr/gather | solution.py:70
  242.2 34.3 %gather_fusion = s32[6144]{0:T(1024)S(1)} fusion(s32[2048]{0:T(1024)S(1)} %get-tuple-element.145, u32[6144]{0:T(1024)S(1)} %broadcast_clamp_fusion.4), kind=kCustom, calls=%fused_computation.clone.clone.1 | custom fusion | bytes 73728 | tf_op jit(solution)/shard_map/jit(searchsorted)/jit(_searchsorted_scan_impl)/vmap(jit(_searchsorted_scan_impl))/while/body/eval_jaxpr/gather | solution.py:70
  276.5 34.3 %gather_fusion = s32[6144]{0:T(1024)S(1)} fusion(s32[2048]{0:T(1024)S(1)} %get-tuple-element.145, u32[6144]{0:T(1024)S(1)} %broadcast_clamp_fusion.4), kind=kCustom, calls=%fused_computation.clone.clone.1 | custom fusion | bytes 73728 | tf_op jit(solution)/shard_map/jit(searchsorted)/jit(_searchsorted_scan_impl)/vmap(jit(_searchsorted_scan_impl))/while/body/eval_jaxpr/gather | solution.py:70
  310.9 34.3 %gather_fusion = s32[6144]{0:T(1024)S(1)} fusion(s32[2048]{0:T(1024)S(1)} %get-tuple-element.145, u32[6144]{0:T(1024)S(1)} %broadcast_clamp_fusion.4), kind=kCustom, calls=%fused_computation.clone.clone.1 | custom fusion | bytes 73728 | tf_op jit(solution)/shard_map/jit(searchsorted)/jit(_searchsorted_scan_impl)/vmap(jit(_searchsorted_scan_impl))/while/body/eval_jaxpr/gather | solution.py:70
  345.3 34.3 %gather_fusion = s32[6144]{0:T(1024)S(1)} fusion(s32[2048]{0:T(1024)S(1)} %get-tuple-element.145, u32[6144]{0:T(1024)S(1)} %broadcast_clamp_fusion.4), kind=kCustom, calls=%fused_computation.clone.clone.1 | custom fusion | bytes 73728 | tf_op jit(solution)/shard_map/jit(searchsorted)/jit(_searchsorted_scan_impl)/vmap(jit(_searchsorted_scan_impl))/while/body/eval_jaxpr/gather | solution.py:70
  379.7 34.3 %gather_fusion = s32[6144]{0:T(1024)S(1)} fusion(s32[2048]{0:T(1024)S(1)} %get-tuple-element.145, u32[6144]{0:T(1024)S(1)} %broadcast_clamp_fusion.4), kind=kCustom, calls=%fused_computation.clone.clone.1 | custom fusion | bytes 73728 | tf_op jit(solution)/shard_map/jit(searchsorted)/jit(_searchsorted_scan_impl)/vmap(jit(_searchsorted_scan_impl))/while/body/eval_jaxpr/gather | solution.py:70
  414.1 34.3 %gather_fusion = s32[6144]{0:T(1024)S(1)} fusion(s32[2048]{0:T(1024)S(1)} %get-tuple-element.145, u32[6144]{0:T(1024)S(1)} %broadcast_clamp_fusion.4), kind=kCustom, calls=%fused_computation.clone.clone.1 | custom fusion | bytes 73728 | tf_op jit(solution)/shard_map/jit(searchsorted)/jit(_searchsorted_scan_impl)/vmap(jit(_searchsorted_scan_impl))/while/body/eval_jaxpr/gather | solution.py:70
  448.6 54.5 %scatter_custom_fusion.1 = f32[2048,128]{1,0:T(8,128)S(1)} fusion(s32[6144]{0:T(1024)S(1)} %convert_element_type.19, f32[2048,128]{1,0:T(8,128)S(1)} %broadcast_select_fusion.1, s32[6144]{0:T(1024)S(1)} %fusion.29, f32[]{:T(128)} %constant.78.clone.1), kind=kCustom, calls=%fused_computation.20 | custom fusion | flops 786432 | bytes 1048580 | tf_op jit(solution)/shard_map/scatter-add | solution.py:100
  503.1 7.0 scatter_custom_fusion.2
  510.2 9.7 %all-to-all-start.1 = ((f32[128,1,1,32,128]{4,3,2,1,0:T(8,128)}), f32[128,1,1,32,128]{4,3,2,1,0:T(8,128)S(1)}, u32[]{:S(2)}, u32[]{:S(2)}) async-start(f32[128,1,1,32,128]{4,3,2,1,0:T(8,128)} %bitcast.17), calls=%async_computation.1 | async-start | bytes 4194304 | tf_op jit(solution)/shard_map/all_to_all | solution.py:45
  520.8 30.0 %all-to-all-done.1 = f32[128,1,1,32,128]{4,3,2,1,0:T(8,128)S(1)} async-done(((f32[128,1,1,32,128]{4,3,2,1,0:T(8,128)}), f32[128,1,1,32,128]{4,3,2,1,0:T(8,128)S(1)}, u32[]{:S(2)}, u32[]{:S(2)}) %all-to-all-start.1) | async-done | bytes 2097184 | tf_op jit(solution)/shard_map/all_to_all | solution.py:45
  552.2 25.3 %scatter_custom_fusion.3 = f32[2049,128]{1,0:T(8,128)S(1)} fusion(s32[4096]{0:T(1024)S(1)} %reshape.189, f32[4096,128]{1,0:T(8,128)} %bitcast.79, f32[]{:T(128)} %constant.78.clone.1), kind=kCustom, calls=%fused_computation.44 | custom fusion | flops 524288 | bytes 1049600 | tf_op jit(solution)/shard_map/scatter-add | solution.py:126
  577.5 2.7 fusion.8
  585.8 8.2 %scatter_fusion = f32[128,17,17]{0,2,1:T(8,128)S(1)} fusion(f32[128,17,17]{0,2,1:T(8,128)S(1)} %broadcast_in_dim.60, s32[136]{0:T(256)S(1)} %copy-done, f32[136,128]{1,0:T(8,128)S(1)} %convolution_bitcast_fusion), kind=kCustom, calls=%fused_computation.10 | custom fusion | flops 17408 | bytes 209984 | tf_op jit(solution)/shard_map/transpose(jvp())/scatter-add | solution.py:53
  594.6 3.0 fusion.7
  597.6 2.9 fusion.6
  600.8 14.1 %gather_fusion.2 = f32[4096,128]{1,0:T(8,128)} fusion(f32[2049,128]{1,0:T(8,128)S(1)} %concatenate.15, s32[4096]{0:T(1024)S(1)} %broadcast_clamp_fusion.1), kind=kCustom, calls=%fused_computation.3 | custom fusion | bytes 4210688 | tf_op jit(solution)/shard_map/gather | solution.py:131
  614.8 3.7 all-to-all-start.2
  620.7 21.9 %collective-permute-done.2 = f32[2048]{0:T(1024)S(1)} collective-permute-done((f32[2048]{0:T(1024)S(1)}, f32[2048]{0:T(1024)S(1)}, u32[]{:S(2)}, u32[]{:S(2)}) %collective-permute-start.2) | collective-permute-done | bytes 8224 | tf_op jit(solution)/shard_map/ppermute | solution.py:25
  647.8 66.7 %psum.15 = f32[1024]{0:T(1024)} all-reduce(f32[1024]{0:T(1024)S(1)} %bitcast.95), channel_id=1, replica_groups=mesh['gx'=32,'gy'=4] {'gx','gy'}, use_global_device_ids=true, to_apply=%region_15.16 | all-reduce | flops 1024 | bytes 8192 | tf_op jit(solution)/shard_map/psum | solution.py:143
  714.5 5.5 gather_fusion.3
  719.9 51.6 %scatter_custom_fusion.5 = f32[2048,128]{1,0:T(8,128)S(1)} fusion(s32[6144]{0:T(1024)} %param.20, f32[2048,128]{1,0:T(8,128)S(1)} %gather_fusion.3, s32[6144]{0:T(1024)} %fusion.30, f32[]{:T(128)} %constant.78.clone.1), kind=kCustom, calls=%fused_computation.18 | custom fusion | flops 786432 | bytes 1049088 | tf_op jit(solution)/shard_map/scatter-add | solution.py:140
  773.8 22.5 %all-reduce.3.cloned.1.call-done = f32[264,1024]{1,0:T(8,128)} async-done(((f32[264,1024]{1,0:T(8,128)}), f32[264,1024]{1,0:T(8,128)}) %all-reduce.3.cloned.1.call-update) | async-done | bytes 1081360 | tf_op jit(solution)/shard_map/psum | solution.py:143
  (131 shorter events, 27.3 us)
Async XLA Ops:
  7.2 25.6 %collective-permute-start = (f32[2048,128]{1,0:T(8,128)}, f32[2048,128]{1,0:T(8,128)S(1)}, u32[]{:S(2)}, u32[]{:S(2)}) collective-permute-start(f32[2048,128]{1,0:T(8,128)} %param.17), channel_id=1, source_target_pairs={{0,1},{1,0},{2,3},{3,2},{4,5},{5,4},{6,7},{7,6},{8,9},{9,8},{10,11... | collective-permute-start | bytes 3145736 | tf_op jit(solution)/shard_map/ppermute | solution.py:25
  10.5 0.7 copy-start.8
  10.6 21.6 %copy-start.11 = (s32[1,2048]{1,0:T(1,128)S(1)}, s32[1,2048]{1,0:T(1,128)}, u32[]{:S(2)}) copy-start(s32[1,2048]{1,0:T(1,128)} %param.21) | copy-start | bytes 24580
  10.6 22.2 %copy-start.6 = (f32[2048,128]{1,0:T(8,128)S(1)}, f32[2048,128]{1,0:T(8,128)}, u32[]{:S(2)}) copy-start(f32[2048,128]{1,0:T(8,128)} %param.17) | copy-start | bytes 3145732
  20.9 489.3 %all-to-all-start = ((s32[128,1,1,32]{3,2,1,0:T(1,128)}), s32[128,1,1,32]{3,2,1,0:T(1,128)S(1)}, u32[]{:S(2)}, u32[]{:S(2)}) async-start(s32[128,1,1,32]{3,2,1,0:T(1,128)} %bitcast.10), calls=%async_computation | async-start | bytes 131072 | tf_op jit(solution)/shard_map/all_to_all | solution.py:45
  32.9 415.6 %collective-permute-start.1 = (f32[2048,128]{1,0:T(8,128)S(1)}, f32[2048,128]{1,0:T(8,128)S(1)}, u32[]{:S(2)}, u32[]{:S(2)}) collective-permute-start(f32[2048,128]{1,0:T(8,128)S(1)} %broadcast_select_fusion), channel_id=1, source_target_pairs={{0,2},{2,0},{1,3},{3,1},{4,6},{6,4},{5,7},{7,5},{8,10},{10,8},{9,1... | collective-permute-start | bytes 3145736 | tf_op jit(solution)/shard_map/ppermute | solution.py:25
  35.8 412.6 %copy-start.9 = (s32[6144]{0:T(1024)S(1)}, s32[6144]{0:T(1024)}, u32[]{:S(2)}) copy-start(s32[6144]{0:T(1024)} %param.20) | copy-start | bytes 73732
  448.6 61.6 %copy-start.1 = (f32[2048,128]{1,0:T(8,128)}, f32[2048,128]{1,0:T(8,128)S(1)}, u32[]{:S(2)}) copy-start(f32[2048,128]{1,0:T(8,128)S(1)} %broadcast_select_fusion.1) | copy-start | bytes 3145732
  510.2 9.7 %copy-start.5 = (f32[128,128]{1,0:T(8,128)S(1)}, f32[128,128]{1,0:T(8,128)}, u32[]{:S(2)}) copy-start(f32[128,128]{1,0:T(8,128)} %param.24) | copy-start | bytes 196612
  510.2 40.6 %all-to-all-start.1 = ((f32[128,1,1,32,128]{4,3,2,1,0:T(8,128)}), f32[128,1,1,32,128]{4,3,2,1,0:T(8,128)S(1)}, u32[]{:S(2)}, u32[]{:S(2)}) async-start(f32[128,1,1,32,128]{4,3,2,1,0:T(8,128)} %bitcast.17), calls=%async_computation.1 | async-start | bytes 4194304 | tf_op jit(solution)/shard_map/all_to_all | solution.py:45
  550.8 1.4 copy-start.3
  577.5 3.1 copy-start
  580.6 1.8 copy-start.4
  580.6 3.7 copy-start.12
  580.6 3.7 copy-start.13
  614.8 3.8 copy-start.10
  614.8 30.2 %copy-start.7 = (f32[128,128]{0,1:T(8,128)S(1)}, f32[128,128]{0,1:T(8,128)}, u32[]{:S(2)}) copy-start(f32[128,128]{0,1:T(8,128)} %copy.34) | copy-start | bytes 196612
  614.8 99.6 %all-to-all-start.2 = ((f32[128,1,1,32,128]{4,3,2,1,0:T(8,128)}), f32[128,1,1,32,128]{4,3,2,1,0:T(8,128)S(1)}, u32[]{:S(2)}, u32[]{:S(2)}) async-start(f32[128,1,1,32,128]{4,3,2,1,0:T(8,128)} %bitcast.77), calls=%async_computation.2 | async-start | bytes 4194304 | tf_op jit(solution)/shard_map/all_to_all | solution.py:45
  618.6 177.7 %all-reduce.3.cloned.1.call-start = ((), (), s32[]{:S(2)}) async-start(), calls=%async_computation.3 | async-start | bytes 2162688 | tf_op jit(solution)/shard_map/psum | solution.py:143
  618.7 24.0 %collective-permute-start.2 = (f32[2048]{0:T(1024)S(1)}, f32[2048]{0:T(1024)S(1)}, u32[]{:S(2)}, u32[]{:S(2)}) collective-permute-start(f32[2048]{0:T(1024)S(1)} %copy-done.10), channel_id=1, source_target_pairs={{0,1},{1,0},{2,3},{3,2},{4,5},{5,4},{6,7},{7,6},{8,9},{9,8},{10,11... | collective-permute-start | bytes 24584 | tf_op jit(solution)/shard_map/ppermute | solution.py:25
  642.6 129.2 %collective-permute-start.3 = (f32[2048]{0:T(1024)S(1)}, f32[2048]{0:T(1024)S(1)}, u32[]{:S(2)}, u32[]{:S(2)}) collective-permute-start(f32[2048]{0:T(1024)S(1)} %broadcast_select_fusion.2), channel_id=1, source_target_pairs={{0,2},{2,0},{1,3},{3,1},{4,6},{6,4},{5,7},{7,5},{8,10},{10,8},{9,1... | collective-permute-start | bytes 24584 | tf_op jit(solution)/shard_map/ppermute | solution.py:25
  719.9 52.6 %copy-start.2 = (f32[2048,128]{1,0:T(8,128)S(1)}, f32[2048,128]{1,0:T(8,128)}, u32[]{:S(2)}) copy-start(f32[2048,128]{1,0:T(8,128)} %copy-done.1) | copy-start | bytes 3145732
Sparse Core Ops, SparseCore 0:
  647.4 148.8 all-reduce.2
where the time goes:
time: 806 us; the launch traced here: 805 us
  local copies, waits for them, and re-layouts  456 us (57%)
  other arithmetic  145 us (18%)
  waiting for transfers between devices  74.4 us (9%)
  blocking collectives  66.7 us (8%)
  starting transfers between devices  33 us (4%)
  between operations  15.1 us (2%)
  matrix products  14.6 us (2%)
    gather x12, local copies, waits for them, and re-layouts, bag_index(): return jnp.searchsorted(ending, positions, side='right')  411 us
    psum x1, blocking collectives, embed_step(): top_grad, out_grad = lax.psum((top_local, out_local), ('gx', 'gy'))  66.7 us
    scatter-add x1, other arithmetic, embed_step(): jax.ops.segment_sum(held_table[look_rows], bag_of, num_segments=bag_count)  54.5 us
    scatter-add x1, other arithmetic, embed_step(): jax.ops.segment_sum(bag_grads[bag_of], look_rows, num_segments=held_table...  51.6 us
    all_to_all x3, waiting for transfers between devices, exchange_both(): lax.all_to_all(pieces, axis, split_axis=0, concat_axis=0, tiled=True)  30 us
    scatter-add x1, other arithmetic, embed_step(): jax.ops.segment_sum(got_rows, got_slots, num_segments=unused_slot + 1)  25.3 us
    all_to_all x3, starting transfers between devices, exchange_both(): lax.all_to_all(pieces, axis, split_axis=0, concat_axis=0, tiled=True)  24.1 us
    psum x1, waiting for transfers between devices, embed_step(): top_grad, out_grad = lax.psum((top_local, out_local), ('gx', 'gy'))  22.5 us
  transfers between devices with their start and end apart: 8, of which 3 were waited for; matrix products, arithmetic and copies ran while one was open for 68% of the time, Pallas kernels for 0%

commit v1 on v0

v1 whole, which is shorter than its diff:
```python
import jax
import jax.numpy as jnp
from jax import lax
from jax.experimental import pallas as pl
from jax.experimental.pallas import tpu as pltpu
from jax.sharding import PartitionSpec as P

E = 128
F = 16
B_DEV = 128
BAGS = 2048
ROWS = 2048
LOOKS = 6144
DEVICES = 128
CAP = 32
INTER = 264
HID = 1024
CHUNK = 256
SPAN = CHUNK + 16
C_ROWS = 2304
PAIRS = [(i, j) for i in range(F + 1) for j in range(i + 1, F + 1)]
PAIR_ROW = {pair: 128 + n for n, pair in enumerate(PAIRS)}

learn_rate = 0.05
epsilon = 1e-08
f32, bf16, i32 = jnp.float32, jnp.bfloat16, jnp.int32

VMEM = pl.BlockSpec(memory_space=pltpu.VMEM)
SMEM = pl.BlockSpec(memory_space=pltpu.SMEM)


def split(x):
    hi = x.astype(bf16)
    return hi, (x - hi.astype(f32)).astype(bf16)


def mxu(a, b, dims):
    return lax.dot_general(a, b, (dims, ((), ())), preferred_element_type=f32)


def dot3(a, b, dims):
    return mxu(a[0], b[0], dims) + (mxu(a[0], b[1], dims) + mxu(a[1], b[0], dims))


NN = ((1,), (0,))
NT = ((1,), (1,))


def down_sublanes(row):
    return jnp.broadcast_to(row, (128, 128)).T


def count_kernel(first_ref, look_ref, start_ref, end_ref, c_ref, start_t, end_t):
    for r in range(C_ROWS // 128):
        here = slice(r * 128, (r + 1) * 128)
        start_t[here, :] = down_sublanes(start_ref[r : r + 1, :])
        end_t[here, :] = down_sublanes(end_ref[r : r + 1, :])
    c_ref[0:16, :] = jnp.zeros((16, ROWS), bf16)
    lane = lax.broadcasted_iota(i32, (1, 128), 1)

    def chunk(t, carry):
        at = pl.multiple_of(first_ref[t], 16)
        start, end = start_t[pl.ds(at, SPAN), :], end_t[pl.ds(at, SPAN), :]
        halves, columns = [], []
        for h in range(2):
            k = lane + (t * CHUNK + h * 128)
            halves.append(((start <= k) & (k < end)).astype(f32).astype(bf16))
            columns.append(down_sublanes(look_ref[pl.ds(2 * t + h, 1), :]))
        in_bag = jnp.concatenate(halves, axis=1)
        column = jnp.concatenate(columns, axis=0)
        for n in range(0, 16, 4):
            of_row = jnp.concatenate(
                [(column == lane + 128 * q).astype(f32).astype(bf16) for q in range(n, n + 4)],
                axis=1,
            )
            counts = mxu(in_bag, of_row, NN)
            cols = slice(n * 128, (n + 4) * 128)
            before = c_ref[pl.ds(at, 16), cols].astype(f32)
            c_ref[pl.ds(at, 16), cols] = (counts[:16] + before).astype(bf16)
            c_ref[pl.ds(pl.multiple_of(at + 16, 16), SPAN - 16), cols] = counts[16:].astype(bf16)
        return carry

    lax.fori_loop(0, LOOKS // CHUNK, chunk, 0)


def pool_kernel(where_ref, c_ref, table_ref, send_ref, split_ref, partial_ref):
    hi, lo = split(table_ref[...])
    split_ref[:, :128] = hi
    split_ref[:, 128:] = lo

    def block(m, carry):
        at = pl.multiple_of(m * 256, 256)
        both = mxu(c_ref[pl.ds(at, 256), :], split_ref[...], NN)
        partial_ref[pl.ds(at, 256), :] = both[:, :128] + both[:, 128:]
        return carry

    lax.fori_loop(0, BAGS // 256, block, 0)

    def place(n, carry):
        for u in range(16):
            b = n * 16 + u
            send_ref[pl.ds(where_ref[b], 1), :] = partial_ref[pl.ds(b, 1), :]
        return carry

    lax.fori_loop(0, BAGS // 16, place, 0)


def dense_kernel(
    slot_ref, got_ref, dense_ref, label_ref, w_ref, wo_ref, back_ref, grad_ref, pooled, vt, inter_t
):
    def place(c, carry):
        @pl.when(slot_ref[c * CAP] < BAGS)
        def _():
            for u in range(CAP):
                p = c * CAP + u
                pooled[pl.ds(slot_ref[p], 1), :] = got_ref[pl.ds(p, 1), :]

        return carry

    lax.fori_loop(0, DEVICES, place, 0)

    dense_t = dense_ref[...].T
    vt[0] = dense_t
    inter_t[0:128, :] = dense_t
    for f in range(F):
        vt[f + 1] = pooled[f * 128 : (f + 1) * 128, :].T
    for i in range(F):
        for j in range(i + 1, F + 1):
            row = PAIR_ROW[i, j]
            inter_t[row : row + 1, :] = jnp.sum(vt[i] * vt[j], axis=0, keepdims=True)

    it = inter_t[...]
    w = split(w_ref[...])
    pre = dot3(split(it.T), w, NN)
    sig = 1.0 / (1.0 + jnp.exp(-pre))
    hidden = pre * sig
    logits = jnp.sum(hidden * wo_ref[...], axis=1, keepdims=True)
    d_logits = 1.0 / (1.0 + jnp.exp(-logits)) - label_ref[...]
    grad_ref[INTER : INTER + 8, :] = jnp.broadcast_to(
        jnp.sum(hidden * d_logits, axis=0, keepdims=True), (8, HID)
    )
    d_pre = split(d_logits * wo_ref[...] * (sig * (1.0 + pre * (1.0 - sig))))
    grad_ref[0:INTER, :] = dot3(split(it), d_pre, NN)
    inter_t[...] = dot3(w, d_pre, NT)

    for j in range(1, F + 1):
        total = None
        for i in range(F + 1):
            if i != j:
                row = PAIR_ROW[min(i, j), max(i, j)]
                term = inter_t[row : row + 1, :] * vt[i]
                total = term if total is None else total + term
        pooled[(j - 1) * 128 : j * 128, :] = total.T

    def give(c, carry):
        @pl.when(slot_ref[c * CAP] < BAGS)
        def _():
            for u in range(CAP):
                p = c * CAP + u
                back_ref[pl.ds(p, 1), :] = pooled[pl.ds(slot_ref[p], 1), :]

        return carry

    lax.fori_loop(0, DEVICES, give, 0)


def update_kernel(
    where_ref, c_ref, came_ref, table_ref, state_ref, new_table_ref, new_state_ref, grads, sides
):
    def take(n, carry):
        for u in range(16):
            b = n * 16 + u
            grads[pl.ds(b, 1), :] = came_ref[pl.ds(where_ref[b], 1), :]
        return carry

    lax.fori_loop(0, BAGS // 16, take, 0)
    for q in range(BAGS // 128):
        here = slice(q * 128, (q + 1) * 128)
        hi, lo = split(grads[here, :].T)
        sides[0:128, here] = hi
        sides[128:256, here] = lo

    def block(n, carry):
        here = pl.ds(pl.multiple_of(n * 256, 256), 256)
        both = mxu(sides[...], c_ref[0:BAGS, here], NN)
        row_grad = both[:128] + both[128:]
        state = state_ref[:, here] + jnp.sum(row_grad * row_grad, axis=0, keepdims=True) * (1.0 / E)
        new_state_ref[:, here] = state
        step = row_grad * (learn_rate / (jnp.sqrt(state) + epsilon))
        new_table_ref[here, :] = table_ref[here, :] - step.T
        return carry

    lax.fori_loop(0, ROWS // 256, block, 0)


def params(**kw):
    return pltpu.CompilerParams(**kw)


def from_partner(block, flip):
    return lax.ppermute(block, "gy", [(y, y ^ flip) for y in range(4)])


def trade_blocks(table, state, mask):
    first, second = (mask == 1) | (mask == 2), mask >= 2
    cut = ROWS // 2
    pieces = [table[:cut], jnp.concatenate([table[cut:], state.reshape(16, 128)], axis=0)]
    out = []
    for piece in pieces:
        piece = jnp.where(first, from_partner(piece, 1), piece)
        piece = jnp.where(second, from_partner(piece, 3), piece)
        out.append(piece)
    held = jnp.concatenate([out[0], out[1][:cut]], axis=0)
    return held, out[1][cut:].reshape(1, ROWS)


def swap_all(x):
    return lax.all_to_all(x, ("gx", "gy"), split_axis=0, concat_axis=0, tiled=True)


def on_device(
    emb_table,
    row_state,
    pair_mask,
    look_rows,
    bag_sizes,
    bag_owner,
    bag_slot,
    dense_vectors,
    labels,
    top_weight,
    out_weight,
):
    held, held_state = trade_blocks(emb_table, row_state, pair_mask[0])

    owners = bag_owner[:, 0]
    onehot = (owners[:, None] == jnp.arange(DEVICES, dtype=i32)[None, :]).astype(i32)
    placed_at = jnp.sum((jnp.cumsum(onehot, axis=0) - onehot) * onehot, axis=1)
    where_to = owners * CAP + placed_at
    spot = (placed_at[:, None] == jnp.arange(CAP, dtype=i32)[None, :]).astype(f32)
    sample, feature = bag_slot // F, bag_slot % F
    parts = jnp.concatenate(
        [spot * (sample.astype(f32)[:, None]), spot * ((feature + 1).astype(f32)[:, None])], axis=1
    )
    coded = mxu(onehot.astype(bf16), parts.astype(bf16), ((0,), (0,))).astype(i32)
    sample_at, feature_at = coded[:, :CAP], coded[:, CAP:]
    send_slots = jnp.where(feature_at > 0, (feature_at - 1) * B_DEV + sample_at, BAGS)
    got_slots = swap_all(send_slots).reshape(DEVICES * CAP)

    sizes = bag_sizes[0]
    ends = jnp.cumsum(sizes)
    starts = ends - sizes
    bounds = jnp.arange(LOOKS // CHUNK, dtype=i32) * CHUNK
    first_bag = jnp.sum((ends[None, :] <= bounds[:, None]).astype(i32), axis=1) // 16 * 16
    extra = C_ROWS - BAGS
    ends2 = jnp.concatenate([ends, jnp.zeros((extra,), i32)]).reshape(C_ROWS // 128, 128)
    starts2 = jnp.concatenate([starts, jnp.full((extra,), LOOKS, i32)]).reshape(C_ROWS // 128, 128)
    counts = pl.pallas_call(
        count_kernel,
        out_shape=jax.ShapeDtypeStruct((C_ROWS, ROWS), bf16),
        in_specs=[SMEM, VMEM, VMEM, VMEM],
        out_specs=VMEM,
        scratch_shapes=[pltpu.VMEM((C_ROWS, 128), i32), pltpu.VMEM((C_ROWS, 128), i32)],
        compiler_params=params(vmem_limit_bytes=24 << 20),
        cost_estimate=pl.CostEstimate(flops=2 * LOOKS * SPAN * ROWS, bytes_accessed=10 << 20, transcendentals=0),
        name="count",
    )(first_bag, look_rows.reshape(LOOKS // 128, 128), starts2, ends2)

    send_rows = pl.pallas_call(
        pool_kernel,
        out_shape=jax.ShapeDtypeStruct((DEVICES * CAP, E), f32),
        in_specs=[SMEM, VMEM, VMEM],
        out_specs=VMEM,
        scratch_shapes=[pltpu.VMEM((ROWS, 256), bf16), pltpu.VMEM((BAGS, E), f32)],
        compiler_params=params(vmem_limit_bytes=24 << 20),
        name="pool",
    )(where_to, counts, held)
    got_rows = swap_all(send_rows.reshape(DEVICES, CAP, E)).reshape(DEVICES * CAP, E)

    back_rows, grads = pl.pallas_call(
        dense_kernel,
        out_shape=(
            jax.ShapeDtypeStruct((DEVICES * CAP, E), f32),
            jax.ShapeDtypeStruct((INTER + 8, HID), f32),
        ),
        in_specs=[SMEM, VMEM, VMEM, VMEM, VMEM, VMEM],
        out_specs=(VMEM, VMEM),
        scratch_shapes=[
            pltpu.VMEM((BAGS, E), f32),
            pltpu.VMEM((F + 1, E, B_DEV), f32),
            pltpu.VMEM((INTER, B_DEV), f32),
        ],
        compiler_params=params(vmem_limit_bytes=24 << 20),
        name="dense",
    )(got_slots, got_rows, dense_vectors, labels[:, None], top_weight, out_weight[None, :])

    came_back = swap_all(back_rows.reshape(DEVICES, CAP, E)).reshape(DEVICES * CAP, E)
    total = lax.psum(grads[: INTER + 1], ("gx", "gy"))

    new_table, new_state = pl.pallas_call(
        update_kernel,
        out_shape=(
            jax.ShapeDtypeStruct((ROWS, E), f32),
            jax.ShapeDtypeStruct((1, ROWS), f32),
        ),
        in_specs=[SMEM, VMEM, VMEM, VMEM, VMEM],
        out_specs=(VMEM, VMEM),
        scratch_shapes=[pltpu.VMEM((BAGS, E), f32), pltpu.VMEM((2 * E, BAGS), bf16)],
        compiler_params=params(vmem_limit_bytes=24 << 20),
        name="update",
    )(where_to, counts, came_back, held, held_state)
    return new_table, new_state.reshape(ROWS), total[:INTER], total[INTER]


def solution(mesh):
    both = ("gx", "gy")
    in_specs = (
        P(both, None),
        P(both),
        P("gx"),
        P(both),
        P(both, None),
        P(both, None),
        P(both),
        P(both, None),
        P(both),
        P(),
        P(),
    )
    out_specs = (P(both, None), P(both), P(), P())
    return jax.shard_map(
        on_device, mesh=mesh, in_specs=in_specs, out_specs=out_specs, check_vma=False
    )
```

time: 806 us -> 318 us (0.39)
  local copies, waits for them, and re-layouts: 456 us -> 21.6 us
  other arithmetic: 145 us -> 5.26 us
  waiting for transfers between devices: 74.4 us -> 200 us
  blocking collectives: 66.7 us -> 0 us
  Pallas kernels: 0 us -> 42.7 us
  matrix products: 14.6 us -> 0.88 us
    gather x15 -> x0, local copies, waits for them, and re-layouts: 433 us -> none  [the longest x12 411 us: bag_index(): return jnp.searchsorted(ending, positions, side='right')]
    scatter-add x4 -> x0, other arithmetic: 140 us -> none  [the longest x1 54.5 us: embed_step(): jax.ops.segment_sum(held_table[look_rows], bag_of, num_segments=bag_count)]
    psum x1, waiting for transfers between devices: 22.5 us -> 160 us  [on_device(): total = lax.psum(grads[:INTER + 1], ('gx', 'gy'))]
    psum x1 -> x0, blocking collectives: 66.7 us -> none  [embed_step(): top_grad, out_grad = lax.psum((top_local, out_local), ('gx', 'gy'))]
    pallas_call x0 -> x4, Pallas kernels: none -> 42.7 us  [the longest x1 16 us: on_device(): pl.pallas_call(count_kernel, out_shape=jax.ShapeDtypeStruct((C_ROWS, ROWS...]
    scatter x2 -> x0, local copies, waits for them, and re-layouts: 15.3 us -> none  [the longest x1 8.23 us: embed_step(): jnp.full((devices * capacity,), unused_slot, jnp.int32).at[where_to]]
    dot_general x8 -> x1, matrix products: 14.6 us -> 0.88 us  [mxu(): return lax.dot_general(a, b, (dims, ((), ())), preferred_element_type=f32)]
    ppermute x4, waiting for transfers between devices: 21.9 us -> 9.16 us  [from_partner(): return lax.ppermute(block, 'gy', [(y, y ^ flip) for y in range(4)])]
  transfers between devices with their start and end apart: 8 -> 8, of which waited for: 3 -> 3; matrix products, arithmetic and copies ran while one was open for 68% -> 4% of each run, Pallas kernels for 0% -> 7%
where the time goes in v1:
time: 318 us; the launch traced here: 317 us
  waiting for transfers between devices  200 us (63%)
  Pallas kernels  42.7 us (13%)
  starting transfers between devices  31.7 us (10%)
  local copies, waits for them, and re-layouts  21.6 us (7%)
  between operations  15 us (5%)
  other arithmetic  5.26 us (2%)
    psum x1, waiting for transfers between devices, on_device(): total = lax.psum(grads[:INTER + 1], ('gx', 'gy'))  160 us
    all_to_all x3, waiting for transfers between devices, swap_all(): lax.all_to_all(x, ('gx', 'gy'), split_axis=0, concat_axis=0, tiled=True)  29.4 us
    all_to_all x3, starting transfers between devices, swap_all(): lax.all_to_all(x, ('gx', 'gy'), split_axis=0, concat_axis=0, tiled=True)  22.9 us
    pallas_call x1, Pallas kernels, on_device(): pl.pallas_call(count_kernel, out_shape=jax.ShapeDtypeStruct((C_ROWS, ROWS...  16 us
    unnamed x30, local copies, waits for them, and re-layouts  13.3 us
    pallas_call x1, Pallas kernels, on_device(): pl.pallas_call(dense_kernel, out_shape=(jax.ShapeDtypeStruct((DEVICES * C...  11.4 us
    ppermute x4, waiting for transfers between devices, from_partner(): return lax.ppermute(block, 'gy', [(y, y ^ flip) for y in range(4)])  9.16 us
    pallas_call x1, Pallas kernels, on_device(): pl.pallas_call(update_kernel, out_shape=(jax.ShapeDtypeStruct((ROWS, E),...  8.84 us
  transfers between devices with their start and end apart: 8, of which 3 were waited for; matrix products, arithmetic and copies ran while one was open for 4% of the time, Pallas kernels for 7%

profile of v1, /device:TPU:1, one launch (start us, length us, event | category | flops | bytes accessed | tf_op | source)
XLA Modules:
  0.0 316.8 jit_solution(14254019128489507972)
XLA Ops:
  7.2 1.1 slice.46
  8.2 2.1 collective-permute-start
  10.4 0.7 fusion.11
  11.1 0.8 copy.25
  13.6 1.6 select_convert_fusion.1
  15.2 0.9 convolution_convert_fusion
  16.1 0.7 copy.27
  16.9 10.7 %all-to-all-start = ((s32[128,1,32]{2,1,0:T(1,128)}), s32[128,1,32]{2,1,0:T(1,128)S(1)}, u32[]{:S(2)}, u32[]{:S(2)}) async-start(s32[128,1,32]{2,1,0:T(1,128)} %copy.27), calls=%async_computation | async-start | bytes 131072 | tf_op jit(solution)/shard_map/all_to_all | solution.py:218
  29.0 1.4 collective-permute-start.2
  30.6 1.9 collective-permute-start.1
  32.5 9.2 %collective-permute-done.2 = f32[1040,128]{1,0:T(8,128)S(1)} collective-permute-done((f32[1040,128]{1,0:T(8,128)S(1)}, f32[1040,128]{1,0:T(8,128)S(1)}, u32[]{:S(2)}, u32[]{:S(2)}) %collective-permute-start.2) | collective-permute-done | bytes 532512 | tf_op jit(solution)/shard_map/ppermute | solution.py:201
  41.7 3.3 %collective-permute-start.3 = (f32[1040,128]{1,0:T(8,128)S(1)}, f32[1040,128]{1,0:T(8,128)S(1)}, u32[]{:S(2)}, u32[]{:S(2)}) collective-permute-start(f32[1040,128]{1,0:T(8,128)S(1)} %broadcast_select_fusion), channel_id=1, source_target_pairs={{0,3},{1,2},{2,1},{3,0},{4,7},{5,6},{6,5},{7,4},{8,11},{9,10},{10,... | collective-permute-start | bytes 1597448 | tf_op jit(solution)/shard_map/ppermute | solution.py:201
  45.0 16.0 %count.1.c_ref = bf16[2304,2048]{1,0:T(8,128)(2,1)S(1)} custom-call(s32[24]{0:T(128)S(1)} %fusion.16.first_ref, s32[48,128]{1,0:T(8,128)S(1)} %bitcast.40, s32[18,128]{1,0:T(8,128)S(1)} %get-tuple-element.21.start_ref, s32[18,128]{1,0:T(8,128)S(1)} %get-tuple-element.20.end_ref), custom_call_target="tpu_custom_call" | custom-call | flops 6845104128 | bytes 10485760 | tf_op jit(solution)/shard_map/count/pallas_call | solution.py:258
  61.2 0.8 copy-done.10
  62.1 6.5 %pool.1 = f32[4096,128]{1,0:T(8,128)S(1)} custom-call(s32[2048]{0:T(1024)S(1)} %multiply_add_fusion.where_ref, bf16[2304,2048]{1,0:T(8,128)(2,1)S(1)} %count.1.c_ref, f32[2048,128]{1,0:T(8,128)S(1)} %pad_maximum_fusion.table_ref), custom_call_target="tpu_custom_call" | custom-call | tf_op jit(solution)/shard_map/pool/pallas_call | solution.py:269
  68.7 3.6 %copy-done = bf16[2304,2048]{1,0:T(8,128)(2,1)} copy-done((bf16[2304,2048]{1,0:T(8,128)(2,1)}, bf16[2304,2048]{1,0:T(8,128)(2,1)S(1)}, u32[]{:S(2)}) %copy-start) | copy-done | bytes 9437208
  72.3 1.3 copy-done.2
  73.6 8.7 %all-to-all-start.1 = ((f32[128,32,128]{2,1,0:T(8,128)}), f32[128,32,128]{2,1,0:T(8,128)S(1)}, u32[]{:S(2)}, u32[]{:S(2)}) async-start(f32[128,32,128]{2,1,0:T(8,128)} %bitcast.35), calls=%async_computation.1 | async-start | bytes 4194304 | tf_op jit(solution)/shard_map/all_to_all | solution.py:218
  82.9 0.8 reduce.5
  83.8 29.4 %all-to-all-done.1 = f32[128,32,128]{2,1,0:T(8,128)S(1)} async-done(((f32[128,32,128]{2,1,0:T(8,128)}), f32[128,32,128]{2,1,0:T(8,128)S(1)}, u32[]{:S(2)}, u32[]{:S(2)}) %all-to-all-start.1) | async-done | bytes 2097184 | tf_op jit(solution)/shard_map/all_to_all | solution.py:218
  113.3 1.2 copy-done.5
  114.5 11.4 %dense.1 = (f32[4096,128]{1,0:T(8,128)S(1)}, f32[272,1024]{1,0:T(8,128)S(1)}) custom-call(s32[4096]{0:T(1024)S(1)} %reshape.107.slot_ref, f32[4096,128]{1,0:T(8,128)S(1)} %bitcast.33, f32[128,128]{1,0:T(8,128)S(1)} %copy-done.6, f32[128,1]{1,0:T(8,128)S(1)} %copy.28.label_ref, f32[264,1024]{1,0:T(8,128)S(1)} %copy-done.5, f32[1,1024]{1,0:T(1,128)S(1)} %bitcast.39), custom_call_target="tpu_custom_call" | custom-call | tf_op jit(solution)/shard_map/dense/pallas_call | solution.py:280
  125.9 1.3 copy-done.3
  127.2 1.1 copy-done.4
  128.3 3.6 %all-to-all-start.2 = ((f32[128,32,128]{2,1,0:T(8,128)}), f32[128,32,128]{2,1,0:T(8,128)S(1)}, u32[]{:S(2)}, u32[]{:S(2)}) async-start(f32[128,32,128]{2,1,0:T(8,128)} %bitcast.36), calls=%async_computation.2 | async-start | bytes 4194304 | tf_op jit(solution)/shard_map/all_to_all | solution.py:218
  131.9 0.7 all-reduce.4.cloned.1.call-update
  132.6 0.7 slice.60
  133.3 160.5 %all-reduce.4.cloned.1.call-done = f32[265,1024]{1,0:T(8,128)} async-done(((f32[265,1024]{1,0:T(8,128)}), f32[265,1024]{1,0:T(8,128)}) %all-reduce.4.cloned.1.call-update) | async-done | bytes 1085456 | tf_op jit(solution)/shard_map/psum | solution.py:298
  293.8 1.4 slice.62
  295.1 2.3 slice.61
  297.5 3.7 %copy-done.1 = bf16[2304,2048]{1,0:T(8,128)(2,1)S(1)} copy-done((bf16[2304,2048]{1,0:T(8,128)(2,1)S(1)}, bf16[2304,2048]{1,0:T(8,128)(2,1)}, u32[]{:S(2)}) %copy-start.1) | copy-done | bytes 9437208
  301.1 8.8 %update.1 = (f32[2048,128]{1,0:T(8,128)}, f32[1,2048]{1,0:T(1,128)}) custom-call(s32[2048]{0:T(1024)S(1)} %multiply_add_fusion.where_ref, bf16[2304,2048]{1,0:T(8,128)(2,1)S(1)} %copy-done.1, f32[4096,128]{1,0:T(8,128)S(1)} %bitcast.34, f32[2048,128]{1,0:T(8,128)S(1)} %pad_maximum_fusion.table_ref, f32[1,2048]{1,0:T(1,128)S(1)} %bitcast.38), custom_call_target="tpu_custom_call" | custom-call | tf_op jit(solution)/shard_map/update/pallas_call | solution.py:300
  (57 shorter events, 3.7 us)
Async XLA Ops:
  8.2 20.5 %collective-permute-start = (f32[1024,128]{1,0:T(8,128)S(1)}, f32[1024,128]{1,0:T(8,128)S(1)}, u32[]{:S(2)}, u32[]{:S(2)}) collective-permute-start(f32[1024,128]{1,0:T(8,128)S(1)} %slice.46), channel_id=1, source_target_pairs={{0,1},{1,0},{2,3},{3,2},{4,5},{5,4},{6,7},{7,6},{8,9},{9,8},{10,11... | collective-permute-start | bytes 1572872 | tf_op jit(solution)/shard_map/ppermute | solution.py:201
  12.3 0.7 copy-start.11
  12.7 15.5 %copy-start.13 = (s32[1,2048]{1,0:T(1,128)S(1)}, s32[1,2048]{1,0:T(1,128)}, u32[]{:S(2)}) copy-start(s32[1,2048]{1,0:T(1,128)} %param.15) | copy-start | bytes 24580
  12.7 16.1 %copy-start.9 = (f32[2048,128]{1,0:T(8,128)S(1)}, f32[2048,128]{1,0:T(8,128)}, u32[]{:S(2)}) copy-start(f32[2048,128]{1,0:T(8,128)} %param.11) | copy-start | bytes 3145732
  15.2 13.7 %copy-start.12 = (f32[2048]{0:T(1024)S(1)}, f32[2048]{0:T(1024)}, u32[]{:S(2)}) copy-start(f32[2048]{0:T(1024)} %param.12) | copy-start | bytes 24580
  16.9 56.8 %all-to-all-start = ((s32[128,1,32]{2,1,0:T(1,128)}), s32[128,1,32]{2,1,0:T(1,128)S(1)}, u32[]{:S(2)}, u32[]{:S(2)}) async-start(s32[128,1,32]{2,1,0:T(1,128)} %copy.27), calls=%async_computation | async-start | bytes 131072 | tf_op jit(solution)/shard_map/all_to_all | solution.py:218
  28.8 16.2 %copy-start.8 = (s32[6144]{0:T(1024)S(1)}, s32[6144]{0:T(1024)}, u32[]{:S(2)}) copy-start(s32[6144]{0:T(1024)} %param.14) | copy-start | bytes 73732
  29.0 12.7 %collective-permute-start.2 = (f32[1040,128]{1,0:T(8,128)S(1)}, f32[1040,128]{1,0:T(8,128)S(1)}, u32[]{:S(2)}, u32[]{:S(2)}) collective-permute-start(f32[1040,128]{1,0:T(8,128)S(1)} %pad_maximum_fusion.1), channel_id=1, source_target_pairs={{0,1},{1,0},{2,3},{3,2},{4,5},{5,4},{6,7},{7,6},{8,9},{9,8},{10,11... | collective-permute-start | bytes 1597448 | tf_op jit(solution)/shard_map/ppermute | solution.py:201
  30.6 30.4 %collective-permute-start.1 = (f32[1024,128]{1,0:T(8,128)S(1)}, f32[1024,128]{1,0:T(8,128)S(1)}, u32[]{:S(2)}, u32[]{:S(2)}) collective-permute-start(f32[1024,128]{1,0:T(8,128)S(1)} %get-tuple-element.14), channel_id=1, source_target_pairs={{0,3},{1,2},{2,1},{3,0},{4,7},{5,6},{6,5},{7,4},{8,11},{9,10},{10,... | collective-permute-start | bytes 1572872 | tf_op jit(solution)/shard_map/ppermute | solution.py:201
  41.7 19.4 %collective-permute-start.3 = (f32[1040,128]{1,0:T(8,128)S(1)}, f32[1040,128]{1,0:T(8,128)S(1)}, u32[]{:S(2)}, u32[]{:S(2)}) collective-permute-start(f32[1040,128]{1,0:T(8,128)S(1)} %broadcast_select_fusion), channel_id=1, source_target_pairs={{0,3},{1,2},{2,1},{3,0},{4,7},{5,6},{6,5},{7,4},{8,11},{9,10},{10,... | collective-permute-start | bytes 1597448 | tf_op jit(solution)/shard_map/ppermute | solution.py:201
  61.2 0.8 copy-start.10
  68.7 3.6 %copy-start = (bf16[2304,2048]{1,0:T(8,128)(2,1)}, bf16[2304,2048]{1,0:T(8,128)(2,1)S(1)}, u32[]{:S(2)}) copy-start(bf16[2304,2048]{1,0:T(8,128)(2,1)S(1)} %count.1.c_ref) | copy-start | bytes 28311556
  72.3 1.3 copy-start.2
  73.6 8.7 %copy-start.14 = (f32[128]{0:T(128)S(1)}, f32[128]{0:T(128)}, u32[]{:S(2)}) copy-start(f32[128]{0:T(128)} %param.19) | copy-start | bytes 1540
  73.6 39.6 %copy-start.6 = (f32[128,128]{1,0:T(8,128)S(1)}, f32[128,128]{1,0:T(8,128)}, u32[]{:S(2)}) copy-start(f32[128,128]{1,0:T(8,128)} %dense_ref.1) | copy-start | bytes 196612
  73.6 39.6 %copy-start.7 = (f32[1024]{0:T(1024)S(1)}, f32[1024]{0:T(1024)}, u32[]{:S(2)}) copy-start(f32[1024]{0:T(1024)} %param.21) | copy-start | bytes 12292
  73.6 39.6 %all-to-all-start.1 = ((f32[128,32,128]{2,1,0:T(8,128)}), f32[128,32,128]{2,1,0:T(8,128)S(1)}, u32[]{:S(2)}, u32[]{:S(2)}) async-start(f32[128,32,128]{2,1,0:T(8,128)} %bitcast.35), calls=%async_computation.1 | async-start | bytes 4194304 | tf_op jit(solution)/shard_map/all_to_all | solution.py:218
  113.3 1.2 copy-start.5
  125.9 1.3 copy-start.3
  127.2 1.1 copy-start.4
  128.3 169.2 %all-to-all-start.2 = ((f32[128,32,128]{2,1,0:T(8,128)}), f32[128,32,128]{2,1,0:T(8,128)S(1)}, u32[]{:S(2)}, u32[]{:S(2)}) async-start(f32[128,32,128]{2,1,0:T(8,128)} %bitcast.36), calls=%async_computation.2 | async-start | bytes 4194304 | tf_op jit(solution)/shard_map/all_to_all | solution.py:218
  131.9 161.9 %all-reduce.4.cloned.1.call-start = ((), (), s32[]{:S(2)}) async-start(), calls=%async_computation.3 | async-start | bytes 2228224 | tf_op jit(solution)/shard_map/psum | solution.py:298
  297.5 3.7 %copy-start.1 = (bf16[2304,2048]{1,0:T(8,128)(2,1)S(1)}, bf16[2304,2048]{1,0:T(8,128)(2,1)}, u32[]{:S(2)}) copy-start(bf16[2304,2048]{1,0:T(8,128)(2,1)} %copy-done) | copy-start | bytes 28311556
Sparse Core Ops, SparseCore 0:
  137.5 156.2 all-reduce.3

commit v2 on v1

--- a/solution.py
+++ b/solution.py
@@ -18,11 +18,15 @@
 CHUNK = 256
 SPAN = CHUNK + 16
 C_ROWS = 2304
+G_ROWS = 2304
+HALF = G_ROWS // 2
+SEG = HALF // 16
 PAIRS = [(i, j) for i in range(F + 1) for j in range(i + 1, F + 1)]
 PAIR_ROW = {pair: 128 + n for n, pair in enumerate(PAIRS)}
 
 learn_rate = 0.05
 epsilon = 1e-08
+MESH = pl.DeviceIdType.MESH
 f32, bf16, i32 = jnp.float32, jnp.bfloat16, jnp.int32
 
 VMEM = pl.BlockSpec(memory_space=pltpu.VMEM)
@@ -136,11 +140,14 @@
     hidden = pre * sig
     logits = jnp.sum(hidden * wo_ref[...], axis=1, keepdims=True)
     d_logits = 1.0 / (1.0 + jnp.exp(-logits)) - label_ref[...]
-    grad_ref[INTER : INTER + 8, :] = jnp.broadcast_to(
-        jnp.sum(hidden * d_logits, axis=0, keepdims=True), (8, HID)
-    )
+    out_grad = jnp.sum(hidden * d_logits, axis=0, keepdims=True)
+    for q in range(8):
+        grad_ref[8 * INTER + q : 8 * INTER + q + 1, :] = out_grad[:, q * 128 : (q + 1) * 128]
+    grad_ref[8 * INTER + 8 :, :] = jnp.zeros((G_ROWS - 8 * INTER - 8, 128), f32)
     d_pre = split(d_logits * wo_ref[...] * (sig * (1.0 + pre * (1.0 - sig))))
-    grad_ref[0:INTER, :] = dot3(split(it), d_pre, NN)
+    top_grad = dot3(split(it), d_pre, NN)
+    for q in range(8):
+        grad_ref[q * INTER : (q + 1) * INTER, :] = top_grad[:, q * 128 : (q + 1) * 128]
     inter_t[...] = dot3(w, d_pre, NT)
 
     for j in range(1, F + 1):
@@ -164,9 +171,147 @@
     lax.fori_loop(0, DEVICES, give, 0)
 
 
+def total_kernel(g_ref, fin_ref, r1, acc, r2, mine, r3, s1, q1, s2, q2, s3, q3, s4, q4, s5, q5):
+    gx, x = lax.axis_index("gx"), lax.axis_index("gy")
+    yz, core = gx // 2, gx % 2
+    twin = (gx + 1 - 2 * core, x)
+
+    def chip(k):
+        return (((yz + k) % 16) * 2 + core, x)
+
+    def along(k):
+        return (gx, (x + k) % 4)
+
+    barrier = pltpu.get_barrier_semaphore()
+
+    def hello(device):
+        pl.semaphore_signal(barrier, inc=1, device_id=device, device_id_type=MESH)
+
+    def greet(k, carry):
+        hello(chip(k))
+        return carry
+
+    hello(twin)
+    lax.fori_loop(1, 16, greet, 0)
+    for k in range(1, 4):
+        hello(along(k))
+    pl.semaphore_wait(barrier, 19)
+
+    def put(src, dst, send, recv, device):
+        return pltpu.make_async_remote_copy(
+            src_ref=src, dst_ref=dst, send_sem=send, recv_sem=recv, device_id=device, device_id_type=MESH
+        )
+
+    my_half = pl.multiple_of(core * HALF, 8)
+    other = pl.multiple_of((1 - core) * HALF, 8)
+    swap = put(g_ref.at[pl.ds(other, HALF)], r1, s1, q1, twin)
+    swap.start()
+    swap.wait()
+    acc[...] = g_ref[pl.ds(my_half, HALF), :] + r1[...]
+
+    def seg(n):
+        return pl.ds(pl.multiple_of(n * SEG, 8), SEG)
+
+    def scatter(k):
+        return put(acc.at[seg((yz + k) % 16)], r2.at[k], s2.at[k], q2.at[k], chip(k))
+
+    def start_scatter(k, carry):
+        scatter(k).start()
+        return carry
+
+    lax.fori_loop(1, 16, start_scatter, 0)
+    r2[0] = acc[seg(yz), :]
+
+    def wait_scatter(k, carry):
+        scatter(k).wait()
+        return carry
+
+    lax.fori_loop(1, 16, wait_scatter, 0)
+    part = r2[0]
+    for k in range(1, 16):
+        part = part + r2[k]
+    mine[...] = part
+    r3[x] = part
+    sends = [put(mine, r3.at[x], s3.at[k], q3.at[k], along(k)) for k in range(1, 4)]
+    for copy in sends:
+        copy.start()
+    for k in range(1, 4):
+        put(mine, r3.at[(x + 4 - k) % 4], s3.at[k], q3.at[k], along(k)).wait()
+    whole = (r3[0] + r3[1]) + (r3[2] + r3[3])
+    place = pl.ds(pl.multiple_of(my_half + yz * SEG, 8), SEG)
+    fin_ref[place, :] = whole
+
+    def gather(k, who):
+        there = pl.ds(pl.multiple_of(my_half + who * SEG, 8), SEG)
+        return put(fin_ref.at[there], fin_ref.at[there], s4.at[k], q4.at[k], chip(k))
+
+    def start_gather(k, carry):
+        gather(k, yz).start()
+        return carry
+
+    def wait_gather(k, carry):
+        gather(k, yz).wait_send()
+        gather(k, (yz + 16 - k) % 16).wait_recv()
+        return carry
+
+    lax.fori_loop(1, 16, start_gather, 0)
+    lax.fori_loop(1, 16, wait_gather, 0)
+    half = fin_ref.at[pl.ds(my_half, HALF)]
+    last = put(half, half, s5, q5, twin)
+    last.start()
+    last.wait_send()
+    rest = fin_ref.at[pl.ds(other, HALF)]
+    put(rest, rest, s5, q5, twin).wait_recv()
+
+
+def all_total(grads):
+    dma = pltpu.SemaphoreType.DMA
+    return pl.pallas_call(
+        total_kernel,
+        out_shape=jax.ShapeDtypeStruct((G_ROWS, 128), f32),
+        in_specs=[VMEM],
+        out_specs=VMEM,
+        scratch_shapes=[
+            pltpu.VMEM((HALF, 128), f32),
+            pltpu.VMEM((HALF, 128), f32),
+            pltpu.VMEM((16, SEG, 128), f32),
+            pltpu.VMEM((SEG, 128), f32),
+            pltpu.VMEM((4, SEG, 128), f32),
+            dma,
+            dma,
+            dma((16,)),
+            dma((16,)),
+            dma((4,)),
+            dma((4,)),
+            dma((16,)),
+            dma((16,)),
+            dma,
+            dma,
+        ],
+        compiler_params=params(collective_id=0, has_side_effects=True, vmem_limit_bytes=24 << 20),
+        cost_estimate=pl.CostEstimate(flops=50_000_000, bytes_accessed=4 << 20, transcendentals=0),
+        name="total",
+    )(grads)
+
+
 def update_kernel(
-    where_ref, c_ref, came_ref, table_ref, state_ref, new_table_ref, new_state_ref, grads, sides
+    where_ref,
+    c_ref,
+    came_ref,
+    table_ref,
+    state_ref,
+    total_ref,
+    new_table_ref,
+    new_state_ref,
+    top_ref,
+    out_ref,
+    grads,
+    sides,
 ):
+    for q in range(8):
+        top_ref[:, q * 128 : (q + 1) * 128] = total_ref[q * INTER : (q + 1) * INTER, :]
+        out_ref[:, q * 128 : (q + 1) * 128] = total_ref[8 * INTER + q : 8 * INTER + q + 1, :]
+
     def take(n, carry):
         for u in range(16):
             b = n * 16 + u
@@ -281,7 +426,7 @@
         dense_kernel,
         out_shape=(
             jax.ShapeDtypeStruct((DEVICES * CAP, E), f32),
-            jax.ShapeDtypeStruct((INTER + 8, HID), f32),
+            jax.ShapeDtypeStruct((G_ROWS, 128), f32),
         ),
         in_specs=[SMEM, VMEM, VMEM, VMEM, VMEM, VMEM],
         out_specs=(VMEM, VMEM),
@@ -295,21 +440,23 @@
     )(got_slots, got_rows, dense_vectors, labels[:, None], top_weight, out_weight[None, :])
 
     came_back = swap_all(back_rows.reshape(DEVICES, CAP, E)).reshape(DEVICES * CAP, E)
-    total = lax.psum(grads[: INTER + 1], ("gx", "gy"))
-
-    new_table, new_state = pl.pallas_call(
+    total = all_total(grads)
+
+    new_table, new_state, top_grad, out_grad = pl.pallas_call(
         update_kernel,
         out_shape=(
             jax.ShapeDtypeStruct((ROWS, E), f32),
             jax.ShapeDtypeStruct((1, ROWS), f32),
+            jax.ShapeDtypeStruct((INTER, HID), f32),
+            jax.ShapeDtypeStruct((1, HID), f32),
         ),
-        in_specs=[SMEM, VMEM, VMEM, VMEM, VMEM],
-        out_specs=(VMEM, VMEM),
+        in_specs=[SMEM, VMEM, VMEM, VMEM, VMEM, VMEM],
+        out_specs=(VMEM, VMEM, VMEM, VMEM),
         scratch_shapes=[pltpu.VMEM((BAGS, E), f32), pltpu.VMEM((2 * E, BAGS), bf16)],
         compiler_params=params(vmem_limit_bytes=24 << 20),
         name="update",
-    )(where_to, counts, came_back, held, held_state)
-    return new_table, new_state.reshape(ROWS), total[:INTER], total[INTER]
+    )(where_to, counts, came_back, held, held_state, total)
+    return new_table, new_state.reshape(ROWS), top_grad, out_grad.reshape(HID)
 
 
 def solution(mesh):

time: 318 us -> 192 us (0.60)
  waiting for transfers between devices: 200 us -> 38.6 us
  Pallas kernels: 42.7 us -> 92.1 us
  between operations: 15 us -> 1.59 us
    psum x1 -> x0, waiting for transfers between devices: 160 us -> none  [on_device(): total = lax.psum(grads[:INTER + 1], ('gx', 'gy'))]
    pallas_call x0 -> x1, Pallas kernels: none -> 49 us  [all_total(): pl.pallas_call(total_kernel, out_shape=jax.ShapeDtypeStruct((G_ROWS, 128)...]
    slice x2 -> x0, local copies, waits for them, and re-layouts: 3.69 us -> none  [on_device(): return (new_table, new_state.reshape(ROWS), total[:INTER], total[INTER])]
    unnamed x30 -> x36, local copies, waits for them, and re-layouts: 13.3 us -> 16.8 us
  transfers between devices with their start and end apart: 8 -> 7, of which waited for: 3 -> 2; matrix products, arithmetic and copies ran while one was open for 4% -> 5% of each run, Pallas kernels for 7% -> 37%
where the time goes in v2:
time: 192 us; the launch traced here: 191 us
  Pallas kernels  92.1 us (48%)
  waiting for transfers between devices  38.6 us (20%)
  starting transfers between devices  31.6 us (16%)
  local copies, waits for them, and re-layouts  21.4 us (11%)
  other arithmetic  5.23 us (3%)
    pallas_call x1, Pallas kernels, all_total(): pl.pallas_call(total_kernel, out_shape=jax.ShapeDtypeStruct((G_ROWS, 128)...  49 us
    all_to_all x3, waiting for transfers between devices, swap_all(): lax.all_to_all(x, ('gx', 'gy'), split_axis=0, concat_axis=0, tiled=True)  29.4 us
    all_to_all x3, starting transfers between devices, swap_all(): lax.all_to_all(x, ('gx', 'gy'), split_axis=0, concat_axis=0, tiled=True)  22.9 us
    unnamed x36, local copies, waits for them, and re-layouts  16.8 us
    pallas_call x1, Pallas kernels, on_device(): pl.pallas_call(count_kernel, out_shape=jax.ShapeDtypeStruct((C_ROWS, ROWS...  15.9 us
    pallas_call x1, Pallas kernels, on_device(): pl.pallas_call(dense_kernel, out_shape=(jax.ShapeDtypeStruct((DEVICES * C...  11.3 us
    pallas_call x1, Pallas kernels, on_device(): pl.pallas_call(update_kernel, out_shape=(jax.ShapeDtypeStruct((ROWS, E),...  9.29 us
    ppermute x4, waiting for transfers between devices, from_partner(): return lax.ppermute(block, 'gy', [(y, y ^ flip) for y in range(4)])  9.16 us
  transfers between devices with their start and end apart: 7, of which 2 were waited for; matrix products, arithmetic and copies ran while one was open for 5% of the time, Pallas kernels for 37%

profile of v2, /device:TPU:1, one launch (start us, length us, event | category | flops | bytes accessed | tf_op | source)
XLA Modules:
  0.0 191.4 jit_solution(3375698734168085418)
XLA Ops:
  0.6 1.1 slice.37
  1.7 2.1 %collective-permute-start = (f32[1024,128]{1,0:T(8,128)S(1)}, f32[1024,128]{1,0:T(8,128)S(1)}, u32[]{:S(2)}, u32[]{:S(2)}) collective-permute-start(f32[1024,128]{1,0:T(8,128)S(1)} %slice.37), channel_id=1, source_target_pairs={{0,1},{1,0},{2,3},{3,2},{4,5},{5,4},{6,7},{7,6},{8,9},{9,8},{10,11... | collective-permute-start | bytes 1572872 | tf_op jit(solution)/shard_map/ppermute | solution.py:346
  3.8 0.7 fusion.11
  4.5 0.8 copy.25
  7.1 1.6 select_convert_fusion.1
  8.7 0.9 convolution_convert_fusion
  9.6 0.7 copy.27
  10.3 10.7 %all-to-all-start = ((s32[128,1,32]{2,1,0:T(1,128)}), s32[128,1,32]{2,1,0:T(1,128)S(1)}, u32[]{:S(2)}, u32[]{:S(2)}) async-start(s32[128,1,32]{2,1,0:T(1,128)} %copy.27), calls=%async_computation | async-start | bytes 131072 | tf_op jit(solution)/shard_map/all_to_all | solution.py:363
  22.4 1.4 collective-permute-start.2
  24.1 1.9 collective-permute-start.1
  25.9 9.2 %collective-permute-done.2 = f32[1040,128]{1,0:T(8,128)S(1)} collective-permute-done((f32[1040,128]{1,0:T(8,128)S(1)}, f32[1040,128]{1,0:T(8,128)S(1)}, u32[]{:S(2)}, u32[]{:S(2)}) %collective-permute-start.2) | collective-permute-done | bytes 532512 | tf_op jit(solution)/shard_map/ppermute | solution.py:346
  35.1 3.3 %collective-permute-start.3 = (f32[1040,128]{1,0:T(8,128)S(1)}, f32[1040,128]{1,0:T(8,128)S(1)}, u32[]{:S(2)}, u32[]{:S(2)}) collective-permute-start(f32[1040,128]{1,0:T(8,128)S(1)} %broadcast_select_fusion), channel_id=1, source_target_pairs={{0,3},{1,2},{2,1},{3,0},{4,7},{5,6},{6,5},{7,4},{8,11},{9,10},{10,... | collective-permute-start | bytes 1597448 | tf_op jit(solution)/shard_map/ppermute | solution.py:346
  38.5 15.9 %count.1.c_ref = bf16[2304,2048]{1,0:T(8,128)(2,1)S(1)} custom-call(s32[24]{0:T(128)S(1)} %fusion.16.first_ref, s32[48,128]{1,0:T(8,128)S(1)} %bitcast.38, s32[18,128]{1,0:T(8,128)S(1)} %get-tuple-element.25.start_ref, s32[18,128]{1,0:T(8,128)S(1)} %get-tuple-element.24.end_ref), custom_call_target="tpu_custom_call" | custom-call | flops 6845104128 | bytes 10485760 | tf_op jit(solution)/shard_map/count/pallas_call | solution.py:403
  54.6 0.8 copy-done.13
  55.5 6.5 %pool.1 = f32[4096,128]{1,0:T(8,128)S(1)} custom-call(s32[2048]{0:T(1024)S(1)} %multiply_add_fusion.where_ref, bf16[2304,2048]{1,0:T(8,128)(2,1)S(1)} %count.1.c_ref, f32[2048,128]{1,0:T(8,128)S(1)} %pad_maximum_fusion.table_ref), custom_call_target="tpu_custom_call" | custom-call | tf_op jit(solution)/shard_map/pool/pallas_call | solution.py:414
  62.1 3.6 %copy-done = bf16[2304,2048]{1,0:T(8,128)(2,1)} copy-done((bf16[2304,2048]{1,0:T(8,128)(2,1)}, bf16[2304,2048]{1,0:T(8,128)(2,1)S(1)}, u32[]{:S(2)}) %copy-start) | copy-done | bytes 9437208
  65.7 1.3 copy-done.2
  67.0 8.6 %all-to-all-start.1 = ((f32[128,32,128]{2,1,0:T(8,128)}), f32[128,32,128]{2,1,0:T(8,128)S(1)}, u32[]{:S(2)}, u32[]{:S(2)}) async-start(f32[128,32,128]{2,1,0:T(8,128)} %bitcast.34), calls=%async_computation.1 | async-start | bytes 4194304 | tf_op jit(solution)/shard_map/all_to_all | solution.py:363
  76.3 0.8 reduce.5
  77.2 29.4 %all-to-all-done.1 = f32[128,32,128]{2,1,0:T(8,128)S(1)} async-done(((f32[128,32,128]{2,1,0:T(8,128)}), f32[128,32,128]{2,1,0:T(8,128)S(1)}, u32[]{:S(2)}, u32[]{:S(2)}) %all-to-all-start.1) | async-done | bytes 2097184 | tf_op jit(solution)/shard_map/all_to_all | solution.py:363
  106.6 1.2 copy-done.8
  107.9 11.3 %dense.1 = (f32[4096,128]{1,0:T(8,128)S(1)}, f32[2304,128]{1,0:T(8,128)S(1)}) custom-call(s32[4096]{0:T(1024)S(1)} %reshape.110.slot_ref, f32[4096,128]{1,0:T(8,128)S(1)} %bitcast.32, f32[128,128]{1,0:T(8,128)S(1)} %copy-done.9, f32[128,1]{1,0:T(8,128)S(1)} %copy.28.label_ref, f32[264,1024]{1,0:T(8,128)S(1)} %copy-done.8, f32[1,1024]{1,0:T(1,128)S(1)} %bitcast.37), custom_call_target="tpu_custom_call" | custom-call | tf_op jit(solution)/shard_map/dense/pallas_call | solution.py:425
  119.2 1.3 copy-done.5
  120.5 1.0 copy-done.6
  121.5 3.6 %all-to-all-start.2 = ((f32[128,32,128]{2,1,0:T(8,128)}), f32[128,32,128]{2,1,0:T(8,128)S(1)}, u32[]{:S(2)}, u32[]{:S(2)}) async-start(f32[128,32,128]{2,1,0:T(8,128)} %bitcast.35), calls=%async_computation.2 | async-start | bytes 4194304 | tf_op jit(solution)/shard_map/all_to_all | solution.py:363
  125.1 0.7 slice.48
  125.9 1.3 copy-done.7
  127.1 49.0 %total.1.total_ref = f32[2304,128]{1,0:T(8,128)S(1)} custom-call(f32[2304,128]{1,0:T(8,128)S(1)} %copy-done.7), custom_call_target="tpu_custom_call" | custom-call | flops 50000000 | bytes 4194304 | tf_op jit(solution)/shard_map/total/pallas_call | solution.py:269
  176.1 1.0 copy-done.3
  177.2 3.7 %copy-done.1 = bf16[2304,2048]{1,0:T(8,128)(2,1)S(1)} copy-done((bf16[2304,2048]{1,0:T(8,128)(2,1)S(1)}, bf16[2304,2048]{1,0:T(8,128)(2,1)}, u32[]{:S(2)}) %copy-start.1) | copy-done | bytes 9437208
  180.9 1.3 copy-done.4
  182.1 9.3 %update.1 = (f32[2048,128]{1,0:T(8,128)}, f32[1,2048]{1,0:T(1,128)}, f32[264,1024]{1,0:T(8,128)}, f32[1,1024]{1,0:T(1,128)}) custom-call(s32[2048]{0:T(1024)S(1)} %multiply_add_fusion.where_ref, bf16[2304,2048]{1,0:T(8,128)(2,1)S(1)} %copy-done.1, f32[4096,128]{1,0:T(8,128)S(1)} %bitcast.33, f32[2048,128]{1,0:T(8,128)S(1)} %pad_maximum_fusion.table_ref, ...), custom_call_target="tpu_custom_call" | custom-call | tf_op jit(solution)/shard_map/update/pallas_call | solution.py:445
  (59 shorter events, 3.7 us)
Async XLA Ops:
  1.7 20.5 %collective-permute-start = (f32[1024,128]{1,0:T(8,128)S(1)}, f32[1024,128]{1,0:T(8,128)S(1)}, u32[]{:S(2)}, u32[]{:S(2)}) collective-permute-start(f32[1024,128]{1,0:T(8,128)S(1)} %slice.37), channel_id=1, source_target_pairs={{0,1},{1,0},{2,3},{3,2},{4,5},{5,4},{6,7},{7,6},{8,9},{9,8},{10,11... | collective-permute-start | bytes 1572872 | tf_op jit(solution)/shard_map/ppermute | solution.py:346
  5.7 0.7 copy-start.14
  6.2 15.5 %copy-start.16 = (s32[1,2048]{1,0:T(1,128)S(1)}, s32[1,2048]{1,0:T(1,128)}, u32[]{:S(2)}) copy-start(s32[1,2048]{1,0:T(1,128)} %param.15) | copy-start | bytes 24580
  6.2 16.1 %copy-start.12 = (f32[2048,128]{1,0:T(8,128)S(1)}, f32[2048,128]{1,0:T(8,128)}, u32[]{:S(2)}) copy-start(f32[2048,128]{1,0:T(8,128)} %param.11) | copy-start | bytes 3145732
  8.7 13.7 %copy-start.15 = (f32[2048]{0:T(1024)S(1)}, f32[2048]{0:T(1024)}, u32[]{:S(2)}) copy-start(f32[2048]{0:T(1024)} %param.12) | copy-start | bytes 24580
  10.3 56.7 %all-to-all-start = ((s32[128,1,32]{2,1,0:T(1,128)}), s32[128,1,32]{2,1,0:T(1,128)S(1)}, u32[]{:S(2)}, u32[]{:S(2)}) async-start(s32[128,1,32]{2,1,0:T(1,128)} %copy.27), calls=%async_computation | async-start | bytes 131072 | tf_op jit(solution)/shard_map/all_to_all | solution.py:363
  22.2 16.2 %copy-start.11 = (s32[6144]{0:T(1024)S(1)}, s32[6144]{0:T(1024)}, u32[]{:S(2)}) copy-start(s32[6144]{0:T(1024)} %param.14) | copy-start | bytes 73732
  22.4 12.7 %collective-permute-start.2 = (f32[1040,128]{1,0:T(8,128)S(1)}, f32[1040,128]{1,0:T(8,128)S(1)}, u32[]{:S(2)}, u32[]{:S(2)}) collective-permute-start(f32[1040,128]{1,0:T(8,128)S(1)} %pad_maximum_fusion.1), channel_id=1, source_target_pairs={{0,1},{1,0},{2,3},{3,2},{4,5},{5,4},{6,7},{7,6},{8,9},{9,8},{10,11... | collective-permute-start | bytes 1597448 | tf_op jit(solution)/shard_map/ppermute | solution.py:346
  24.1 30.4 %collective-permute-start.1 = (f32[1024,128]{1,0:T(8,128)S(1)}, f32[1024,128]{1,0:T(8,128)S(1)}, u32[]{:S(2)}, u32[]{:S(2)}) collective-permute-start(f32[1024,128]{1,0:T(8,128)S(1)} %get-tuple-element.18), channel_id=1, source_target_pairs={{0,3},{1,2},{2,1},{3,0},{4,7},{5,6},{6,5},{7,4},{8,11},{9,10},{10,... | collective-permute-start | bytes 1572872 | tf_op jit(solution)/shard_map/ppermute | solution.py:346
  35.1 19.4 %collective-permute-start.3 = (f32[1040,128]{1,0:T(8,128)S(1)}, f32[1040,128]{1,0:T(8,128)S(1)}, u32[]{:S(2)}, u32[]{:S(2)}) collective-permute-start(f32[1040,128]{1,0:T(8,128)S(1)} %broadcast_select_fusion), channel_id=1, source_target_pairs={{0,3},{1,2},{2,1},{3,0},{4,7},{5,6},{6,5},{7,4},{8,11},{9,10},{10,... | collective-permute-start | bytes 1597448 | tf_op jit(solution)/shard_map/ppermute | solution.py:346
  54.6 0.8 copy-start.13
  62.0 3.6 %copy-start = (bf16[2304,2048]{1,0:T(8,128)(2,1)}, bf16[2304,2048]{1,0:T(8,128)(2,1)S(1)}, u32[]{:S(2)}) copy-start(bf16[2304,2048]{1,0:T(8,128)(2,1)S(1)} %count.1.c_ref) | copy-start | bytes 28311556
  65.7 1.3 copy-start.2
  67.0 8.7 %copy-start.17 = (f32[128]{0:T(128)S(1)}, f32[128]{0:T(128)}, u32[]{:S(2)}) copy-start(f32[128]{0:T(128)} %param.19) | copy-start | bytes 1540
  67.0 39.6 %copy-start.9 = (f32[128,128]{1,0:T(8,128)S(1)}, f32[128,128]{1,0:T(8,128)}, u32[]{:S(2)}) copy-start(f32[128,128]{1,0:T(8,128)} %dense_ref.1) | copy-start | bytes 196612
  67.0 39.6 %copy-start.10 = (f32[1024]{0:T(1024)S(1)}, f32[1024]{0:T(1024)}, u32[]{:S(2)}) copy-start(f32[1024]{0:T(1024)} %param.21) | copy-start | bytes 12292
  67.0 39.6 %all-to-all-start.1 = ((f32[128,32,128]{2,1,0:T(8,128)}), f32[128,32,128]{2,1,0:T(8,128)S(1)}, u32[]{:S(2)}, u32[]{:S(2)}) async-start(f32[128,32,128]{2,1,0:T(8,128)} %bitcast.34), calls=%async_computation.1 | async-start | bytes 4194304 | tf_op jit(solution)/shard_map/all_to_all | solution.py:363
  106.6 1.2 copy-start.8
  119.2 1.3 copy-start.5
  120.5 1.1 copy-start.6
  121.5 55.6 %all-to-all-start.2 = ((f32[128,32,128]{2,1,0:T(8,128)}), f32[128,32,128]{2,1,0:T(8,128)S(1)}, u32[]{:S(2)}, u32[]{:S(2)}) async-start(f32[128,32,128]{2,1,0:T(8,128)} %bitcast.35), calls=%async_computation.2 | async-start | bytes 4194304 | tf_op jit(solution)/shard_map/all_to_all | solution.py:363
  125.8 1.3 copy-start.7
  176.1 1.1 copy-start.3
  177.2 3.7 %copy-start.1 = (bf16[2304,2048]{1,0:T(8,128)(2,1)S(1)}, bf16[2304,2048]{1,0:T(8,128)(2,1)}, u32[]{:S(2)}) copy-start(bf16[2304,2048]{1,0:T(8,128)(2,1)} %copy-done) | copy-start | bytes 28311556
  180.9 1.3 copy-start.4

commit v3 on v1

--- a/solution.py
+++ b/solution.py
@@ -18,11 +18,17 @@
 CHUNK = 256
 SPAN = CHUNK + 16
 C_ROWS = 2304
+G_ROWS = 2304
+HALF = G_ROWS // 2
+SEG = HALF // 16
+STRIDE = 37
+CUT_A, CUT_B = 48, 88
 PAIRS = [(i, j) for i in range(F + 1) for j in range(i + 1, F + 1)]
 PAIR_ROW = {pair: 128 + n for n, pair in enumerate(PAIRS)}
 
 learn_rate = 0.05
 epsilon = 1e-08
+MESH = pl.DeviceIdType.MESH
 f32, bf16, i32 = jnp.float32, jnp.bfloat16, jnp.int32
 
 VMEM = pl.BlockSpec(memory_space=pltpu.VMEM)
@@ -83,7 +89,59 @@
     lax.fori_loop(0, LOOKS // CHUNK, chunk, 0)
 
 
-def pool_kernel(where_ref, c_ref, table_ref, send_ref, split_ref, partial_ref):
+def device_at(n):
+    return (n // 4, n % 4)
+
+
+def my_number():
+    return lax.axis_index("gx") * 4 + lax.axis_index("gy")
+
+
+def peer_of(k):
+    return (my_number() + STRIDE * k) % DEVICES
+
+
+def greet_all(barrier):
+    def greet(k, carry):
+        pl.semaphore_signal(barrier, inc=1, device_id=device_at(peer_of(k)), device_id_type=MESH)
+        return carry
+
+    lax.fori_loop(1, DEVICES, greet, 0)
+
+
+def put(src, dst, send, recv, device):
+    return pltpu.make_async_remote_copy(
+        src_ref=src, dst_ref=dst, send_sem=send, recv_sem=recv, device_id=device, device_id_type=MESH
+    )
+
+
+def chunk_at(n):
+    return pl.ds(pl.multiple_of(n * CAP, CAP), CAP)
+
+
+def pick_rows(dst, to, src, index_ref, at):
+    for u in range(CAP):
+        dst[pl.ds(to + u, 1), :] = src[pl.ds(index_ref[at + u], 1), :]
+
+
+def pool_kernel(
+    bag_ref,
+    slots_ref,
+    c_ref,
+    table_ref,
+    recv_ref,
+    got_ref,
+    split_ref,
+    partial_ref,
+    send_ref,
+    row_send,
+    row_recv,
+    slot_send,
+    slot_recv,
+):
+    barrier = pltpu.get_barrier_semaphore()
+    greet_all(barrier)
+    me = my_number()
     hi, lo = split(table_ref[...])
     split_ref[:, :128] = hi
     split_ref[:, 128:] = lo
@@ -95,25 +153,46 @@
         return carry
 
     lax.fori_loop(0, BAGS // 256, block, 0)
-
-    def place(n, carry):
-        for u in range(16):
-            b = n * 16 + u
-            send_ref[pl.ds(where_ref[b], 1), :] = partial_ref[pl.ds(b, 1), :]
-        return carry
-
-    lax.fori_loop(0, BAGS // 16, place, 0)
+    got_ref[me] = slots_ref[me]
+    pick_rows(recv_ref, me * CAP, partial_ref, bag_ref, me * CAP)
+
+    def ready(k):
+        at = peer_of(k) * CAP
+        pick_rows(send_ref, at, partial_ref, bag_ref, at)
+
+    def start(k):
+        peer = peer_of(k)
+        to = device_at(peer)
+        put(slots_ref.at[peer], got_ref.at[me], slot_send, slot_recv, to).start()
+        put(send_ref.at[chunk_at(peer)], recv_ref.at[chunk_at(me)], row_send, row_recv, to).start()
+
+    ready(1)
+    pl.semaphore_wait(barrier, DEVICES - 1)
+
+    def step(k, carry):
+        ready(k)
+        start(k - 1)
+        return carry
+
+    lax.fori_loop(2, DEVICES, step, 0)
+    start(DEVICES - 1)
+    to = device_at(peer_of(1))
+    some = pl.ds(0, DEVICES - 1)
+    put(slots_ref.at[some], got_ref.at[some], slot_send, slot_recv, to).wait()
+    rows = pl.ds(0, (DEVICES - 1) * CAP)
+    put(send_ref.at[rows], recv_ref.at[rows], row_send, row_recv, to).wait()
 
 
 def dense_kernel(
-    slot_ref, got_ref, dense_ref, label_ref, w_ref, wo_ref, back_ref, grad_ref, pooled, vt, inter_t
+    slot_ref, got_ref, dense_ref, label_ref, w_ref, wo_ref, pooled, grad_ref, vt, inter_t
 ):
+    pooled[BAGS:, :] = jnp.zeros((8, E), f32)
+
     def place(c, carry):
-        @pl.when(slot_ref[c * CAP] < BAGS)
+        @pl.when(slot_ref[c * 128] < BAGS)
         def _():
             for u in range(CAP):
-                p = c * CAP + u
-                pooled[pl.ds(slot_ref[p], 1), :] = got_ref[pl.ds(p, 1), :]
+                pooled[pl.ds(slot_ref[c * 128 + u], 1), :] = got_ref[pl.ds(c * CAP + u, 1), :]
 
         return carry
 
@@ -136,11 +215,14 @@
     hidden = pre * sig
     logits = jnp.sum(hidden * wo_ref[...], axis=1, keepdims=True)
     d_logits = 1.0 / (1.0 + jnp.exp(-logits)) - label_ref[...]
-    grad_ref[INTER : INTER + 8, :] = jnp.broadcast_to(
-        jnp.sum(hidden * d_logits, axis=0, keepdims=True), (8, HID)
-    )
+    out_grad = jnp.sum(hidden * d_logits, axis=0, keepdims=True)
+    for q in range(8):
+        grad_ref[8 * INTER + q : 8 * INTER + q + 1, :] = out_grad[:, q * 128 : (q + 1) * 128]
+    grad_ref[8 * INTER + 8 :, :] = jnp.zeros((G_ROWS - 8 * INTER - 8, 128), f32)
     d_pre = split(d_logits * wo_ref[...] * (sig * (1.0 + pre * (1.0 - sig))))
-    grad_ref[0:INTER, :] = dot3(split(it), d_pre, NN)
+    top_grad = dot3(split(it), d_pre, NN)
+    for q in range(8):
+        grad_ref[q * INTER : (q + 1) * INTER, :] = top_grad[:, q * 128 : (q + 1) * 128]
     inter_t[...] = dot3(w, d_pre, NT)
 
     for j in range(1, F + 1):
@@ -152,25 +234,131 @@
                 total = term if total is None else total + term
         pooled[(j - 1) * 128 : j * 128, :] = total.T
 
-    def give(c, carry):
-        @pl.when(slot_ref[c * CAP] < BAGS)
-        def _():
-            for u in range(CAP):
-                p = c * CAP + u
-                back_ref[pl.ds(p, 1), :] = pooled[pl.ds(slot_ref[p], 1), :]
-
-        return carry
-
-    lax.fori_loop(0, DEVICES, give, 0)
-
 
 def update_kernel(
-    where_ref, c_ref, came_ref, table_ref, state_ref, new_table_ref, new_state_ref, grads, sides
+    slot_ref,
+    where_ref,
+    pooled_ref,
+    g_ref,
+    c_ref,
+    table_ref,
+    state_ref,
+    new_table_ref,
+    new_state_ref,
+    top_ref,
+    out_ref,
+    back,
+    came,
+    grads,
+    sides,
+    fin,
+    r1,
+    acc,
+    r2,
+    mine,
+    r3,
+    row_send,
+    row_recv,
+    s1,
+    q1,
+    s2,
+    q2,
+    s3,
+    q3,
+    s4,
+    q4,
+    s5,
+    q5,
 ):
+    barrier = pltpu.get_barrier_semaphore()
+    greet_all(barrier)
+    me = my_number()
+    gx, x = lax.axis_index("gx"), lax.axis_index("gy")
+    yz, core = gx // 2, gx % 2
+    twin = (gx + 1 - 2 * core, x)
+
+    def chip(k):
+        return (((yz + k) % 16) * 2 + core, x)
+
+    def along(k):
+        return (gx, (x + k) % 4)
+
+    pick_rows(came, me * CAP, pooled_ref, slot_ref, me * 128)
+
+    def ready(k, carry):
+        peer = peer_of(k)
+        pick_rows(back, peer * CAP, pooled_ref, slot_ref, peer * 128)
+        return carry
+
+    lax.fori_loop(1, DEVICES, ready, 0)
+
+    def start(k, carry):
+        peer = peer_of(k)
+        put(
+            back.at[chunk_at(peer)], came.at[chunk_at(me)], row_send, row_recv, device_at(peer)
+        ).start()
+        return carry
+
+    pl.semaphore_wait(barrier, DEVICES - 1)
+
+    my_half = pl.multiple_of(core * HALF, 8)
+    other = pl.multiple_of((1 - core) * HALF, 8)
+    swap = put(g_ref.at[pl.ds(other, HALF)], r1, s1, q1, twin)
+    swap.start()
+    lax.fori_loop(1, CUT_A, start, 0)
+    swap.wait()
+    acc[...] = g_ref[pl.ds(my_half, HALF), :] + r1[...]
+
+    def seg(n):
+        return pl.ds(pl.multiple_of(n * SEG, 8), SEG)
+
+    def scatter(k):
+        return put(acc.at[seg((yz + k) % 16)], r2.at[k], s2.at[k], q2.at[k], chip(k))
+
+    def start_scatter(k, carry):
+        scatter(k).start()
+        return carry
+
+    lax.fori_loop(1, 16, start_scatter, 0)
+    lax.fori_loop(CUT_A, CUT_B, start, 0)
+    r2[0] = acc[seg(yz), :]
+
+    def wait_scatter(k, carry):
+        scatter(k).wait()
+        return carry
+
+    lax.fori_loop(1, 16, wait_scatter, 0)
+    part = r2[0]
+    for k in range(1, 16):
+        part = part + r2[k]
+    mine[...] = part
+    r3[x] = part
+    for k in range(1, 4):
+        put(mine, r3.at[x], s3.at[k], q3.at[k], along(k)).start()
+    lax.fori_loop(CUT_B, DEVICES, start, 0)
+    for k in range(1, 4):
+        put(mine, r3.at[(x + 4 - k) % 4], s3.at[k], q3.at[k], along(k)).wait()
+    whole = (r3[0] + r3[1]) + (r3[2] + r3[3])
+    place = pl.ds(pl.multiple_of(my_half + yz * SEG, 8), SEG)
+    fin[place, :] = whole
+
+    def gather(k, who):
+        there = pl.ds(pl.multiple_of(my_half + who * SEG, 8), SEG)
+        return put(fin.at[there], fin.at[there], s4.at[k], q4.at[k], chip(k))
+
+    def start_gather(k, carry):
+        gather(k, yz).start()
+        return carry
+
+    lax.fori_loop(1, 16, start_gather, 0)
+
+    rows = pl.ds(0, (DEVICES - 1) * CAP)
+    put(back.at[rows], came.at[rows], row_send, row_recv, device_at(peer_of(1))).wait()
+
     def take(n, carry):
         for u in range(16):
             b = n * 16 + u
-            grads[pl.ds(b, 1), :] = came_ref[pl.ds(where_ref[b], 1), :]
+            grads[pl.ds(b, 1), :] = came[pl.ds(where_ref[b], 1), :]
         return carry
 
     lax.fori_loop(0, BAGS // 16, take, 0)
@@ -191,6 +379,22 @@
         return carry
 
     lax.fori_loop(0, ROWS // 256, block, 0)
+
+    def wait_gather(k, carry):
+        gather(k, yz).wait_send()
+        gather(k, (yz + 16 - k) % 16).wait_recv()
+        return carry
+
+    lax.fori_loop(1, 16, wait_gather, 0)
+    half = fin.at[pl.ds(my_half, HALF)]
+    rest = fin.at[pl.ds(other, HALF)]
+    last = put(half, half, s5, q5, twin)
+    last.start()
+    last.wait_send()
+    put(rest, rest, s5, q5, twin).wait_recv()
+    for q in range(8):
+        top_ref[:, q * 128 : (q + 1) * 128] = fin[q * INTER : (q + 1) * INTER, :]
+        out_ref[:, q * 128 : (q + 1) * 128] = fin[8 * INTER + q : 8 * INTER + q + 1, :]
 
 
 def params(**kw):
@@ -212,10 +416,6 @@
         out.append(piece)
     held = jnp.concatenate([out[0], out[1][:cut]], axis=0)
     return held, out[1][cut:].reshape(1, ROWS)
-
-
-def swap_all(x):
-    return lax.all_to_all(x, ("gx", "gy"), split_axis=0, concat_axis=0, tiled=True)
 
 
 def on_device(
@@ -239,13 +439,14 @@
     where_to = owners * CAP + placed_at
     spot = (placed_at[:, None] == jnp.arange(CAP, dtype=i32)[None, :]).astype(f32)
     sample, feature = bag_slot // F, bag_slot % F
-    parts = jnp.concatenate(
-        [spot * (sample.astype(f32)[:, None]), spot * ((feature + 1).astype(f32)[:, None])], axis=1
-    )
+    bag = jnp.arange(BAGS, dtype=i32)
+    pieces = [sample, feature + 1, bag // 16, bag % 16]
+    parts = jnp.concatenate([spot * piece.astype(f32)[:, None] for piece in pieces], axis=1)
     coded = mxu(onehot.astype(bf16), parts.astype(bf16), ((0,), (0,))).astype(i32)
-    sample_at, feature_at = coded[:, :CAP], coded[:, CAP:]
+    sample_at, feature_at = coded[:, :CAP], coded[:, CAP : 2 * CAP]
     send_slots = jnp.where(feature_at > 0, (feature_at - 1) * B_DEV + sample_at, BAGS)
-    got_slots = swap_all(send_slots).reshape(DEVICES * CAP)
+    send_slots = jnp.pad(send_slots, ((0, 0), (0, 128 - CAP))).reshape(DEVICES, 1, 128)
+    send_bags = (coded[:, 2 * CAP : 3 * CAP] * 16 + coded[:, 3 * CAP :]).reshape(DEVICES * CAP)
 
     sizes = bag_sizes[0]
     ends = jnp.cumsum(sizes)
@@ -266,50 +467,83 @@
         name="count",
     )(first_bag, look_rows.reshape(LOOKS // 128, 128), starts2, ends2)
 
-    send_rows = pl.pallas_call(
+    dma = pltpu.SemaphoreType.DMA
+    got_rows, got_slots = pl.pallas_call(
         pool_kernel,
-        out_shape=jax.ShapeDtypeStruct((DEVICES * CAP, E), f32),
-        in_specs=[SMEM, VMEM, VMEM],
-        out_specs=VMEM,
-        scratch_shapes=[pltpu.VMEM((ROWS, 256), bf16), pltpu.VMEM((BAGS, E), f32)],
-        compiler_params=params(vmem_limit_bytes=24 << 20),
+        out_shape=(
+            jax.ShapeDtypeStruct((DEVICES * CAP, E), f32),
+            jax.ShapeDtypeStruct((DEVICES, 1, 128), i32),
+        ),
+        in_specs=[SMEM, VMEM, VMEM, VMEM],
+        out_specs=(VMEM, VMEM),
+        scratch_shapes=[
+            pltpu.VMEM((ROWS, 256), bf16),
+            pltpu.VMEM((BAGS, E), f32),
+            pltpu.VMEM((DEVICES * CAP, E), f32),
+            dma,
+            dma,
+            dma,
+            dma,
+        ],
+        compiler_params=params(collective_id=0, has_side_effects=True, vmem_limit_bytes=20 << 20),
         name="pool",
-    )(where_to, counts, held)
-    got_rows = swap_all(send_rows.reshape(DEVICES, CAP, E)).reshape(DEVICES * CAP, E)
-
-    back_rows, grads = pl.pallas_call(
+    )(send_bags, send_slots, counts, held)
+    slot_of = got_slots.reshape(DEVICES * 128)
+
+    pooled_grads, grads = pl.pallas_call(
         dense_kernel,
         out_shape=(
-            jax.ShapeDtypeStruct((DEVICES * CAP, E), f32),
-            jax.ShapeDtypeStruct((INTER + 8, HID), f32),
+            jax.ShapeDtypeStruct((BAGS + 8, E), f32),
+            jax.ShapeDtypeStruct((G_ROWS, 128), f32),
         ),
         in_specs=[SMEM, VMEM, VMEM, VMEM, VMEM, VMEM],
         out_specs=(VMEM, VMEM),
         scratch_shapes=[
-            pltpu.VMEM((BAGS, E), f32),
             pltpu.VMEM((F + 1, E, B_DEV), f32),
             pltpu.VMEM((INTER, B_DEV), f32),
         ],
-        compiler_params=params(vmem_limit_bytes=24 << 20),
+        compiler_params=params(vmem_limit_bytes=20 << 20),
         name="dense",
-    )(got_slots, got_rows, dense_vectors, labels[:, None], top_weight, out_weight[None, :])
-
-    came_back = swap_all(back_rows.reshape(DEVICES, CAP, E)).reshape(DEVICES * CAP, E)
-    total = lax.psum(grads[: INTER + 1], ("gx", "gy"))
-
-    new_table, new_state = pl.pallas_call(
+    )(slot_of, got_rows, dense_vectors, labels[:, None], top_weight, out_weight[None, :])
+
+    new_table, new_state, top_grad, out_grad = pl.pallas_call(
         update_kernel,
         out_shape=(
             jax.ShapeDtypeStruct((ROWS, E), f32),
             jax.ShapeDtypeStruct((1, ROWS), f32),
+            jax.ShapeDtypeStruct((INTER, HID), f32),
+            jax.ShapeDtypeStruct((1, HID), f32),
         ),
-        in_specs=[SMEM, VMEM, VMEM, VMEM, VMEM],
-        out_specs=(VMEM, VMEM),
-        scratch_shapes=[pltpu.VMEM((BAGS, E), f32), pltpu.VMEM((2 * E, BAGS), bf16)],
-        compiler_params=params(vmem_limit_bytes=24 << 20),
+        in_specs=[SMEM, SMEM, VMEM, VMEM, VMEM, VMEM, VMEM],
+        out_specs=(VMEM, VMEM, VMEM, VMEM),
+        scratch_shapes=[
+            pltpu.VMEM((DEVICES * CAP, E), f32),
+            pltpu.VMEM((DEVICES * CAP, E), f32),
+            pltpu.VMEM((BAGS, E), f32),
+            pltpu.VMEM((2 * E, BAGS), bf16),
+            pltpu.VMEM((G_ROWS, 128), f32),
+            pltpu.VMEM((HALF, 128), f32),
+            pltpu.VMEM((HALF, 128), f32),
+            pltpu.VMEM((16, SEG, 128), f32),
+            pltpu.VMEM((SEG, 128), f32),
+            pltpu.VMEM((4, SEG, 128), f32),
+            dma,
+            dma,
+            dma,
+            dma,
+            dma((16,)),
+            dma((16,)),
+            dma((4,)),
+            dma((4,)),
+            dma((16,)),
+            dma((16,)),
+            dma,
+            dma,
+        ],
+        compiler_params=params(collective_id=1, has_side_effects=True, vmem_limit_bytes=24 << 20),
         name="update",
-    )(where_to, counts, came_back, held, held_state)
-    return new_table, new_state.reshape(ROWS), total[:INTER], total[INTER]
+    )(slot_of, where_to, pooled_grads, grads, counts, held, held_state)
+    return new_table, new_state.reshape(ROWS), top_grad, out_grad.reshape(HID)
 
 
 def solution(mesh):

time: 318 us -> 179 us (0.56)
  waiting for transfers between devices: 200 us -> 24.9 us
  Pallas kernels: 42.7 us -> 126 us
  starting transfers between devices: 31.7 us -> 6.54 us
  between operations: 15 us -> 1.56 us
  local copies, waits for them, and re-layouts: 21.6 us -> 13.4 us
    psum x1 -> x0, waiting for transfers between devices: 160 us -> none  [on_device(): total = lax.psum(grads[:INTER + 1], ('gx', 'gy'))]
    pallas_call x1, Pallas kernels: 8.84 us -> 59.9 us  [on_device(): pl.pallas_call(update_kernel, out_shape=(jax.ShapeDtypeStruct((ROWS, E),...]
    pallas_call x2, Pallas kernels: 17.9 us -> 49.9 us  [the longest x1 41.1 us: on_device(): pl.pallas_call(pool_kernel, out_shape=(jax.ShapeDtypeStruct((DEVICES * CA...]
    all_to_all x3 -> x0, waiting for transfers between devices: 29.4 us -> none  [swap_all(): lax.all_to_all(x, ('gx', 'gy'), split_axis=0, concat_axis=0, tiled=True)]
    all_to_all x3 -> x0, starting transfers between devices: 22.9 us -> none  [swap_all(): lax.all_to_all(x, ('gx', 'gy'), split_axis=0, concat_axis=0, tiled=True)]
    ppermute x4, waiting for transfers between devices: 9.16 us -> 24.9 us  [from_partner(): return lax.ppermute(block, 'gy', [(y, y ^ flip) for y in range(4)])]
    slice x2 -> x0, local copies, waits for them, and re-layouts: 3.69 us -> none  [on_device(): return (new_table, new_state.reshape(ROWS), total[:INTER], total[INTER])]
  transfers between devices with their start and end apart: 8 -> 4, of which waited for: 3 -> 3; matrix products, arithmetic and copies ran while one was open for 4% -> 4% of each run, Pallas kernels for 7% -> 9%
where the time goes in v3:
time: 179 us; the launch traced here: 178 us
  Pallas kernels  126 us (70%)
  waiting for transfers between devices  24.9 us (14%)
  local copies, waits for them, and re-layouts  13.4 us (7%)
  starting transfers between devices  6.54 us (4%)
  other arithmetic  4.9 us (3%)
    pallas_call x1, Pallas kernels, on_device(): pl.pallas_call(update_kernel, out_shape=(jax.ShapeDtypeStruct((ROWS, E),...  59.9 us
    pallas_call x1, Pallas kernels, on_device(): pl.pallas_call(pool_kernel, out_shape=(jax.ShapeDtypeStruct((DEVICES * CA...  41.1 us
    ppermute x4, waiting for transfers between devices, from_partner(): return lax.ppermute(block, 'gy', [(y, y ^ flip) for y in range(4)])  24.9 us
    pallas_call x1, Pallas kernels, on_device(): pl.pallas_call(count_kernel, out_shape=jax.ShapeDtypeStruct((C_ROWS, ROWS...  16 us
    unnamed x30, local copies, waits for them, and re-layouts  11.4 us
    pallas_call x1, Pallas kernels, on_device(): pl.pallas_call(dense_kernel, out_shape=(jax.ShapeDtypeStruct((BAGS + 8, E...  8.81 us
    ppermute x4, starting transfers between devices, from_partner(): return lax.ppermute(block, 'gy', [(y, y ^ flip) for y in range(4)])  6.54 us
  transfers between devices with their start and end apart: 4, of which 3 were waited for; matrix products, arithmetic and copies ran while one was open for 4% of the time, Pallas kernels for 9%

profile of v3, /device:TPU:1, one launch (start us, length us, event | category | flops | bytes accessed | tf_op | source)
XLA Modules:
  0.0 178.3 jit_solution(11407776517169807323)
XLA Ops:
  0.7 1.1 slice.45
  1.7 2.1 %collective-permute-start = (f32[1024,128]{1,0:T(8,128)S(1)}, f32[1024,128]{1,0:T(8,128)S(1)}, u32[]{:S(2)}, u32[]{:S(2)}) collective-permute-start(f32[1024,128]{1,0:T(8,128)S(1)} %slice.45), channel_id=1, source_target_pairs={{0,1},{1,0},{2,3},{3,2},{4,5},{5,4},{6,7},{7,6},{8,9},{9,8},{10,11... | collective-permute-start | bytes 1572872 | tf_op jit(solution)/shard_map/ppermute | solution.py:405
  4.5 1.0 reduce-window.19
  5.6 0.1 slice_reduce_fusion
  5.8 0.1 copy.22
  5.9 0.3 fusion.2
  6.3 0.3 copy.23
  6.7 0.3 copy-done.10
  7.1 0.2 convert_reduce_fusion
  7.3 0.6 fusion.1
  7.9 2.0 %select_convert_fusion.3 = (bf16[2048,32]{1,0:T(8,128)(2,1)S(1)}, bf16[2048,32]{1,0:T(8,128)(2,1)S(1)}, bf16[2048,32]{1,0:T(8,128)(2,1)S(1)}, bf16[2048,32]{1,0:T(8,128)(2,1)S(1)}) fusion(bf16[2048]{0:T(1024)(128)(2,1)S(1)} %get-tuple-element.30, s32[2048]{0:T(1024)S(1)} %fusion.1, bf16[2048]{0:T(1024)(128)(2,1)S(1)} %fusion.24, ...), kind=kLoop, calls=%fused_computation.9 | loop fusion | flops 327680 | bytes 548864 | tf_op jit(solution)/shard_map/convert
  10.0 1.3 convolution_convert_fusion
  11.3 3.8 %collective-permute-done = f32[1024,128]{1,0:T(8,128)S(1)} collective-permute-done((f32[1024,128]{1,0:T(8,128)S(1)}, f32[1024,128]{1,0:T(8,128)S(1)}, u32[]{:S(2)}, u32[]{:S(2)}) %collective-permute-start) | collective-permute-done | bytes 524320 | tf_op jit(solution)/shard_map/ppermute | solution.py:405
  15.1 0.1 broadcast_select_fusion.2
  15.2 0.6 copy-done.9
  15.8 1.7 collective-permute-start.2
  17.5 16.0 %count.1.c_ref = bf16[2304,2048]{1,0:T(8,128)(2,1)S(1)} custom-call(s32[24]{0:T(128)S(1)} %fusion.28.first_ref, s32[48,128]{1,0:T(8,128)S(1)} %bitcast.35, s32[18,128]{1,0:T(8,128)S(1)} %get-tuple-element.34.start_ref, s32[18,128]{1,0:T(8,128)S(1)} %get-tuple-element.33.end_ref), custom_call_target="tpu_custom_call" | custom-call | flops 6845104128 | bytes 10485760 | tf_op jit(solution)/shard_map/count/pallas_call | solution.py:459
  33.5 3.6 %copy-done = bf16[2304,2048]{1,0:T(8,128)(2,1)} copy-done((bf16[2304,2048]{1,0:T(8,128)(2,1)}, bf16[2304,2048]{1,0:T(8,128)(2,1)S(1)}, u32[]{:S(2)}) %copy-start) | copy-done | bytes 9437208
  37.1 1.8 %collective-permute-start.1 = (f32[1024,128]{1,0:T(8,128)S(1)}, f32[1024,128]{1,0:T(8,128)S(1)}, u32[]{:S(2)}, u32[]{:S(2)}) collective-permute-start(f32[1024,128]{1,0:T(8,128)S(1)} %get-tuple-element.22), channel_id=1, source_target_pairs={{0,3},{1,2},{2,1},{3,0},{4,7},{5,6},{6,5},{7,4},{8,11},{9,10},{10,... | collective-permute-start | bytes 1572872 | tf_op jit(solution)/shard_map/ppermute | solution.py:405
  38.9 0.9 collective-permute-start.3
  39.9 0.1 fusion.13
  40.0 0.1 copy.25.label_ref
  40.2 9.7 %collective-permute-done.1 = f32[1024,128]{1,0:T(8,128)S(1)} collective-permute-done((f32[1024,128]{1,0:T(8,128)S(1)}, f32[1024,128]{1,0:T(8,128)S(1)}, u32[]{:S(2)}, u32[]{:S(2)}) %collective-permute-start.1) | collective-permute-done | bytes 524320 | tf_op jit(solution)/shard_map/ppermute | solution.py:405
  50.0 11.3 %collective-permute-done.3 = f32[1040,128]{1,0:T(8,128)S(1)} collective-permute-done((f32[1040,128]{1,0:T(8,128)S(1)}, f32[1040,128]{1,0:T(8,128)S(1)}, u32[]{:S(2)}, u32[]{:S(2)}) %collective-permute-start.3) | collective-permute-done | bytes 532512 | tf_op jit(solution)/shard_map/ppermute | solution.py:405
  61.6 3.7 %copy-done.1 = bf16[2304,2048]{1,0:T(8,128)(2,1)S(1)} copy-done((bf16[2304,2048]{1,0:T(8,128)(2,1)S(1)}, bf16[2304,2048]{1,0:T(8,128)(2,1)}, u32[]{:S(2)}) %copy-start.1) | copy-done | bytes 9437208
  65.3 41.1 %pool.1 = (f32[4096,128]{1,0:T(8,128)S(1)}, s32[128,1,128]{2,1,0:T(1,128)S(1)}) custom-call(s32[4096]{0:T(1024)S(1)} %reshape.120.bag_ref, s32[128,1,128]{2,1,0:T(1,128)S(1)} %bitcast.30, bf16[2304,2048]{1,0:T(8,128)(2,1)S(1)} %copy-done.1, f32[2048,128]{1,0:T(8,128)S(1)} %pad_maximum_fusion.table_ref), custom_call_target="tpu_custom_call" | custom-call | tf_op jit(solution)/shard_map/pool/pallas_call | solution.py:471
  106.4 8.8 %dense.1 = (f32[2056,128]{1,0:T(8,128)S(1)}, f32[2304,128]{1,0:T(8,128)S(1)}) custom-call(s32[16384]{0:T(1024)S(1)} %bitcast.28, f32[4096,128]{1,0:T(8,128)S(1)} %get-tuple-element.13.got_ref, f32[128,128]{1,0:T(8,128)S(1)} %copy-done.4, f32[128,1]{1,0:T(8,128)S(1)} %copy.25.label_ref, f32[264,1024]{1,0:T(8,128)S(1)} %copy-done.3, f32[1,1024]{1,0:T(1,128)S(1)} %bitcast.33), custom_call_target="tpu_custom_call" | custom-call | tf_op jit(solution)/shard_map/dense/pallas_call | solution.py:493
  115.2 59.9 %update.1 = (f32[2048,128]{1,0:T(8,128)S(1)}, f32[1,2048]{1,0:T(1,128)S(1)}, f32[264,1024]{1,0:T(8,128)S(1)}, f32[1,1024]{1,0:T(1,128)S(1)}) custom-call(s32[16384]{0:T(1024)S(1)} %bitcast.29, s32[2048]{0:T(1024)S(1)} %multiply_add_fusion.where_ref, f32[2056,128]{1,0:T(8,128)S(1)} %get-tuple-element.14.pooled_ref, f32[2304,128]{1,0:T(8,128)S(1)} %get-tuple-element.15.g_ref, ...), custom_call_target="tpu_custom_call" | custom-call | tf_op jit(solution)/shard_map/update/pallas_call | solution.py:509
  175.1 1.0 copy.32
  176.1 0.6 copy.33
  176.7 1.0 copy.34
  177.7 0.6 copy.35
  (45 shorter events, 0.8 us)
Async XLA Ops:
  0.6 5.1 %copy-start.11 = (s32[2048]{0:T(1024)S(1)}, s32[2048]{0:T(1024)}, u32[]{:S(2)}) copy-start(s32[2048]{0:T(1024)} %param.17) | copy-start | bytes 24580
  0.6 5.1 %copy-start.8 = (s32[2048,1]{0,1:T(1,128)S(1)}, s32[2048,1]{0,1:T(1,128)}, u32[]{:S(2)}) copy-start(s32[2048,1]{0,1:T(1,128)} %param.16) | copy-start | bytes 24580
  1.7 13.3 %collective-permute-start = (f32[1024,128]{1,0:T(8,128)S(1)}, f32[1024,128]{1,0:T(8,128)S(1)}, u32[]{:S(2)}, u32[]{:S(2)}) collective-permute-start(f32[1024,128]{1,0:T(8,128)S(1)} %slice.45), channel_id=1, source_target_pairs={{0,1},{1,0},{2,3},{3,2},{4,5},{5,4},{6,7},{7,6},{8,9},{9,8},{10,11... | collective-permute-start | bytes 1572872 | tf_op jit(solution)/shard_map/ppermute | solution.py:405
  6.3 0.7 copy-start.10
  10.0 5.1 %copy-start.7 = (f32[2048,128]{1,0:T(8,128)S(1)}, f32[2048,128]{1,0:T(8,128)}, u32[]{:S(2)}) copy-start(f32[2048,128]{1,0:T(8,128)} %param.11) | copy-start | bytes 3145732
  15.1 0.7 copy-start.9
  15.1 2.4 %copy-start.6 = (s32[6144]{0:T(1024)S(1)}, s32[6144]{0:T(1024)}, u32[]{:S(2)}) copy-start(s32[6144]{0:T(1024)} %param.14) | copy-start | bytes 73732
  15.8 23.1 %collective-permute-start.2 = (f32[1040,128]{1,0:T(8,128)S(1)}, f32[1040,128]{1,0:T(8,128)S(1)}, u32[]{:S(2)}, u32[]{:S(2)}) collective-permute-start(f32[1040,128]{1,0:T(8,128)S(1)} %pad_maximum_fusion.1), channel_id=1, source_target_pairs={{0,1},{1,0},{2,3},{3,2},{4,5},{5,4},{6,7},{7,6},{8,9},{9,8},{10,11... | collective-permute-start | bytes 1597448 | tf_op jit(solution)/shard_map/ppermute | solution.py:405
  33.5 3.6 %copy-start = (bf16[2304,2048]{1,0:T(8,128)(2,1)}, bf16[2304,2048]{1,0:T(8,128)(2,1)S(1)}, u32[]{:S(2)}) copy-start(bf16[2304,2048]{1,0:T(8,128)(2,1)S(1)} %count.1.c_ref) | copy-start | bytes 28311556
  37.1 3.0 %copy-start.12 = (f32[128]{0:T(128)S(1)}, f32[128]{0:T(128)}, u32[]{:S(2)}) copy-start(f32[128]{0:T(128)} %param.19) | copy-start | bytes 1540
  37.1 12.9 %collective-permute-start.1 = (f32[1024,128]{1,0:T(8,128)S(1)}, f32[1024,128]{1,0:T(8,128)S(1)}, u32[]{:S(2)}, u32[]{:S(2)}) collective-permute-start(f32[1024,128]{1,0:T(8,128)S(1)} %get-tuple-element.22), channel_id=1, source_target_pairs={{0,3},{1,2},{2,1},{3,0},{4,7},{5,6},{6,5},{7,4},{8,11},{9,10},{10,... | collective-permute-start | bytes 1572872 | tf_op jit(solution)/shard_map/ppermute | solution.py:405
  38.9 22.4 %collective-permute-start.3 = (f32[1040,128]{1,0:T(8,128)S(1)}, f32[1040,128]{1,0:T(8,128)S(1)}, u32[]{:S(2)}, u32[]{:S(2)}) collective-permute-start(f32[1040,128]{1,0:T(8,128)S(1)} %broadcast_select_fusion), channel_id=1, source_target_pairs={{0,3},{1,2},{2,1},{3,0},{4,7},{5,6},{6,5},{7,4},{8,11},{9,10},{10,... | collective-permute-start | bytes 1597448 | tf_op jit(solution)/shard_map/ppermute | solution.py:405
  61.5 44.9 %copy-start.4 = (f32[128,128]{1,0:T(8,128)S(1)}, f32[128,128]{1,0:T(8,128)}, u32[]{:S(2)}) copy-start(f32[128,128]{1,0:T(8,128)} %dense_ref.1) | copy-start | bytes 196612
  61.6 3.7 %copy-start.1 = (bf16[2304,2048]{1,0:T(8,128)(2,1)S(1)}, bf16[2304,2048]{1,0:T(8,128)(2,1)}, u32[]{:S(2)}) copy-start(bf16[2304,2048]{1,0:T(8,128)(2,1)} %copy-done) | copy-start | bytes 28311556
  65.3 41.1 %copy-start.3 = (f32[264,1024]{1,0:T(8,128)S(1)}, f32[264,1024]{1,0:T(8,128)}, u32[]{:S(2)}) copy-start(f32[264,1024]{1,0:T(8,128)} %w_ref.1) | copy-start | bytes 3244036
  65.3 41.1 %copy-start.5 = (f32[1024]{0:T(1024)S(1)}, f32[1024]{0:T(1024)}, u32[]{:S(2)}) copy-start(f32[1024]{0:T(1024)} %param.21) | copy-start | bytes 12292
  65.3 50.0 %copy-start.2 = (bf16[2304,2048]{1,0:T(8,128)(2,1)S(1)}, bf16[2304,2048]{1,0:T(8,128)(2,1)}, u32[]{:S(2)}) copy-start(bf16[2304,2048]{1,0:T(8,128)(2,1)} %copy-done) | copy-start | bytes 28311556

commit v4 on v3

--- a/solution.py
+++ b/solution.py
@@ -125,12 +125,17 @@
 
 
 def pool_kernel(
+    mask_ref,
     bag_ref,
     slots_ref,
     c_ref,
-    table_ref,
+    a_ref,
+    a2_ref,
+    b_ref,
+    b2_ref,
     recv_ref,
     got_ref,
+    held_ref,
     split_ref,
     partial_ref,
     send_ref,
@@ -142,7 +147,10 @@
     barrier = pltpu.get_barrier_semaphore()
     greet_all(barrier)
     me = my_number()
-    hi, lo = split(table_ref[...])
+    mask = jnp.full((ROWS // 2, E), mask_ref[0], i32)
+    held_ref[: ROWS // 2, :] = jnp.where(mask >= 2, a2_ref[...], a_ref[...])
+    held_ref[ROWS // 2 :, :] = jnp.where((mask == 1) | (mask == 2), b2_ref[...], b_ref[...])
+    hi, lo = split(held_ref[...])
     split_ref[:, :128] = hi
     split_ref[:, 128:] = lo
 
@@ -236,6 +244,7 @@
 
 
 def update_kernel(
+    mask_ref,
     slot_ref,
     where_ref,
     pooled_ref,
@@ -257,6 +266,9 @@
     r2,
     mine,
     r3,
+    states,
+    state_send,
+    state_recv,
     row_send,
     row_recv,
     s1,
@@ -305,6 +317,13 @@
     other = pl.multiple_of((1 - core) * HALF, 8)
     swap = put(g_ref.at[pl.ds(other, HALF)], r1, s1, q1, twin)
     swap.start()
+    flips = [None, x + 1 - 2 * (x % 2), (x + 2) % 4, 3 - x]
+    state_moves = [
+        put(state_ref, states.at[f], state_send.at[f], state_recv.at[f], (gx, flips[f]))
+        for f in range(1, 4)
+    ]
+    for move in state_moves:
+        move.start()
     lax.fori_loop(1, CUT_A, start, 0)
     swap.wait()
     acc[...] = g_ref[pl.ds(my_half, HALF), :] + r1[...]
@@ -355,6 +374,14 @@
     rows = pl.ds(0, (DEVICES - 1) * CAP)
     put(back.at[rows], came.at[rows], row_send, row_recv, device_at(peer_of(1))).wait()
 
+    for move in state_moves:
+        move.wait()
+    mask = jnp.full((1, ROWS), mask_ref[0], i32)
+    held_state = state_ref[...]
+    for f in range(1, 4):
+        held_state = jnp.where(mask == f, states[f], held_state)
+    states[0] = held_state
+
     def take(n, carry):
         for u in range(16):
             b = n * 16 + u
@@ -372,7 +399,7 @@
         here = pl.ds(pl.multiple_of(n * 256, 256), 256)
         both = mxu(sides[...], c_ref[0:BAGS, here], NN)
         row_grad = both[:128] + both[128:]
-        state = state_ref[:, here] + jnp.sum(row_grad * row_grad, axis=0, keepdims=True) * (1.0 / E)
+        state = states[0, :, here] + jnp.sum(row_grad * row_grad, axis=0, keepdims=True) * (1.0 / E)
         new_state_ref[:, here] = state
         step = row_grad * (learn_rate / (jnp.sqrt(state) + epsilon))
         new_table_ref[here, :] = table_ref[here, :] - step.T
@@ -403,19 +430,6 @@
 
 def from_partner(block, flip):
     return lax.ppermute(block, "gy", [(y, y ^ flip) for y in range(4)])
-
-
-def trade_blocks(table, state, mask):
-    first, second = (mask == 1) | (mask == 2), mask >= 2
-    cut = ROWS // 2
-    pieces = [table[:cut], jnp.concatenate([table[cut:], state.reshape(16, 128)], axis=0)]
-    out = []
-    for piece in pieces:
-        piece = jnp.where(first, from_partner(piece, 1), piece)
-        piece = jnp.where(second, from_partner(piece, 3), piece)
-        out.append(piece)
-    held = jnp.concatenate([out[0], out[1][:cut]], axis=0)
-    return held, out[1][cut:].reshape(1, ROWS)
 
 
 def on_device(
@@ -431,7 +445,11 @@
     top_weight,
     out_weight,
 ):
-    held, held_state = trade_blocks(emb_table, row_state, pair_mask[0])
+    mask = pair_mask[0]
+    first, second = (mask == 1) | (mask == 2), mask >= 2
+    upper, lower = emb_table[: ROWS // 2], emb_table[ROWS // 2 :]
+    upper = jnp.where(first, from_partner(upper, 1), upper)
+    lower = jnp.where(second, from_partner(lower, 3), lower)
 
     owners = bag_owner[:, 0]
     onehot = (owners[:, None] == jnp.arange(DEVICES, dtype=i32)[None, :]).astype(i32)
@@ -456,6 +474,10 @@
     extra = C_ROWS - BAGS
     ends2 = jnp.concatenate([ends, jnp.zeros((extra,), i32)]).reshape(C_ROWS // 128, 128)
     starts2 = jnp.concatenate([starts, jnp.full((extra,), LOOKS, i32)]).reshape(C_ROWS // 128, 128)
+    upper, lower, look_rows, first_bag, starts2, ends2 = lax.optimization_barrier(
+        (upper, lower, look_rows, first_bag, starts2, ends2)
+    )
+    upper2, lower2 = from_partner(upper, 3), from_partner(lower, 1)
     counts = pl.pallas_call(
         count_kernel,
         out_shape=jax.ShapeDtypeStruct((C_ROWS, ROWS), bf16),
@@ -468,14 +490,15 @@
     )(first_bag, look_rows.reshape(LOOKS // 128, 128), starts2, ends2)
 
     dma = pltpu.SemaphoreType.DMA
-    got_rows, got_slots = pl.pallas_call(
+    got_rows, got_slots, held = pl.pallas_call(
         pool_kernel,
         out_shape=(
             jax.ShapeDtypeStruct((DEVICES * CAP, E), f32),
             jax.ShapeDtypeStruct((DEVICES, 1, 128), i32),
+            jax.ShapeDtypeStruct((ROWS, E), f32),
         ),
-        in_specs=[SMEM, VMEM, VMEM, VMEM],
-        out_specs=(VMEM, VMEM),
+        in_specs=[SMEM, SMEM, VMEM, VMEM, VMEM, VMEM, VMEM, VMEM],
+        out_specs=(VMEM, VMEM, VMEM),
         scratch_shapes=[
             pltpu.VMEM((ROWS, 256), bf16),
             pltpu.VMEM((BAGS, E), f32),
@@ -487,7 +510,7 @@
         ],
         compiler_params=params(collective_id=0, has_side_effects=True, vmem_limit_bytes=20 << 20),
         name="pool",
-    )(send_bags, send_slots, counts, held)
+    )(pair_mask, send_bags, send_slots, counts, upper, upper2, lower, lower2)
     slot_of = got_slots.reshape(DEVICES * 128)
 
     pooled_grads, grads = pl.pallas_call(
@@ -514,7 +537,7 @@
             jax.ShapeDtypeStruct((INTER, HID), f32),
             jax.ShapeDtypeStruct((1, HID), f32),
         ),
-        in_specs=[SMEM, SMEM, VMEM, VMEM, VMEM, VMEM, VMEM],
+        in_specs=[SMEM, SMEM, SMEM, VMEM, VMEM, VMEM, VMEM, VMEM],
         out_specs=(VMEM, VMEM, VMEM, VMEM),
         scratch_shapes=[
             pltpu.VMEM((DEVICES * CAP, E), f32),
@@ -527,6 +550,9 @@
             pltpu.VMEM((16, SEG, 128), f32),
             pltpu.VMEM((SEG, 128), f32),
             pltpu.VMEM((4, SEG, 128), f32),
+            pltpu.VMEM((4, 1, ROWS), f32),
+            dma((4,)),
+            dma((4,)),
             dma,
             dma,
             dma,
@@ -542,7 +568,7 @@
         ],
         compiler_params=params(collective_id=1, has_side_effects=True, vmem_limit_bytes=24 << 20),
         name="update",
-    )(slot_of, where_to, pooled_grads, grads, counts, held, held_state)
+    )(pair_mask, slot_of, where_to, pooled_grads, grads, counts, held, row_state[None, :])
     return new_table, new_state.reshape(ROWS), top_grad, out_grad.reshape(HID)
 
 

time: 179 us -> 149 us (0.83)
  waiting for transfers between devices: 24.9 us -> 5.79 us
  local copies, waits for them, and re-layouts: 13.4 us -> 5.33 us
    ppermute x4, waiting for transfers between devices: 24.9 us -> 5.79 us  [from_partner(): return lax.ppermute(block, 'gy', [(y, y ^ flip) for y in range(4)])]
    unnamed x30 -> x24, local copies, waits for them, and re-layouts: 11.4 us -> 3.2 us
  transfers between devices with their start and end apart: 4 -> 4, of which waited for: 3 -> 2; matrix products, arithmetic and copies ran while one was open for 4% -> 4% of each run, Pallas kernels for 9% -> 11%
where the time goes in v4:
time: 149 us
  Pallas kernels  126 us (85%)
  waiting for transfers between devices  5.79 us (4%)
  local copies, waits for them, and re-layouts  5.33 us (4%)
  starting transfers between devices  4.97 us (3%)
  other arithmetic  3.92 us (3%)
  between operations  1.57 us (1%)
    pallas_call x1, Pallas kernels, on_device(): pl.pallas_call(update_kernel, out_shape=(jax.ShapeDtypeStruct((ROWS, E),...  59.3 us
    pallas_call x1, Pallas kernels, on_device(): pl.pallas_call(pool_kernel, out_shape=(jax.ShapeDtypeStruct((DEVICES * CA...  41.9 us
    pallas_call x1, Pallas kernels, on_device(): pl.pallas_call(count_kernel, out_shape=jax.ShapeDtypeStruct((C_ROWS, ROWS...  16 us
    pallas_call x1, Pallas kernels, on_device(): pl.pallas_call(dense_kernel, out_shape=(jax.ShapeDtypeStruct((BAGS + 8, E...  8.8 us
    ppermute x4, waiting for transfers between devices, from_partner(): return lax.ppermute(block, 'gy', [(y, y ^ flip) for y in range(4)])  5.79 us
    ppermute x4, starting transfers between devices, from_partner(): return lax.ppermute(block, 'gy', [(y, y ^ flip) for y in range(4)])  4.97 us
    unnamed x24, local copies, waits for them, and re-layouts  3.2 us
  transfers between devices with their start and end apart: 4, of which 2 were waited for; matrix products, arithmetic and copies ran while one was open for 4% of the time, Pallas kernels for 11%

profile of v4, /device:TPU:1, one launch (start us, length us, event | category | flops | bytes accessed | tf_op | source)
XLA Modules:
  0.0 148.9 jit_solution(9423796442156507536)
XLA Ops:
  0.7 1.3 fusion.31
  2.0 3.4 %collective-permute-start.1 = (f32[1024,128]{1,0:T(8,128)S(1)}, f32[1024,128]{1,0:T(8,128)S(1)}, u32[]{:S(2)}, u32[]{:S(2)}) collective-permute-start(f32[1024,128]{1,0:T(8,128)S(1)} %get-tuple-element.38), channel_id=1, source_target_pairs={{0,3},{1,2},{2,1},{3,0},{4,7},{5,6},{6,5},{7,4},{8,11},{9,10},{10,... | collective-permute-start | bytes 1572872 | tf_op jit(solution)/shard_map/ppermute | solution.py:432
  6.0 0.3 reduce-window.19
  6.3 0.1 slice.47
  6.4 0.1 slice_reduce_fusion
  6.6 0.1 copy.25.label_ref
  6.7 0.1 copy.22
  6.8 0.3 fusion.2
  7.2 0.1 broadcast_add_fusion
  7.3 0.3 copy.23
  7.6 0.6 fusion.1
  8.3 2.0 %select_convert_fusion.3 = (bf16[2048,32]{1,0:T(8,128)(2,1)S(1)}, bf16[2048,32]{1,0:T(8,128)(2,1)S(1)}, bf16[2048,32]{1,0:T(8,128)(2,1)S(1)}, bf16[2048,32]{1,0:T(8,128)(2,1)S(1)}) fusion(bf16[2048]{0:T(1024)(128)(2,1)S(1)} %get-tuple-element.46, s32[2048]{0:T(1024)S(1)} %fusion.1, bf16[2048]{0:T(1024)(128)(2,1)S(1)} %fusion.24, ...), kind=kLoop, calls=%fused_computation.8 | loop fusion | flops 327680 | bytes 548864 | tf_op jit(solution)/shard_map/convert
  10.3 0.0 copy-start.5
  10.3 1.3 convolution_convert_fusion
  11.6 0.1 fusion.13
  11.7 0.1 reshape.114.bag_ref
  11.8 0.1 fusion.30
  11.8 0.2 convert_reduce_fusion
  12.1 4.5 %collective-permute-done.1 = f32[1024,128]{1,0:T(8,128)S(1)} collective-permute-done((f32[1024,128]{1,0:T(8,128)S(1)}, f32[1024,128]{1,0:T(8,128)S(1)}, u32[]{:S(2)}, u32[]{:S(2)}) %collective-permute-start.1) | collective-permute-done | bytes 524320 | tf_op jit(solution)/shard_map/ppermute | solution.py:432
  16.6 1.3 collective-permute-done
  17.9 0.1 broadcast_select_fusion
  18.0 1.6 %collective-permute-start.2 = (f32[1024,128]{1,0:T(8,128)S(1)}, f32[1024,128]{1,0:T(8,128)S(1)}, u32[]{:S(2)}, u32[]{:S(2)}) collective-permute-start(f32[1024,128]{1,0:T(8,128)S(1)} %get-tuple-element.23.a_ref), channel_id=1, source_target_pairs={{0,3},{1,2},{2,1},{3,0},{4,7},{5,6},{6,5},{7,4},{8,11},{9,10},{10,... | collective-permute-start | bytes 1572872 | tf_op jit(solution)/shard_map/ppermute | solution.py:432
  19.6 16.0 %count.1.c_ref = bf16[2304,2048]{1,0:T(8,128)(2,1)S(1)} custom-call(s32[24]{0:T(128)S(1)} %fusion.28.first_ref, s32[48,128]{1,0:T(8,128)S(1)} %bitcast.34, s32[18,128]{1,0:T(8,128)S(1)} %get-tuple-element.21.start_ref, s32[18,128]{1,0:T(8,128)S(1)} %get-tuple-element.22.end_ref), custom_call_target="tpu_custom_call" | custom-call | flops 6845104128 | bytes 10485760 | tf_op jit(solution)/shard_map/count/pallas_call | solution.py:481
  35.6 0.0 copy-start.1
  35.6 0.0 copy-start.3
  35.6 41.9 %pool.1 = (f32[4096,128]{1,0:T(8,128)S(1)}, s32[128,1,128]{2,1,0:T(1,128)S(1)}, f32[2048,128]{1,0:T(8,128)S(1)}) custom-call(s32[1]{0:T(128)S(6)} %copy.31.mask_ref, s32[4096]{0:T(1024)S(1)} %reshape.114.bag_ref, s32[128,1,128]{2,1,0:T(1,128)S(1)} %bitcast.29, bf16[2304,2048]{1,0:T(8,128)(2,1)S(1)} %count.1.c_ref, f32[1024,128]{1,0:T(8,128)S(1)} %get-tuple-element.23.a_ref, ...), custom_call_target="tpu_custom_call" | custom-call | tf_op jit(solution)/shard_map/pool/pallas_call | solution.py:493
  77.6 8.8 %dense.1 = (f32[2056,128]{1,0:T(8,128)S(1)}, f32[2304,128]{1,0:T(8,128)S(1)}) custom-call(s32[16384]{0:T(1024)S(1)} %bitcast.27, f32[4096,128]{1,0:T(8,128)S(1)} %get-tuple-element.26.got_ref, f32[128,128]{1,0:T(8,128)S(1)} %copy-done.1, f32[128,1]{1,0:T(8,128)S(1)} %copy.25.label_ref, f32[264,1024]{1,0:T(8,128)S(1)} %copy-done, f32[1,1024]{1,0:T(1,128)S(1)} %bitcast.32), custom_call_target="tpu_custom_call" | custom-call | tf_op jit(solution)/shard_map/dense/pallas_call | solution.py:516
  86.4 59.3 %update.1 = (f32[2048,128]{1,0:T(8,128)S(1)}, f32[1,2048]{1,0:T(1,128)S(1)}, f32[264,1024]{1,0:T(8,128)S(1)}, f32[1,1024]{1,0:T(1,128)S(1)}) custom-call(s32[1]{0:T(128)S(6)} %copy.31.mask_ref, s32[16384]{0:T(1024)S(1)} %bitcast.28, s32[2048]{0:T(1024)S(1)} %multiply_add_fusion.where_ref, f32[2056,128]{1,0:T(8,128)S(1)} %get-tuple-element.27.pooled_ref, ...), custom_call_target="tpu_custom_call" | custom-call | tf_op jit(solution)/shard_map/update/pallas_call | solution.py:532
  145.7 1.0 copy.32
  146.7 0.6 copy.33
  147.3 1.0 copy.34
  148.3 0.6 copy.35
  (32 shorter events, 0.2 us)
Async XLA Ops:
  0.6 5.4 %copy-start.7 = (s32[1,2048]{1,0:T(1,128)S(1)}, s32[1,2048]{1,0:T(1,128)}, u32[]{:S(2)}) copy-start(s32[1,2048]{1,0:T(1,128)} %param.15) | copy-start | bytes 24580
  0.6 5.9 %copy-start.8 = (s32[2048]{0:T(1024)S(1)}, s32[2048]{0:T(1024)}, u32[]{:S(2)}) copy-start(s32[2048]{0:T(1024)} %param.17) | copy-start | bytes 24580
  0.7 5.9 %copy-start.9 = (f32[128]{0:T(128)S(1)}, f32[128]{0:T(128)}, u32[]{:S(2)}) copy-start(f32[128]{0:T(128)} %param.19) | copy-start | bytes 1540
  0.7 6.0 %copy-start.6 = (s32[2048,1]{0,1:T(1,128)S(1)}, s32[2048,1]{0,1:T(1,128)}, u32[]{:S(2)}) copy-start(s32[2048,1]{0,1:T(1,128)} %param.16) | copy-start | bytes 24580
  2.0 14.6 %collective-permute-start.1 = (f32[1024,128]{1,0:T(8,128)S(1)}, f32[1024,128]{1,0:T(8,128)S(1)}, u32[]{:S(2)}, u32[]{:S(2)}) collective-permute-start(f32[1024,128]{1,0:T(8,128)S(1)} %get-tuple-element.38), channel_id=1, source_target_pairs={{0,3},{1,2},{2,1},{3,0},{4,7},{5,6},{6,5},{7,4},{8,11},{9,10},{10,... | collective-permute-start | bytes 1572872 | tf_op jit(solution)/shard_map/ppermute | solution.py:432
  5.3 12.5 %collective-permute-start = (f32[1024,128]{1,0:T(8,128)S(1)}, f32[1024,128]{1,0:T(8,128)S(1)}, u32[]{:S(2)}, u32[]{:S(2)}) collective-permute-start(f32[1024,128]{1,0:T(8,128)S(1)} %get-tuple-element.39), channel_id=1, source_target_pairs={{0,1},{1,0},{2,3},{3,2},{4,5},{5,4},{6,7},{7,6},{8,9},{9,8},{10,11... | collective-permute-start | bytes 1572872 | tf_op jit(solution)/shard_map/ppermute | solution.py:432
  10.3 7.6 %copy-start.5 = (f32[2048,128]{1,0:T(8,128)S(1)}, f32[2048,128]{1,0:T(8,128)}, u32[]{:S(2)}) copy-start(f32[2048,128]{1,0:T(8,128)} %param.11) | copy-start | bytes 3145732
  17.9 1.7 %copy-start.4 = (s32[6144]{0:T(1024)S(1)}, s32[6144]{0:T(1024)}, u32[]{:S(2)}) copy-start(s32[6144]{0:T(1024)} %param.14) | copy-start | bytes 73732
  18.0 17.6 %collective-permute-start.2 = (f32[1024,128]{1,0:T(8,128)S(1)}, f32[1024,128]{1,0:T(8,128)S(1)}, u32[]{:S(2)}, u32[]{:S(2)}) collective-permute-start(f32[1024,128]{1,0:T(8,128)S(1)} %get-tuple-element.23.a_ref), channel_id=1, source_target_pairs={{0,3},{1,2},{2,1},{3,0},{4,7},{5,6},{6,5},{7,4},{8,11},{9,10},{10,... | collective-permute-start | bytes 1572872 | tf_op jit(solution)/shard_map/ppermute | solution.py:432
  19.6 16.0 %collective-permute-start.3 = (f32[1024,128]{1,0:T(8,128)S(1)}, f32[1024,128]{1,0:T(8,128)S(1)}, u32[]{:S(2)}, u32[]{:S(2)}) collective-permute-start(f32[1024,128]{1,0:T(8,128)S(1)} %get-tuple-element.24.b_ref), channel_id=1, source_target_pairs={{0,1},{1,0},{2,3},{3,2},{4,5},{5,4},{6,7},{7,6},{8,9},{9,8},{10,11... | collective-permute-start | bytes 1572872 | tf_op jit(solution)/shard_map/ppermute | solution.py:432
  35.6 42.0 %copy-start = (f32[264,1024]{1,0:T(8,128)S(1)}, f32[264,1024]{1,0:T(8,128)}, u32[]{:S(2)}) copy-start(f32[264,1024]{1,0:T(8,128)} %w_ref.1) | copy-start | bytes 3244036
  35.6 42.0 %copy-start.1 = (f32[128,128]{1,0:T(8,128)S(1)}, f32[128,128]{1,0:T(8,128)}, u32[]{:S(2)}) copy-start(f32[128,128]{1,0:T(8,128)} %dense_ref.1) | copy-start | bytes 196612
  35.6 42.0 %copy-start.3 = (f32[1024]{0:T(1024)S(1)}, f32[1024]{0:T(1024)}, u32[]{:S(2)}) copy-start(f32[1024]{0:T(1024)} %param.21) | copy-start | bytes 12292
  77.6 8.8 %copy-start.2 = (f32[2048]{0:T(1024)S(1)}, f32[2048]{0:T(1024)}, u32[]{:S(2)}) copy-start(f32[2048]{0:T(1024)} %param.12) | copy-start | bytes 24580

commit v5 on v4

--- a/solution.py
+++ b/solution.py
@@ -20,9 +20,9 @@
 C_ROWS = 2304
 G_ROWS = 2304
 HALF = G_ROWS // 2
-SEG = HALF // 16
+PART = (40, 32)
 STRIDE = 37
-CUT_A, CUT_B = 48, 88
+CUTS = (1, 36, 60, 84, 108, 128)
 PAIRS = [(i, j) for i in range(F + 1) for j in range(i + 1, F + 1)]
 PAIR_ROW = {pair: 128 + n for n, pair in enumerate(PAIRS)}
 
@@ -192,9 +192,8 @@
 
 
 def dense_kernel(
-    slot_ref, got_ref, dense_ref, label_ref, w_ref, wo_ref, pooled, grad_ref, vt, inter_t
+    slot_ref, got_ref, dense_ref, label_ref, w_ref, wo_ref, vt, d_pre_ref, grad_ref, pooled, inter_t
 ):
-    pooled[BAGS:, :] = jnp.zeros((8, E), f32)
 
     def place(c, carry):
         @pl.when(slot_ref[c * 128] < BAGS)
@@ -227,27 +226,19 @@
     for q in range(8):
         grad_ref[8 * INTER + q : 8 * INTER + q + 1, :] = out_grad[:, q * 128 : (q + 1) * 128]
     grad_ref[8 * INTER + 8 :, :] = jnp.zeros((G_ROWS - 8 * INTER - 8, 128), f32)
-    d_pre = split(d_logits * wo_ref[...] * (sig * (1.0 + pre * (1.0 - sig))))
-    top_grad = dot3(split(it), d_pre, NN)
+    d_pre_ref[...] = d_logits * wo_ref[...] * (sig * (1.0 + pre * (1.0 - sig)))
+    top_grad = dot3(split(it), split(d_pre_ref[...]), NN)
     for q in range(8):
         grad_ref[q * INTER : (q + 1) * INTER, :] = top_grad[:, q * 128 : (q + 1) * 128]
-    inter_t[...] = dot3(w, d_pre, NT)
-
-    for j in range(1, F + 1):
-        total = None
-        for i in range(F + 1):
-            if i != j:
-                row = PAIR_ROW[min(i, j), max(i, j)]
-                term = inter_t[row : row + 1, :] * vt[i]
-                total = term if total is None else total + term
-        pooled[(j - 1) * 128 : j * 128, :] = total.T
 
 
 def update_kernel(
     mask_ref,
     slot_ref,
     where_ref,
-    pooled_ref,
+    vt,
+    d_pre_ref,
+    w_ref,
     g_ref,
     c_ref,
     table_ref,
@@ -261,26 +252,31 @@
     grads,
     sides,
     fin,
+    pooled,
+    d_inter,
     r1,
     acc,
-    r2,
-    mine,
-    r3,
     states,
+    ra0,
+    ra1,
+    acc0,
+    acc1,
+    rb0,
+    rb1,
+    mine0,
+    mine1,
+    rx0,
+    rx1,
     state_send,
     state_recv,
     row_send,
     row_recv,
-    s1,
-    q1,
-    s2,
-    q2,
-    s3,
-    q3,
-    s4,
-    q4,
-    s5,
-    q5,
+    swap_send,
+    swap_recv,
+    last_send,
+    last_recv,
+    color_send,
+    color_recv,
 ):
     barrier = pltpu.get_barrier_semaphore()
     greet_all(barrier)
@@ -289,33 +285,131 @@
     yz, core = gx // 2, gx % 2
     twin = (gx + 1 - 2 * core, x)
 
-    def chip(k):
-        return (((yz + k) % 16) * 2 + core, x)
-
-    def along(k):
+    y, z = yz // 4, yz % 4
+
+    def along_x(k):
         return (gx, (x + k) % 4)
 
-    pick_rows(came, me * CAP, pooled_ref, slot_ref, me * 128)
-
-    def ready(k, carry):
+    def along_y(k):
+        return (((y + k) % 4 * 4 + z) * 2 + core, x)
+
+    def along_z(k):
+        return ((y * 4 + (z + k) % 4) * 2 + core, x)
+
+    d_inter[...] = dot3(split(w_ref[...]), split(d_pre_ref[...]), NT)
+    for j in range(1, F + 1):
+        total = None
+        for i in range(F + 1):
+            if i != j:
+                row = PAIR_ROW[min(i, j), max(i, j)]
+                term = d_inter[row : row + 1, :] * vt[i]
+                total = term if total is None else total + term
+        pooled[(j - 1) * 128 : j * 128, :] = total.T
+    pooled[BAGS:, :] = jnp.zeros((8, E), f32)
+    pick_rows(came, me * CAP, pooled, slot_ref, me * 128)
+
+    def ready(k):
         peer = peer_of(k)
-        pick_rows(back, peer * CAP, pooled_ref, slot_ref, peer * 128)
-        return carry
-
-    lax.fori_loop(1, DEVICES, ready, 0)
-
-    def start(k, carry):
+        pick_rows(back, peer * CAP, pooled, slot_ref, peer * 128)
+
+    def start(k):
         peer = peer_of(k)
         put(
             back.at[chunk_at(peer)], came.at[chunk_at(me)], row_send, row_recv, device_at(peer)
         ).start()
-        return carry
-
-    pl.semaphore_wait(barrier, DEVICES - 1)
-
+
+    def send_rows(n):
+        def step(k, carry):
+            ready(k + 1)
+            start(k)
+            return carry
+
+        last = DEVICES - 1 if CUTS[n + 1] == DEVICES else CUTS[n + 1]
+        lax.fori_loop(CUTS[n], last, step, 0)
+        if last < CUTS[n + 1]:
+            start(last)
+
+    ready(1)
     my_half = pl.multiple_of(core * HALF, 8)
     other = pl.multiple_of((1 - core) * HALF, 8)
-    swap = put(g_ref.at[pl.ds(other, HALF)], r1, s1, q1, twin)
+
+    class Color:
+        def __init__(self, n, base, at, to_a, to_b, ra, acc2, rb, mine, rx):
+            self.n, self.rows, self.base, self.at = n, PART[n], base, at
+            self.to = (to_a, to_b, along_x, to_b, to_a)
+            self.ra, self.acc2, self.rb, self.mine, self.rx = ra, acc2, rb, mine, rx
+
+        def move(self, phase, k, src, dst):
+            sem = (self.n * 5 + phase) * 4 + k
+            return put(src, dst, color_send.at[sem], color_recv.at[sem], self.to[phase](k))
+
+        def rows_a(self, a, base):
+            return pl.ds(pl.multiple_of(base + self.base + a * (4 * self.rows), 8), 4 * self.rows)
+
+        def rows_b(self, a, b, base):
+            return pl.ds(
+                pl.multiple_of(base + self.base + (a * 4 + b) * self.rows, 8), self.rows
+            )
+
+        def moves(self, phase, waiting):
+            a, b = self.at
+            out = []
+            for k in range(1, 4):
+                if phase == 0:
+                    out.append(self.move(0, k, acc.at[self.rows_a((a + k) % 4, 0)], self.ra.at[k]))
+                if phase == 1:
+                    there = pl.ds(pl.multiple_of((b + k) % 4 * self.rows, 8), self.rows)
+                    out.append(self.move(1, k, self.acc2.at[there], self.rb.at[k]))
+                if phase == 2:
+                    slot = (x + 4 - k) % 4 if waiting else x
+                    out.append(self.move(2, k, self.mine, self.rx.at[slot]))
+                if phase == 3:
+                    who = (b + 4 - k) % 4 if waiting else b
+                    there = fin.at[self.rows_b(a, who, my_half)]
+                    out.append(self.move(3, k, there, there))
+                if phase == 4:
+                    who = (a + 4 - k) % 4 if waiting else a
+                    there = fin.at[self.rows_a(who, my_half)]
+                    out.append(self.move(4, k, there, there))
+            return out
+
+        def begin(self, phase):
+            for copy in self.moves(phase, False):
+                copy.start()
+
+        def finish(self, phase):
+            for copy in self.moves(phase, False):
+                copy.wait_send()
+            for copy in self.moves(phase, True):
+                copy.wait_recv()
+            a, b = self.at
+            if phase == 0:
+                own = acc[self.rows_a(a, 0), :]
+                self.acc2[...] = (own + self.ra[1]) + (self.ra[2] + self.ra[3])
+            if phase == 1:
+                own = self.acc2[pl.ds(pl.multiple_of(b * self.rows, 8), self.rows), :]
+                part = (own + self.rb[1]) + (self.rb[2] + self.rb[3])
+                self.mine[...] = part
+                self.rx[x] = part
+            if phase == 2:
+                whole = (self.rx[0] + self.rx[1]) + (self.rx[2] + self.rx[3])
+                fin[self.rows_b(a, b, my_half), :] = whole
+
+    colors = (
+        Color(0, 0, (z, y), along_z, along_y, ra0, acc0, rb0, mine0, rx0),
+        Color(1, 16 * PART[0], (y, z), along_y, along_z, ra1, acc1, rb1, mine1, rx1),
+    )
+
+    def phase_on(phase):
+        for color in colors:
+            color.begin(phase)
+
+    def phase_off(phase):
+        for color in colors:
+            color.finish(phase)
+
+    pl.semaphore_wait(barrier, DEVICES - 1)
+    swap = put(g_ref.at[pl.ds(other, HALF)], r1, swap_send, swap_recv, twin)
     swap.start()
     flips = [None, x + 1 - 2 * (x % 2), (x + 2) % 4, 3 - x]
     state_moves = [
@@ -324,56 +418,17 @@
     ]
     for move in state_moves:
         move.start()
-    lax.fori_loop(1, CUT_A, start, 0)
+    send_rows(0)
     swap.wait()
     acc[...] = g_ref[pl.ds(my_half, HALF), :] + r1[...]
-
-    def seg(n):
-        return pl.ds(pl.multiple_of(n * SEG, 8), SEG)
-
-    def scatter(k):
-        return put(acc.at[seg((yz + k) % 16)], r2.at[k], s2.at[k], q2.at[k], chip(k))
-
-    def start_scatter(k, carry):
-        scatter(k).start()
-        return carry
-
-    lax.fori_loop(1, 16, start_scatter, 0)
-    lax.fori_loop(CUT_A, CUT_B, start, 0)
-    r2[0] = acc[seg(yz), :]
-
-    def wait_scatter(k, carry):
-        scatter(k).wait()
-        return carry
-
-    lax.fori_loop(1, 16, wait_scatter, 0)
-    part = r2[0]
-    for k in range(1, 16):
-        part = part + r2[k]
-    mine[...] = part
-    r3[x] = part
-    for k in range(1, 4):
-        put(mine, r3.at[x], s3.at[k], q3.at[k], along(k)).start()
-    lax.fori_loop(CUT_B, DEVICES, start, 0)
-    for k in range(1, 4):
-        put(mine, r3.at[(x + 4 - k) % 4], s3.at[k], q3.at[k], along(k)).wait()
-    whole = (r3[0] + r3[1]) + (r3[2] + r3[3])
-    place = pl.ds(pl.multiple_of(my_half + yz * SEG, 8), SEG)
-    fin[place, :] = whole
-
-    def gather(k, who):
-        there = pl.ds(pl.multiple_of(my_half + who * SEG, 8), SEG)
-        return put(fin.at[there], fin.at[there], s4.at[k], q4.at[k], chip(k))
-
-    def start_gather(k, carry):
-        gather(k, yz).start()
-        return carry
-
-    lax.fori_loop(1, 16, start_gather, 0)
+    phase_on(0)
+    for phase in range(4):
+        send_rows(phase + 1)
+        phase_off(phase)
+        phase_on(phase + 1)
 
     rows = pl.ds(0, (DEVICES - 1) * CAP)
     put(back.at[rows], came.at[rows], row_send, row_recv, device_at(peer_of(1))).wait()
-
     for move in state_moves:
         move.wait()
     mask = jnp.full((1, ROWS), mask_ref[0], i32)
@@ -407,18 +462,13 @@
 
     lax.fori_loop(0, ROWS // 256, block, 0)
 
-    def wait_gather(k, carry):
-        gather(k, yz).wait_send()
-        gather(k, (yz + 16 - k) % 16).wait_recv()
-        return carry
-
-    lax.fori_loop(1, 16, wait_gather, 0)
+    phase_off(4)
     half = fin.at[pl.ds(my_half, HALF)]
     rest = fin.at[pl.ds(other, HALF)]
-    last = put(half, half, s5, q5, twin)
+    last = put(half, half, last_send, last_recv, twin)
     last.start()
     last.wait_send()
-    put(rest, rest, s5, q5, twin).wait_recv()
+    put(rest, rest, last_send, last_recv, twin).wait_recv()
     for q in range(8):
         top_ref[:, q * 128 : (q + 1) * 128] = fin[q * INTER : (q + 1) * INTER, :]
         out_ref[:, q * 128 : (q + 1) * 128] = fin[8 * INTER + q : 8 * INTER + q + 1, :]
@@ -513,16 +563,17 @@
     )(pair_mask, send_bags, send_slots, counts, upper, upper2, lower, lower2)
     slot_of = got_slots.reshape(DEVICES * 128)
 
-    pooled_grads, grads = pl.pallas_call(
+    vectors_t, d_pre, grads = pl.pallas_call(
         dense_kernel,
         out_shape=(
-            jax.ShapeDtypeStruct((BAGS + 8, E), f32),
+            jax.ShapeDtypeStruct((F + 1, E, B_DEV), f32),
+            jax.ShapeDtypeStruct((B_DEV, HID), f32),
             jax.ShapeDtypeStruct((G_ROWS, 128), f32),
         ),
         in_specs=[SMEM, VMEM, VMEM, VMEM, VMEM, VMEM],
-        out_specs=(VMEM, VMEM),
+        out_specs=(VMEM, VMEM, VMEM),
         scratch_shapes=[
-            pltpu.VMEM((F + 1, E, B_DEV), f32),
+            pltpu.VMEM((BAGS, E), f32),
             pltpu.VMEM((INTER, B_DEV), f32),
         ],
         compiler_params=params(vmem_limit_bytes=20 << 20),
@@ -537,7 +588,7 @@
             jax.ShapeDtypeStruct((INTER, HID), f32),
             jax.ShapeDtypeStruct((1, HID), f32),
         ),
-        in_specs=[SMEM, SMEM, SMEM, VMEM, VMEM, VMEM, VMEM, VMEM],
+        in_specs=[SMEM, SMEM, SMEM] + [VMEM] * 7,
         out_specs=(VMEM, VMEM, VMEM, VMEM),
         scratch_shapes=[
             pltpu.VMEM((DEVICES * CAP, E), f32),
@@ -545,30 +596,41 @@
             pltpu.VMEM((BAGS, E), f32),
             pltpu.VMEM((2 * E, BAGS), bf16),
             pltpu.VMEM((G_ROWS, 128), f32),
+            pltpu.VMEM((BAGS + 8, E), f32),
+            pltpu.VMEM((INTER, B_DEV), f32),
             pltpu.VMEM((HALF, 128), f32),
             pltpu.VMEM((HALF, 128), f32),
-            pltpu.VMEM((16, SEG, 128), f32),
-            pltpu.VMEM((SEG, 128), f32),
-            pltpu.VMEM((4, SEG, 128), f32),
             pltpu.VMEM((4, 1, ROWS), f32),
+            *[pltpu.VMEM((4, 4 * rows, 128), f32) for rows in PART],
+            *[pltpu.VMEM((4 * rows, 128), f32) for rows in PART],
+            *[pltpu.VMEM((4, rows, 128), f32) for rows in PART],
+            *[pltpu.VMEM((rows, 128), f32) for rows in PART],
+            *[pltpu.VMEM((4, rows, 128), f32) for rows in PART],
             dma((4,)),
             dma((4,)),
             dma,
             dma,
             dma,
             dma,
-            dma((16,)),
-            dma((16,)),
-            dma((4,)),
-            dma((4,)),
-            dma((16,)),
-            dma((16,)),
-            dma,
-            dma,
+            dma,
+            dma,
+            dma((40,)),
+            dma((40,)),
         ],
-        compiler_params=params(collective_id=1, has_side_effects=True, vmem_limit_bytes=24 << 20),
+        compiler_params=params(collective_id=1, has_side_effects=True, vmem_limit_bytes=26 << 20),
         name="update",
-    )(pair_mask, slot_of, where_to, pooled_grads, grads, counts, held, row_state[None, :])
+    )(
+        pair_mask,
+        slot_of,
+        where_to,
+        vectors_t,
+        d_pre,
+        top_weight,
+        grads,
+        counts,
+        held,
+        row_state[None, :],
+    )
     return new_table, new_state.reshape(ROWS), top_grad, out_grad.reshape(HID)
 
 

time: 149 us -> 145 us (0.973)
  Pallas kernels: 126 us -> 122 us
    pallas_call x1, Pallas kernels: 59.3 us -> 57.1 us  [on_device(): pl.pallas_call(update_kernel, out_shape=(jax.ShapeDtypeStruct((ROWS, E),...]
where the time goes in v5:
time: 145 us
  Pallas kernels  122 us (84%)
  waiting for transfers between devices  5.8 us (4%)
  local copies, waits for them, and re-layouts  5.33 us (4%)
  starting transfers between devices  4.97 us (3%)
  other arithmetic  3.92 us (3%)
  between operations  1.57 us (1%)
    pallas_call x1, Pallas kernels, on_device(): pl.pallas_call(update_kernel, out_shape=(jax.ShapeDtypeStruct((ROWS, E),...  57.1 us
    pallas_call x1, Pallas kernels, on_device(): pl.pallas_call(pool_kernel, out_shape=(jax.ShapeDtypeStruct((DEVICES * CA...  42.1 us
    pallas_call x1, Pallas kernels, on_device(): pl.pallas_call(count_kernel, out_shape=jax.ShapeDtypeStruct((C_ROWS, ROWS...  15.9 us
    pallas_call x1, Pallas kernels, on_device(): pl.pallas_call(dense_kernel, out_shape=(jax.ShapeDtypeStruct((F + 1, E, B...  7.33 us
    ppermute x4, waiting for transfers between devices, from_partner(): return lax.ppermute(block, 'gy', [(y, y ^ flip) for y in range(4)])  5.8 us
    ppermute x4, starting transfers between devices, from_partner(): return lax.ppermute(block, 'gy', [(y, y ^ flip) for y in range(4)])  4.97 us
    unnamed x24, local copies, waits for them, and re-layouts  3.2 us
  transfers between devices with their start and end apart: 4, of which 2 were waited for; matrix products, arithmetic and copies ran while one was open for 4% of the time, Pallas kernels for 11%

profile of v5, /device:TPU:1, one launch (start us, length us, event | category | flops | bytes accessed | tf_op | source)
XLA Modules:
  0.0 145.3 jit_solution(2377993181861797108)
XLA Ops:
  0.7 1.3 fusion.31
  2.0 3.4 %collective-permute-start.1 = (f32[1024,128]{1,0:T(8,128)S(1)}, f32[1024,128]{1,0:T(8,128)S(1)}, u32[]{:S(2)}, u32[]{:S(2)}) collective-permute-start(f32[1024,128]{1,0:T(8,128)S(1)} %get-tuple-element.40), channel_id=1, source_target_pairs={{0,3},{1,2},{2,1},{3,0},{4,7},{5,6},{6,5},{7,4},{8,11},{9,10},{10,... | collective-permute-start | bytes 1572872 | tf_op jit(solution)/shard_map/ppermute | solution.py:482
  6.0 0.3 reduce-window.19
  6.3 0.1 slice.47
  6.4 0.1 slice_reduce_fusion
  6.6 0.1 copy.25.label_ref
  6.7 0.1 copy.22
  6.8 0.3 fusion.2
  7.2 0.1 broadcast_add_fusion
  7.3 0.3 copy.23
  7.6 0.6 fusion.1
  8.3 2.0 %select_convert_fusion.3 = (bf16[2048,32]{1,0:T(8,128)(2,1)S(1)}, bf16[2048,32]{1,0:T(8,128)(2,1)S(1)}, bf16[2048,32]{1,0:T(8,128)(2,1)S(1)}, bf16[2048,32]{1,0:T(8,128)(2,1)S(1)}) fusion(bf16[2048]{0:T(1024)(128)(2,1)S(1)} %get-tuple-element.48, s32[2048]{0:T(1024)S(1)} %fusion.1, bf16[2048]{0:T(1024)(128)(2,1)S(1)} %fusion.24, ...), kind=kLoop, calls=%fused_computation.8 | loop fusion | flops 327680 | bytes 548864 | tf_op jit(solution)/shard_map/convert
  10.3 0.0 copy-start.5
  10.3 1.3 convolution_convert_fusion
  11.6 0.1 fusion.13
  11.7 0.1 reshape.114.bag_ref
  11.8 0.1 fusion.30
  11.8 0.2 convert_reduce_fusion
  12.1 4.5 %collective-permute-done.1 = f32[1024,128]{1,0:T(8,128)S(1)} collective-permute-done((f32[1024,128]{1,0:T(8,128)S(1)}, f32[1024,128]{1,0:T(8,128)S(1)}, u32[]{:S(2)}, u32[]{:S(2)}) %collective-permute-start.1) | collective-permute-done | bytes 524320 | tf_op jit(solution)/shard_map/ppermute | solution.py:482
  16.6 1.3 collective-permute-done
  17.9 0.1 broadcast_select_fusion
  18.0 1.6 %collective-permute-start.2 = (f32[1024,128]{1,0:T(8,128)S(1)}, f32[1024,128]{1,0:T(8,128)S(1)}, u32[]{:S(2)}, u32[]{:S(2)}) collective-permute-start(f32[1024,128]{1,0:T(8,128)S(1)} %get-tuple-element.24.a_ref), channel_id=1, source_target_pairs={{0,3},{1,2},{2,1},{3,0},{4,7},{5,6},{6,5},{7,4},{8,11},{9,10},{10,... | collective-permute-start | bytes 1572872 | tf_op jit(solution)/shard_map/ppermute | solution.py:482
  19.6 15.9 %count.1.c_ref = bf16[2304,2048]{1,0:T(8,128)(2,1)S(1)} custom-call(s32[24]{0:T(128)S(1)} %fusion.28.first_ref, s32[48,128]{1,0:T(8,128)S(1)} %bitcast.34, s32[18,128]{1,0:T(8,128)S(1)} %get-tuple-element.22.start_ref, s32[18,128]{1,0:T(8,128)S(1)} %get-tuple-element.23.end_ref), custom_call_target="tpu_custom_call" | custom-call | flops 6845104128 | bytes 10485760 | tf_op jit(solution)/shard_map/count/pallas_call | solution.py:531
  35.6 0.0 copy-start
  35.6 42.1 %pool.1 = (f32[4096,128]{1,0:T(8,128)S(1)}, s32[128,1,128]{2,1,0:T(1,128)S(1)}, f32[2048,128]{1,0:T(8,128)S(1)}) custom-call(s32[1]{0:T(128)S(6)} %copy.31.mask_ref, s32[4096]{0:T(1024)S(1)} %reshape.114.bag_ref, s32[128,1,128]{2,1,0:T(1,128)S(1)} %bitcast.29, bf16[2304,2048]{1,0:T(8,128)(2,1)S(1)} %count.1.c_ref, f32[1024,128]{1,0:T(8,128)S(1)} %get-tuple-element.24.a_ref, ...), custom_call_target="tpu_custom_call" | custom-call | tf_op jit(solution)/shard_map/pool/pallas_call | solution.py:543
  77.7 0.0 copy-start.2
  77.7 7.3 %dense.1 = (f32[17,128,128]{2,1,0:T(8,128)S(1)}, f32[128,1024]{1,0:T(8,128)S(1)}, f32[2304,128]{1,0:T(8,128)S(1)}) custom-call(s32[16384]{0:T(1024)S(1)} %bitcast.27, f32[4096,128]{1,0:T(8,128)S(1)} %get-tuple-element.27.got_ref, f32[128,128]{1,0:T(8,128)S(1)} %copy-done.1, f32[128,1]{1,0:T(8,128)S(1)} %copy.25.label_ref, f32[264,1024]{1,0:T(8,128)S(1)} %copy-done, ...), custom_call_target="tpu_custom_call" | custom-call | tf_op jit(solution)/shard_map/dense/pallas_call | solution.py:566
  85.1 57.1 %update.1 = (f32[2048,128]{1,0:T(8,128)S(1)}, f32[1,2048]{1,0:T(1,128)S(1)}, f32[264,1024]{1,0:T(8,128)S(1)}, f32[1,1024]{1,0:T(1,128)S(1)}) custom-call(s32[1]{0:T(128)S(6)} %copy.31.mask_ref, s32[16384]{0:T(1024)S(1)} %bitcast.28, s32[2048]{0:T(1024)S(1)} %multiply_add_fusion.where_ref, f32[17,128,128]{2,1,0:T(8,128)S(1)} %get-tuple-element.28.vt, ...), custom_call_target="tpu_custom_call" | custom-call | tf_op jit(solution)/shard_map/update/pallas_call | solution.py:583
  142.1 1.0 copy.32
  143.1 0.6 copy.33
  143.7 1.0 copy.34
  144.7 0.6 copy.35
  (32 shorter events, 0.2 us)
Async XLA Ops:
  0.6 5.4 %copy-start.7 = (s32[1,2048]{1,0:T(1,128)S(1)}, s32[1,2048]{1,0:T(1,128)}, u32[]{:S(2)}) copy-start(s32[1,2048]{1,0:T(1,128)} %param.15) | copy-start | bytes 24580
  0.6 5.9 %copy-start.8 = (s32[2048]{0:T(1024)S(1)}, s32[2048]{0:T(1024)}, u32[]{:S(2)}) copy-start(s32[2048]{0:T(1024)} %param.17) | copy-start | bytes 24580
  0.7 5.9 %copy-start.9 = (f32[128]{0:T(128)S(1)}, f32[128]{0:T(128)}, u32[]{:S(2)}) copy-start(f32[128]{0:T(128)} %param.19) | copy-start | bytes 1540
  0.7 6.0 %copy-start.6 = (s32[2048,1]{0,1:T(1,128)S(1)}, s32[2048,1]{0,1:T(1,128)}, u32[]{:S(2)}) copy-start(s32[2048,1]{0,1:T(1,128)} %param.16) | copy-start | bytes 24580
  2.0 14.6 %collective-permute-start.1 = (f32[1024,128]{1,0:T(8,128)S(1)}, f32[1024,128]{1,0:T(8,128)S(1)}, u32[]{:S(2)}, u32[]{:S(2)}) collective-permute-start(f32[1024,128]{1,0:T(8,128)S(1)} %get-tuple-element.40), channel_id=1, source_target_pairs={{0,3},{1,2},{2,1},{3,0},{4,7},{5,6},{6,5},{7,4},{8,11},{9,10},{10,... | collective-permute-start | bytes 1572872 | tf_op jit(solution)/shard_map/ppermute | solution.py:482
  5.3 12.5 %collective-permute-start = (f32[1024,128]{1,0:T(8,128)S(1)}, f32[1024,128]{1,0:T(8,128)S(1)}, u32[]{:S(2)}, u32[]{:S(2)}) collective-permute-start(f32[1024,128]{1,0:T(8,128)S(1)} %get-tuple-element.41), channel_id=1, source_target_pairs={{0,1},{1,0},{2,3},{3,2},{4,5},{5,4},{6,7},{7,6},{8,9},{9,8},{10,11... | collective-permute-start | bytes 1572872 | tf_op jit(solution)/shard_map/ppermute | solution.py:482
  10.3 7.6 %copy-start.5 = (f32[2048,128]{1,0:T(8,128)S(1)}, f32[2048,128]{1,0:T(8,128)}, u32[]{:S(2)}) copy-start(f32[2048,128]{1,0:T(8,128)} %param.11) | copy-start | bytes 3145732
  17.9 1.7 %copy-start.4 = (s32[6144]{0:T(1024)S(1)}, s32[6144]{0:T(1024)}, u32[]{:S(2)}) copy-start(s32[6144]{0:T(1024)} %param.14) | copy-start | bytes 73732
  18.0 17.6 %collective-permute-start.2 = (f32[1024,128]{1,0:T(8,128)S(1)}, f32[1024,128]{1,0:T(8,128)S(1)}, u32[]{:S(2)}, u32[]{:S(2)}) collective-permute-start(f32[1024,128]{1,0:T(8,128)S(1)} %get-tuple-element.24.a_ref), channel_id=1, source_target_pairs={{0,3},{1,2},{2,1},{3,0},{4,7},{5,6},{6,5},{7,4},{8,11},{9,10},{10,... | collective-permute-start | bytes 1572872 | tf_op jit(solution)/shard_map/ppermute | solution.py:482
  19.6 16.0 %collective-permute-start.3 = (f32[1024,128]{1,0:T(8,128)S(1)}, f32[1024,128]{1,0:T(8,128)S(1)}, u32[]{:S(2)}, u32[]{:S(2)}) collective-permute-start(f32[1024,128]{1,0:T(8,128)S(1)} %get-tuple-element.25.b_ref), channel_id=1, source_target_pairs={{0,1},{1,0},{2,3},{3,2},{4,5},{5,4},{6,7},{7,6},{8,9},{9,8},{10,11... | collective-permute-start | bytes 1572872 | tf_op jit(solution)/shard_map/ppermute | solution.py:482
  35.6 42.1 %copy-start = (f32[264,1024]{1,0:T(8,128)S(1)}, f32[264,1024]{1,0:T(8,128)}, u32[]{:S(2)}) copy-start(f32[264,1024]{1,0:T(8,128)} %w_ref.3) | copy-start | bytes 3244036
  35.6 42.1 %copy-start.1 = (f32[128,128]{1,0:T(8,128)S(1)}, f32[128,128]{1,0:T(8,128)}, u32[]{:S(2)}) copy-start(f32[128,128]{1,0:T(8,128)} %dense_ref.1) | copy-start | bytes 196612
  35.6 42.1 %copy-start.3 = (f32[1024]{0:T(1024)S(1)}, f32[1024]{0:T(1024)}, u32[]{:S(2)}) copy-start(f32[1024]{0:T(1024)} %param.21) | copy-start | bytes 12292
  77.7 7.3 %copy-start.2 = (f32[2048]{0:T(1024)S(1)}, f32[2048]{0:T(1024)}, u32[]{:S(2)}) copy-start(f32[2048]{0:T(1024)} %param.12) | copy-start | bytes 24580

commit v6 on v5

--- a/solution.py
+++ b/solution.py
@@ -22,7 +22,7 @@
 HALF = G_ROWS // 2
 PART = (40, 32)
 STRIDE = 37
-CUTS = (1, 36, 60, 84, 108, 128)
+CUTS = (1, 32, 58, 82, 106, 128)
 PAIRS = [(i, j) for i in range(F + 1) for j in range(i + 1, F + 1)]
 PAIR_ROW = {pair: 128 + n for n, pair in enumerate(PAIRS)}
 
@@ -86,7 +86,7 @@
             c_ref[pl.ds(pl.multiple_of(at + 16, 16), SPAN - 16), cols] = counts[16:].astype(bf16)
         return carry
 
-    lax.fori_loop(0, LOOKS // CHUNK, chunk, 0)
+    lax.fori_loop(0, LOOKS // CHUNK, chunk, 0, unroll=2)
 
 
 def device_at(n):
@@ -191,10 +191,7 @@
     put(send_ref.at[rows], recv_ref.at[rows], row_send, row_recv, to).wait()
 
 
-def dense_kernel(
-    slot_ref, got_ref, dense_ref, label_ref, w_ref, wo_ref, vt, d_pre_ref, grad_ref, pooled, inter_t
-):
-
+def place_kernel(slot_ref, got_ref, pooled):
     def place(c, carry):
         @pl.when(slot_ref[c * 128] < BAGS)
         def _():
@@ -205,41 +202,16 @@
 
     lax.fori_loop(0, DEVICES, place, 0)
 
-    dense_t = dense_ref[...].T
-    vt[0] = dense_t
-    inter_t[0:128, :] = dense_t
-    for f in range(F):
-        vt[f + 1] = pooled[f * 128 : (f + 1) * 128, :].T
-    for i in range(F):
-        for j in range(i + 1, F + 1):
-            row = PAIR_ROW[i, j]
-            inter_t[row : row + 1, :] = jnp.sum(vt[i] * vt[j], axis=0, keepdims=True)
-
-    it = inter_t[...]
-    w = split(w_ref[...])
-    pre = dot3(split(it.T), w, NN)
-    sig = 1.0 / (1.0 + jnp.exp(-pre))
-    hidden = pre * sig
-    logits = jnp.sum(hidden * wo_ref[...], axis=1, keepdims=True)
-    d_logits = 1.0 / (1.0 + jnp.exp(-logits)) - label_ref[...]
-    out_grad = jnp.sum(hidden * d_logits, axis=0, keepdims=True)
-    for q in range(8):
-        grad_ref[8 * INTER + q : 8 * INTER + q + 1, :] = out_grad[:, q * 128 : (q + 1) * 128]
-    grad_ref[8 * INTER + 8 :, :] = jnp.zeros((G_ROWS - 8 * INTER - 8, 128), f32)
-    d_pre_ref[...] = d_logits * wo_ref[...] * (sig * (1.0 + pre * (1.0 - sig)))
-    top_grad = dot3(split(it), split(d_pre_ref[...]), NN)
-    for q in range(8):
-        grad_ref[q * INTER : (q + 1) * INTER, :] = top_grad[:, q * 128 : (q + 1) * 128]
-
 
 def update_kernel(
     mask_ref,
     slot_ref,
     where_ref,
-    vt,
-    d_pre_ref,
+    sums_ref,
+    dense_ref,
+    label_ref,
     w_ref,
-    g_ref,
+    wo_ref,
     c_ref,
     table_ref,
     state_ref,
@@ -253,7 +225,10 @@
     sides,
     fin,
     pooled,
-    d_inter,
+    inter_t,
+    vt,
+    d_pre_ref,
+    grad_ref,
     r1,
     acc,
     states,
@@ -296,17 +271,61 @@
     def along_z(k):
         return ((y * 4 + (z + k) % 4) * 2 + core, x)
 
-    d_inter[...] = dot3(split(w_ref[...]), split(d_pre_ref[...]), NT)
-    for j in range(1, F + 1):
+    dense_t = dense_ref[...].T
+    vt[0] = dense_t
+    inter_t[0:128, :] = dense_t
+    for f in range(F):
+        vt[f + 1] = sums_ref[f * 128 : (f + 1) * 128, :].T
+    for i in range(F):
+        for j in range(i + 1, F + 1):
+            row = PAIR_ROW[i, j]
+            inter_t[row : row + 1, :] = jnp.sum(vt[i] * vt[j], axis=0, keepdims=True)
+
+    it = inter_t[...]
+    w = split(w_ref[...])
+    pre = dot3(split(it.T), w, NN)
+    sig = 1.0 / (1.0 + jnp.exp(-pre))
+    hidden = pre * sig
+    logits = jnp.sum(hidden * wo_ref[...], axis=1, keepdims=True)
+    d_logits = 1.0 / (1.0 + jnp.exp(-logits)) - label_ref[...]
+    out_grad = jnp.sum(hidden * d_logits, axis=0, keepdims=True)
+    for q in range(8):
+        grad_ref[8 * INTER + q : 8 * INTER + q + 1, :] = out_grad[:, q * 128 : (q + 1) * 128]
+    grad_ref[8 * INTER + 8 :, :] = jnp.zeros((G_ROWS - 8 * INTER - 8, 128), f32)
+    d_pre_ref[...] = d_logits * wo_ref[...] * (sig * (1.0 + pre * (1.0 - sig)))
+    d_pre = split(d_pre_ref[...])
+    top_grad = dot3(split(it), d_pre, NN)
+    for q in range(8):
+        grad_ref[q * INTER : (q + 1) * INTER, :] = top_grad[:, q * 128 : (q + 1) * 128]
+    inter_t[...] = dot3(w, d_pre, NT)
+
+    def pooled_grad(j):
         total = None
         for i in range(F + 1):
             if i != j:
                 row = PAIR_ROW[min(i, j), max(i, j)]
-                term = d_inter[row : row + 1, :] * vt[i]
+                term = inter_t[row : row + 1, :] * vt[i]
                 total = term if total is None else total + term
         pooled[(j - 1) * 128 : j * 128, :] = total.T
+
+    for j in range(1, 7):
+        pooled_grad(j)
+
+    my_half = pl.multiple_of(core * HALF, 8)
+    other = pl.multiple_of((1 - core) * HALF, 8)
+    pl.semaphore_wait(barrier, DEVICES - 1)
+    swap = put(grad_ref.at[pl.ds(other, HALF)], r1, swap_send, swap_recv, twin)
+    swap.start()
+    flips = [None, x + 1 - 2 * (x % 2), (x + 2) % 4, 3 - x]
+    state_moves = [
+        put(state_ref, states.at[f], state_send.at[f], state_recv.at[f], (gx, flips[f]))
+        for f in range(1, 4)
+    ]
+    for move in state_moves:
+        move.start()
+    for j in range(7, F + 1):
+        pooled_grad(j)
     pooled[BAGS:, :] = jnp.zeros((8, E), f32)
-    pick_rows(came, me * CAP, pooled, slot_ref, me * 128)
 
     def ready(k):
         peer = peer_of(k)
@@ -328,10 +347,6 @@
         lax.fori_loop(CUTS[n], last, step, 0)
         if last < CUTS[n + 1]:
             start(last)
-
-    ready(1)
-    my_half = pl.multiple_of(core * HALF, 8)
-    other = pl.multiple_of((1 - core) * HALF, 8)
 
     class Color:
         def __init__(self, n, base, at, to_a, to_b, ra, acc2, rb, mine, rx):
@@ -408,24 +423,16 @@
         for color in colors:
             color.finish(phase)
 
-    pl.semaphore_wait(barrier, DEVICES - 1)
-    swap = put(g_ref.at[pl.ds(other, HALF)], r1, swap_send, swap_recv, twin)
-    swap.start()
-    flips = [None, x + 1 - 2 * (x % 2), (x + 2) % 4, 3 - x]
-    state_moves = [
-        put(state_ref, states.at[f], state_send.at[f], state_recv.at[f], (gx, flips[f]))
-        for f in range(1, 4)
-    ]
-    for move in state_moves:
-        move.start()
-    send_rows(0)
     swap.wait()
-    acc[...] = g_ref[pl.ds(my_half, HALF), :] + r1[...]
+    acc[...] = grad_ref[pl.ds(my_half, HALF), :] + r1[...]
     phase_on(0)
+    pick_rows(came, me * CAP, pooled, slot_ref, me * 128)
+    ready(1)
     for phase in range(4):
-        send_rows(phase + 1)
+        send_rows(phase)
         phase_off(phase)
         phase_on(phase + 1)
+    send_rows(4)
 
     rows = pl.ds(0, (DEVICES - 1) * CAP)
     put(back.at[rows], came.at[rows], row_send, row_recv, device_at(peer_of(1))).wait()
@@ -450,6 +457,12 @@
         sides[0:128, here] = hi
         sides[128:256, here] = lo
 
+    phase_off(4)
+    half = fin.at[pl.ds(my_half, HALF)]
+    rest = fin.at[pl.ds(other, HALF)]
+    last = put(half, half, last_send, last_recv, twin)
+    last.start()
+
     def block(n, carry):
         here = pl.ds(pl.multiple_of(n * 256, 256), 256)
         both = mxu(sides[...], c_ref[0:BAGS, here], NN)
@@ -462,11 +475,6 @@
 
     lax.fori_loop(0, ROWS // 256, block, 0)
 
-    phase_off(4)
-    half = fin.at[pl.ds(my_half, HALF)]
-    rest = fin.at[pl.ds(other, HALF)]
-    last = put(half, half, last_send, last_recv, twin)
-    last.start()
     last.wait_send()
     put(rest, rest, last_send, last_recv, twin).wait_recv()
     for q in range(8):
@@ -563,22 +571,14 @@
     )(pair_mask, send_bags, send_slots, counts, upper, upper2, lower, lower2)
     slot_of = got_slots.reshape(DEVICES * 128)
 
-    vectors_t, d_pre, grads = pl.pallas_call(
-        dense_kernel,
-        out_shape=(
-            jax.ShapeDtypeStruct((F + 1, E, B_DEV), f32),
-            jax.ShapeDtypeStruct((B_DEV, HID), f32),
-            jax.ShapeDtypeStruct((G_ROWS, 128), f32),
-        ),
-        in_specs=[SMEM, VMEM, VMEM, VMEM, VMEM, VMEM],
-        out_specs=(VMEM, VMEM, VMEM),
-        scratch_shapes=[
-            pltpu.VMEM((BAGS, E), f32),
-            pltpu.VMEM((INTER, B_DEV), f32),
-        ],
-        compiler_params=params(vmem_limit_bytes=20 << 20),
-        name="dense",
-    )(slot_of, got_rows, dense_vectors, labels[:, None], top_weight, out_weight[None, :])
+    sums = pl.pallas_call(
+        place_kernel,
+        out_shape=jax.ShapeDtypeStruct((BAGS, E), f32),
+        in_specs=[SMEM, VMEM],
+        out_specs=VMEM,
+        compiler_params=params(vmem_limit_bytes=16 << 20),
+        name="place",
+    )(slot_of, got_rows)
 
     new_table, new_state, top_grad, out_grad = pl.pallas_call(
         update_kernel,
@@ -588,7 +588,7 @@
             jax.ShapeDtypeStruct((INTER, HID), f32),
             jax.ShapeDtypeStruct((1, HID), f32),
         ),
-        in_specs=[SMEM, SMEM, SMEM] + [VMEM] * 7,
+        in_specs=[SMEM, SMEM, SMEM] + [VMEM] * 8,
         out_specs=(VMEM, VMEM, VMEM, VMEM),
         scratch_shapes=[
             pltpu.VMEM((DEVICES * CAP, E), f32),
@@ -598,6 +598,9 @@
             pltpu.VMEM((G_ROWS, 128), f32),
             pltpu.VMEM((BAGS + 8, E), f32),
             pltpu.VMEM((INTER, B_DEV), f32),
+            pltpu.VMEM((F + 1, E, B_DEV), f32),
+            pltpu.VMEM((B_DEV, HID), f32),
+            pltpu.VMEM((G_ROWS, 128), f32),
             pltpu.VMEM((HALF, 128), f32),
             pltpu.VMEM((HALF, 128), f32),
             pltpu.VMEM((4, 1, ROWS), f32),
@@ -617,16 +620,17 @@
             dma((40,)),
             dma((40,)),
         ],
-        compiler_params=params(collective_id=1, has_side_effects=True, vmem_limit_bytes=26 << 20),
+        compiler_params=params(collective_id=1, has_side_effects=True, vmem_limit_bytes=30 << 20),
         name="update",
     )(
         pair_mask,
         slot_of,
         where_to,
-        vectors_t,
-        d_pre,
+        sums,
+        dense_vectors,
+        labels[:, None],
         top_weight,
-        grads,
+        out_weight[None, :],
         counts,
         held,
         row_state[None, :],

time: 145 us -> 143 us (0.986)
  Pallas kernels: 122 us -> 120 us
    pallas_call x1, Pallas kernels: 15.9 us -> 13.3 us  [on_device(): pl.pallas_call(count_kernel, out_shape=jax.ShapeDtypeStruct((C_ROWS, ROWS...]
    pallas_call x1, Pallas kernels: 7.33 us -> 4.98 us  [on_device(): pl.pallas_call(place_kernel, out_shape=jax.ShapeDtypeStruct((BAGS, E), f3...]
    pallas_call x1, Pallas kernels: 57.1 us -> 59.2 us  [on_device(): pl.pallas_call(update_kernel, out_shape=(jax.ShapeDtypeStruct((ROWS, E),...]
  transfers between devices with their start and end apart: 4 -> 4, of which waited for: 2 -> 2; matrix products, arithmetic and copies ran while one was open for 4% -> 4% of each run, Pallas kernels for 11% -> 9%
where the time goes in v6:
time: 143 us
  Pallas kernels  120 us (84%)
  starting transfers between devices  5.82 us (4%)
  local copies, waits for them, and re-layouts  5.66 us (4%)
  waiting for transfers between devices  4.84 us (3%)
  other arithmetic  3.92 us (3%)
  between operations  1.56 us (1%)
    pallas_call x1, Pallas kernels, on_device(): pl.pallas_call(update_kernel, out_shape=(jax.ShapeDtypeStruct((ROWS, E),...  59.2 us
    pallas_call x1, Pallas kernels, on_device(): pl.pallas_call(pool_kernel, out_shape=(jax.ShapeDtypeStruct((DEVICES * CA...  42 us
    pallas_call x1, Pallas kernels, on_device(): pl.pallas_call(count_kernel, out_shape=jax.ShapeDtypeStruct((C_ROWS, ROWS...  13.3 us
    ppermute x4, starting transfers between devices, from_partner(): return lax.ppermute(block, 'gy', [(y, y ^ flip) for y in range(4)])  5.82 us
    pallas_call x1, Pallas kernels, on_device(): pl.pallas_call(place_kernel, out_shape=jax.ShapeDtypeStruct((BAGS, E), f3...  4.98 us
    ppermute x4, waiting for transfers between devices, from_partner(): return lax.ppermute(block, 'gy', [(y, y ^ flip) for y in range(4)])  4.84 us
    unnamed x24, local copies, waits for them, and re-layouts  3.54 us
  transfers between devices with their start and end apart: 4, of which 2 were waited for; matrix products, arithmetic and copies ran while one was open for 4% of the time, Pallas kernels for 9%

profile of v6, /device:TPU:1, one launch (start us, length us, event | category | flops | bytes accessed | tf_op | source)
XLA Modules:
  0.0 142.6 jit_solution(3172761102640889975)
XLA Ops:
  0.7 1.3 fusion.31
  1.9 2.1 %collective-permute-start = (f32[1024,128]{1,0:T(8,128)S(1)}, f32[1024,128]{1,0:T(8,128)S(1)}, u32[]{:S(2)}, u32[]{:S(2)}) collective-permute-start(f32[1024,128]{1,0:T(8,128)S(1)} %get-tuple-element.35), channel_id=1, source_target_pairs={{0,1},{1,0},{2,3},{3,2},{4,5},{5,4},{6,7},{7,6},{8,9},{9,8},{10,11... | collective-permute-start | bytes 1572872 | tf_op jit(solution)/shard_map/ppermute | solution.py:490
  4.0 1.8 %collective-permute-start.1 = (f32[1024,128]{1,0:T(8,128)S(1)}, f32[1024,128]{1,0:T(8,128)S(1)}, u32[]{:S(2)}, u32[]{:S(2)}) collective-permute-start(f32[1024,128]{1,0:T(8,128)S(1)} %get-tuple-element.34), channel_id=1, source_target_pairs={{0,3},{1,2},{2,1},{3,0},{4,7},{5,6},{6,5},{7,4},{8,11},{9,10},{10,... | collective-permute-start | bytes 1572872 | tf_op jit(solution)/shard_map/ppermute | solution.py:490
  6.6 0.3 reduce-window.19
  6.8 0.1 slice.47
  7.0 0.1 slice_reduce_fusion
  7.1 0.1 copy.22
  7.2 0.3 fusion.2
  7.6 0.1 broadcast_add_fusion
  7.6 0.0 copy-start.8
  7.7 0.3 copy.23
  8.0 0.3 copy-done.8
  8.4 0.6 fusion.1
  9.0 2.0 %select_convert_fusion.3 = (bf16[2048,32]{1,0:T(8,128)(2,1)S(1)}, bf16[2048,32]{1,0:T(8,128)(2,1)S(1)}, bf16[2048,32]{1,0:T(8,128)(2,1)S(1)}, bf16[2048,32]{1,0:T(8,128)(2,1)S(1)}) fusion(bf16[2048]{0:T(1024)(128)(2,1)S(1)} %get-tuple-element.42, s32[2048]{0:T(1024)S(1)} %fusion.1, bf16[2048]{0:T(1024)(128)(2,1)S(1)} %fusion.24, ...), kind=kLoop, calls=%fused_computation.8 | loop fusion | flops 327680 | bytes 548864 | tf_op jit(solution)/shard_map/convert
  11.0 1.3 convolution_convert_fusion
  12.3 0.1 fusion.13
  12.4 0.1 reshape.114.bag_ref
  12.5 0.1 copy.25.label_ref
  12.6 0.1 fusion.30
  12.7 0.2 convert_reduce_fusion
  12.9 2.3 %collective-permute-done = f32[1024,128]{1,0:T(8,128)S(1)} collective-permute-done((f32[1024,128]{1,0:T(8,128)S(1)}, f32[1024,128]{1,0:T(8,128)S(1)}, u32[]{:S(2)}, u32[]{:S(2)}) %collective-permute-start) | collective-permute-done | bytes 524320 | tf_op jit(solution)/shard_map/ppermute | solution.py:490
  15.3 2.5 %collective-permute-done.1 = f32[1024,128]{1,0:T(8,128)S(1)} collective-permute-done((f32[1024,128]{1,0:T(8,128)S(1)}, f32[1024,128]{1,0:T(8,128)S(1)}, u32[]{:S(2)}, u32[]{:S(2)}) %collective-permute-start.1) | collective-permute-done | bytes 524320 | tf_op jit(solution)/shard_map/ppermute | solution.py:490
  17.8 0.1 broadcast_select_fusion
  17.9 1.9 %collective-permute-start.2 = (f32[1024,128]{1,0:T(8,128)S(1)}, f32[1024,128]{1,0:T(8,128)S(1)}, u32[]{:S(2)}, u32[]{:S(2)}) collective-permute-start(f32[1024,128]{1,0:T(8,128)S(1)} %get-tuple-element.21.a_ref), channel_id=1, source_target_pairs={{0,3},{1,2},{2,1},{3,0},{4,7},{5,6},{6,5},{7,4},{8,11},{9,10},{10,... | collective-permute-start | bytes 1572872 | tf_op jit(solution)/shard_map/ppermute | solution.py:490
  19.8 13.3 %count.1.c_ref = bf16[2304,2048]{1,0:T(8,128)(2,1)S(1)} custom-call(s32[24]{0:T(128)S(1)} %fusion.28.first_ref, s32[48,128]{1,0:T(8,128)S(1)} %bitcast.34, s32[18,128]{1,0:T(8,128)S(1)} %get-tuple-element.19.start_ref, s32[18,128]{1,0:T(8,128)S(1)} %get-tuple-element.20.end_ref), custom_call_target="tpu_custom_call" | custom-call | flops 6845104128 | bytes 10485760 | tf_op jit(solution)/shard_map/count/pallas_call | solution.py:539
  33.2 42.0 %pool.1 = (f32[4096,128]{1,0:T(8,128)S(1)}, s32[128,1,128]{2,1,0:T(1,128)S(1)}, f32[2048,128]{1,0:T(8,128)S(1)}) custom-call(s32[1]{0:T(128)S(6)} %copy.31.mask_ref, s32[4096]{0:T(1024)S(1)} %reshape.114.bag_ref, s32[128,1,128]{2,1,0:T(1,128)S(1)} %bitcast.29, bf16[2304,2048]{1,0:T(8,128)(2,1)S(1)} %count.1.c_ref, f32[1024,128]{1,0:T(8,128)S(1)} %get-tuple-element.21.a_ref, ...), custom_call_target="tpu_custom_call" | custom-call | tf_op jit(solution)/shard_map/pool/pallas_call | solution.py:551
  75.3 5.0 %place.1.sums_ref = f32[2048,128]{1,0:T(8,128)S(1)} custom-call(s32[16384]{0:T(1024)S(1)} %bitcast.27, f32[4096,128]{1,0:T(8,128)S(1)} %get-tuple-element.24.got_ref), custom_call_target="tpu_custom_call" | custom-call | tf_op jit(solution)/shard_map/place/pallas_call | solution.py:574
  80.3 59.2 %update.1 = (f32[2048,128]{1,0:T(8,128)S(1)}, f32[1,2048]{1,0:T(1,128)S(1)}, f32[264,1024]{1,0:T(8,128)S(1)}, f32[1,1024]{1,0:T(1,128)S(1)}) custom-call(s32[1]{0:T(128)S(6)} %copy.31.mask_ref, s32[16384]{0:T(1024)S(1)} %bitcast.28, s32[2048]{0:T(1024)S(1)} %multiply_add_fusion.where_ref, f32[2048,128]{1,0:T(8,128)S(1)} %place.1.sums_ref, ...), custom_call_target="tpu_custom_call" | custom-call | tf_op jit(solution)/shard_map/update/pallas_call | solution.py:583
  139.5 1.0 copy.32
  140.4 0.6 copy.33
  141.0 1.0 copy.34
  142.0 0.6 copy.35
  (32 shorter events, 0.2 us)
Async XLA Ops:
  0.6 5.9 %copy-start.7 = (s32[1,2048]{1,0:T(1,128)S(1)}, s32[1,2048]{1,0:T(1,128)}, u32[]{:S(2)}) copy-start(s32[1,2048]{1,0:T(1,128)} %param.15) | copy-start | bytes 24580
  0.6 6.4 %copy-start.6 = (s32[2048,1]{0,1:T(1,128)S(1)}, s32[2048,1]{0,1:T(1,128)}, u32[]{:S(2)}) copy-start(s32[2048,1]{0,1:T(1,128)} %param.16) | copy-start | bytes 24580
  1.9 13.3 %collective-permute-start = (f32[1024,128]{1,0:T(8,128)S(1)}, f32[1024,128]{1,0:T(8,128)S(1)}, u32[]{:S(2)}, u32[]{:S(2)}) collective-permute-start(f32[1024,128]{1,0:T(8,128)S(1)} %get-tuple-element.35), channel_id=1, source_target_pairs={{0,1},{1,0},{2,3},{3,2},{4,5},{5,4},{6,7},{7,6},{8,9},{9,8},{10,11... | collective-permute-start | bytes 1572872 | tf_op jit(solution)/shard_map/ppermute | solution.py:490
  4.0 13.7 %collective-permute-start.1 = (f32[1024,128]{1,0:T(8,128)S(1)}, f32[1024,128]{1,0:T(8,128)S(1)}, u32[]{:S(2)}, u32[]{:S(2)}) collective-permute-start(f32[1024,128]{1,0:T(8,128)S(1)} %get-tuple-element.34), channel_id=1, source_target_pairs={{0,3},{1,2},{2,1},{3,0},{4,7},{5,6},{6,5},{7,4},{8,11},{9,10},{10,... | collective-permute-start | bytes 1572872 | tf_op jit(solution)/shard_map/ppermute | solution.py:490
  7.6 0.7 copy-start.8
  11.0 1.5 %copy-start.9 = (f32[128]{0:T(128)S(1)}, f32[128]{0:T(128)}, u32[]{:S(2)}) copy-start(f32[128]{0:T(128)} %param.19) | copy-start | bytes 1540
  11.0 6.8 %copy-start.5 = (f32[2048,128]{1,0:T(8,128)S(1)}, f32[2048,128]{1,0:T(8,128)}, u32[]{:S(2)}) copy-start(f32[2048,128]{1,0:T(8,128)} %param.11) | copy-start | bytes 3145732
  17.8 2.0 %copy-start.4 = (s32[6144]{0:T(1024)S(1)}, s32[6144]{0:T(1024)}, u32[]{:S(2)}) copy-start(s32[6144]{0:T(1024)} %param.14) | copy-start | bytes 73732
  17.9 15.3 %collective-permute-start.2 = (f32[1024,128]{1,0:T(8,128)S(1)}, f32[1024,128]{1,0:T(8,128)S(1)}, u32[]{:S(2)}, u32[]{:S(2)}) collective-permute-start(f32[1024,128]{1,0:T(8,128)S(1)} %get-tuple-element.21.a_ref), channel_id=1, source_target_pairs={{0,3},{1,2},{2,1},{3,0},{4,7},{5,6},{6,5},{7,4},{8,11},{9,10},{10,... | collective-permute-start | bytes 1572872 | tf_op jit(solution)/shard_map/ppermute | solution.py:490
  19.8 13.4 %collective-permute-start.3 = (f32[1024,128]{1,0:T(8,128)S(1)}, f32[1024,128]{1,0:T(8,128)S(1)}, u32[]{:S(2)}, u32[]{:S(2)}) collective-permute-start(f32[1024,128]{1,0:T(8,128)S(1)} %get-tuple-element.22.b_ref), channel_id=1, source_target_pairs={{0,1},{1,0},{2,3},{3,2},{4,5},{5,4},{6,7},{7,6},{8,9},{9,8},{10,11... | collective-permute-start | bytes 1572872 | tf_op jit(solution)/shard_map/ppermute | solution.py:490
  75.2 5.0 %copy-start = (f32[264,1024]{1,0:T(8,128)S(1)}, f32[264,1024]{1,0:T(8,128)}, u32[]{:S(2)}) copy-start(f32[264,1024]{1,0:T(8,128)} %w_ref.1) | copy-start | bytes 3244036
  75.2 5.0 %copy-start.1 = (f32[128,128]{1,0:T(8,128)S(1)}, f32[128,128]{1,0:T(8,128)}, u32[]{:S(2)}) copy-start(f32[128,128]{1,0:T(8,128)} %dense_ref.1) | copy-start | bytes 196612
  75.2 5.0 %copy-start.2 = (f32[2048]{0:T(1024)S(1)}, f32[2048]{0:T(1024)}, u32[]{:S(2)}) copy-start(f32[2048]{0:T(1024)} %param.12) | copy-start | bytes 24580
  75.2 5.0 %copy-start.3 = (f32[1024]{0:T(1024)S(1)}, f32[1024]{0:T(1024)}, u32[]{:S(2)}) copy-start(f32[1024]{0:T(1024)} %param.21) | copy-start | bytes 12292

commit v7 on v6

--- a/solution.py
+++ b/solution.py
@@ -20,9 +20,9 @@
 C_ROWS = 2304
 G_ROWS = 2304
 HALF = G_ROWS // 2
-PART = (40, 32)
+SEG = HALF // 48
 STRIDE = 37
-CUTS = (1, 32, 58, 82, 106, 128)
+CUTS = (1, 24, 44, 64, 128)
 PAIRS = [(i, j) for i in range(F + 1) for j in range(i + 1, F + 1)]
 PAIR_ROW = {pair: 128 + n for n, pair in enumerate(PAIRS)}
 
@@ -33,6 +33,7 @@
 
 VMEM = pl.BlockSpec(memory_space=pltpu.VMEM)
 SMEM = pl.BlockSpec(memory_space=pltpu.SMEM)
+ANY = pl.BlockSpec(memory_space=pl.ANY)
 
 
 def split(x):
@@ -126,7 +127,7 @@
 
 def pool_kernel(
     mask_ref,
-    bag_ref,
+    bag_in,
     slots_ref,
     c_ref,
     a_ref,
@@ -143,7 +144,11 @@
     row_recv,
     slot_send,
     slot_recv,
+    bag_ref,
+    bag_sem,
 ):
+    bag_copy = pltpu.make_async_copy(bag_in, bag_ref, bag_sem)
+    bag_copy.start()
     barrier = pltpu.get_barrier_semaphore()
     greet_all(barrier)
     me = my_number()
@@ -162,6 +167,7 @@
 
     lax.fori_loop(0, BAGS // 256, block, 0)
     got_ref[me] = slots_ref[me]
+    bag_copy.wait()
     pick_rows(recv_ref, me * CAP, partial_ref, bag_ref, me * CAP)
 
     def ready(k):
@@ -191,7 +197,14 @@
     put(send_ref.at[rows], recv_ref.at[rows], row_send, row_recv, to).wait()
 
 
-def place_kernel(slot_ref, got_ref, pooled):
+def place_kernel(slot_in, got_ref, pooled, slot_ref, sems):
+    part = DEVICES * 128 // 8
+    copies = []
+    for q in range(8):
+        here = pl.ds(q * part, part)
+        copies.append(pltpu.make_async_copy(slot_in.at[here], slot_ref.at[here], sems.at[q]))
+        copies[q].start()
+
     def place(c, carry):
         @pl.when(slot_ref[c * 128] < BAGS)
         def _():
@@ -200,13 +213,24 @@
 
         return carry
 
-    lax.fori_loop(0, DEVICES, place, 0)
+    for q in range(8):
+        copies[q].wait()
+        lax.fori_loop(q * DEVICES // 8, (q + 1) * DEVICES // 8, place, 0)
+
+
+def finish_kernel(a, b, c, d, to_a, to_b, to_c, to_d, sems):
+    pairs = ((a, to_a), (b, to_b), (c, to_c), (d, to_d))
+    copies = [pltpu.make_async_copy(x, y, sems.at[n]) for n, (x, y) in enumerate(pairs)]
+    for copy in copies:
+        copy.start()
+    for copy in copies:
+        copy.wait()
 
 
 def update_kernel(
     mask_ref,
-    slot_ref,
-    where_ref,
+    slot_in,
+    where_in,
     sums_ref,
     dense_ref,
     label_ref,
@@ -232,16 +256,14 @@
     r1,
     acc,
     states,
-    ra0,
-    ra1,
-    acc0,
-    acc1,
-    rb0,
-    rb1,
-    mine0,
-    mine1,
-    rx0,
-    rx1,
+    ra,
+    part_a,
+    rb,
+    mine,
+    rc,
+    slot_ref,
+    where_ref,
+    table_sem,
     state_send,
     state_recv,
     row_send,
@@ -253,6 +275,12 @@
     color_send,
     color_recv,
 ):
+    tables = [
+        pltpu.make_async_copy(slot_in, slot_ref, table_sem.at[0]),
+        pltpu.make_async_copy(where_in, where_ref, table_sem.at[1]),
+    ]
+    for copy in tables:
+        copy.start()
     barrier = pltpu.get_barrier_semaphore()
     greet_all(barrier)
     me = my_number()
@@ -349,35 +377,35 @@
             start(last)
 
     class Color:
-        def __init__(self, n, base, at, to_a, to_b, ra, acc2, rb, mine, rx):
-            self.n, self.rows, self.base, self.at = n, PART[n], base, at
-            self.to = (to_a, to_b, along_x, to_b, to_a)
-            self.ra, self.acc2, self.rb, self.mine, self.rx = ra, acc2, rb, mine, rx
+        def __init__(self, n, at, to):
+            self.n, self.at = n, at
+            self.to = (to[0], to[1], to[2], to[1], to[0])
+            self.base = n * 16 * SEG
 
         def move(self, phase, k, src, dst):
             sem = (self.n * 5 + phase) * 4 + k
             return put(src, dst, color_send.at[sem], color_recv.at[sem], self.to[phase](k))
 
         def rows_a(self, a, base):
-            return pl.ds(pl.multiple_of(base + self.base + a * (4 * self.rows), 8), 4 * self.rows)
+            return pl.ds(pl.multiple_of(base + self.base + a * (4 * SEG), 8), 4 * SEG)
 
         def rows_b(self, a, b, base):
-            return pl.ds(
-                pl.multiple_of(base + self.base + (a * 4 + b) * self.rows, 8), self.rows
-            )
+            return pl.ds(pl.multiple_of(base + self.base + (a * 4 + b) * SEG, 8), SEG)
 
         def moves(self, phase, waiting):
-            a, b = self.at
+            n = self.n
+            a, b, c = self.at
             out = []
             for k in range(1, 4):
                 if phase == 0:
-                    out.append(self.move(0, k, acc.at[self.rows_a((a + k) % 4, 0)], self.ra.at[k]))
+                    there = acc.at[self.rows_a((a + k) % 4, 0)]
+                    out.append(self.move(0, k, there, ra.at[4 * n + k]))
                 if phase == 1:
-                    there = pl.ds(pl.multiple_of((b + k) % 4 * self.rows, 8), self.rows)
-                    out.append(self.move(1, k, self.acc2.at[there], self.rb.at[k]))
+                    there = pl.ds(pl.multiple_of((b + k) % 4 * SEG, 8), SEG)
+                    out.append(self.move(1, k, part_a.at[n, there], rb.at[4 * n + k]))
                 if phase == 2:
-                    slot = (x + 4 - k) % 4 if waiting else x
-                    out.append(self.move(2, k, self.mine, self.rx.at[slot]))
+                    slot = (c + 4 - k) % 4 if waiting else c
+                    out.append(self.move(2, k, mine.at[n], rc.at[4 * n + slot]))
                 if phase == 3:
                     who = (b + 4 - k) % 4 if waiting else b
                     there = fin.at[self.rows_b(a, who, my_half)]
@@ -397,22 +425,24 @@
                 copy.wait_send()
             for copy in self.moves(phase, True):
                 copy.wait_recv()
-            a, b = self.at
+            n = self.n
+            a, b, c = self.at
             if phase == 0:
                 own = acc[self.rows_a(a, 0), :]
-                self.acc2[...] = (own + self.ra[1]) + (self.ra[2] + self.ra[3])
+                part_a[n] = (own + ra[4 * n + 1]) + (ra[4 * n + 2] + ra[4 * n + 3])
             if phase == 1:
-                own = self.acc2[pl.ds(pl.multiple_of(b * self.rows, 8), self.rows), :]
-                part = (own + self.rb[1]) + (self.rb[2] + self.rb[3])
-                self.mine[...] = part
-                self.rx[x] = part
+                own = part_a[n, pl.ds(pl.multiple_of(b * SEG, 8), SEG), :]
+                part = (own + rb[4 * n + 1]) + (rb[4 * n + 2] + rb[4 * n + 3])
+                mine[n] = part
+                rc[4 * n + c] = part
             if phase == 2:
-                whole = (self.rx[0] + self.rx[1]) + (self.rx[2] + self.rx[3])
+                whole = (rc[4 * n] + rc[4 * n + 1]) + (rc[4 * n + 2] + rc[4 * n + 3])
                 fin[self.rows_b(a, b, my_half), :] = whole
 
     colors = (
-        Color(0, 0, (z, y), along_z, along_y, ra0, acc0, rb0, mine0, rx0),
-        Color(1, 16 * PART[0], (y, z), along_y, along_z, ra1, acc1, rb1, mine1, rx1),
+        Color(0, (z, y, x), (along_z, along_y, along_x)),
+        Color(1, (y, x, z), (along_y, along_x, along_z)),
+        Color(2, (x, z, y), (along_x, along_z, along_y)),
     )
 
     def phase_on(phase):
@@ -426,16 +456,17 @@
     swap.wait()
     acc[...] = grad_ref[pl.ds(my_half, HALF), :] + r1[...]
     phase_on(0)
+    tables[0].wait()
     pick_rows(came, me * CAP, pooled, slot_ref, me * 128)
     ready(1)
     for phase in range(4):
         send_rows(phase)
         phase_off(phase)
         phase_on(phase + 1)
-    send_rows(4)
 
     rows = pl.ds(0, (DEVICES - 1) * CAP)
     put(back.at[rows], came.at[rows], row_send, row_recv, device_at(peer_of(1))).wait()
+    tables[1].wait()
     for move in state_moves:
         move.wait()
     mask = jnp.full((1, ROWS), mask_ref[0], i32)
@@ -555,7 +586,7 @@
             jax.ShapeDtypeStruct((DEVICES, 1, 128), i32),
             jax.ShapeDtypeStruct((ROWS, E), f32),
         ),
-        in_specs=[SMEM, SMEM, VMEM, VMEM, VMEM, VMEM, VMEM, VMEM],
+        in_specs=[SMEM, ANY, VMEM, VMEM, VMEM, VMEM, VMEM, VMEM],
         out_specs=(VMEM, VMEM, VMEM),
         scratch_shapes=[
             pltpu.VMEM((ROWS, 256), bf16),
@@ -565,6 +596,8 @@
             dma,
             dma,
             dma,
+            pltpu.SMEM((DEVICES * CAP,), i32),
+            dma,
         ],
         compiler_params=params(collective_id=0, has_side_effects=True, vmem_limit_bytes=20 << 20),
         name="pool",
@@ -574,13 +607,14 @@
     sums = pl.pallas_call(
         place_kernel,
         out_shape=jax.ShapeDtypeStruct((BAGS, E), f32),
-        in_specs=[SMEM, VMEM],
+        in_specs=[ANY, VMEM],
         out_specs=VMEM,
+        scratch_shapes=[pltpu.SMEM((DEVICES * 128,), i32), dma((8,))],
         compiler_params=params(vmem_limit_bytes=16 << 20),
         name="place",
     )(slot_of, got_rows)
 
-    new_table, new_state, top_grad, out_grad = pl.pallas_call(
+    results = pl.pallas_call(
         update_kernel,
         out_shape=(
             jax.ShapeDtypeStruct((ROWS, E), f32),
@@ -588,7 +622,7 @@
             jax.ShapeDtypeStruct((INTER, HID), f32),
             jax.ShapeDtypeStruct((1, HID), f32),
         ),
-        in_specs=[SMEM, SMEM, SMEM] + [VMEM] * 8,
+        in_specs=[SMEM, ANY, ANY] + [VMEM] * 8,
         out_specs=(VMEM, VMEM, VMEM, VMEM),
         scratch_shapes=[
             pltpu.VMEM((DEVICES * CAP, E), f32),
@@ -604,11 +638,14 @@
             pltpu.VMEM((HALF, 128), f32),
             pltpu.VMEM((HALF, 128), f32),
             pltpu.VMEM((4, 1, ROWS), f32),
-            *[pltpu.VMEM((4, 4 * rows, 128), f32) for rows in PART],
-            *[pltpu.VMEM((4 * rows, 128), f32) for rows in PART],
-            *[pltpu.VMEM((4, rows, 128), f32) for rows in PART],
-            *[pltpu.VMEM((rows, 128), f32) for rows in PART],
-            *[pltpu.VMEM((4, rows, 128), f32) for rows in PART],
+            pltpu.VMEM((12, 4 * SEG, 128), f32),
+            pltpu.VMEM((3, 4 * SEG, 128), f32),
+            pltpu.VMEM((12, SEG, 128), f32),
+            pltpu.VMEM((3, SEG, 128), f32),
+            pltpu.VMEM((12, SEG, 128), f32),
+            pltpu.SMEM((DEVICES * 128,), i32),
+            pltpu.SMEM((BAGS,), i32),
+            dma((2,)),
             dma((4,)),
             dma((4,)),
             dma,
@@ -617,8 +654,8 @@
             dma,
             dma,
             dma,
-            dma((40,)),
-            dma((40,)),
+            dma((60,)),
+            dma((60,)),
         ],
         compiler_params=params(collective_id=1, has_side_effects=True, vmem_limit_bytes=30 << 20),
         name="update",
@@ -635,6 +672,15 @@
         held,
         row_state[None, :],
     )
+    new_table, new_state, top_grad, out_grad = pl.pallas_call(
+        finish_kernel,
+        out_shape=tuple(jax.ShapeDtypeStruct(r.shape, f32) for r in results),
+        in_specs=[ANY] * 4,
+        out_specs=(ANY,) * 4,
+        scratch_shapes=[dma((4,))],
+        compiler_params=params(vmem_limit_bytes=16 << 20),
+        name="finish",
+    )(*results)
     return new_table, new_state.reshape(ROWS), top_grad, out_grad.reshape(HID)
 
 

time: 143 us -> 134 us (0.937)
  Pallas kernels: 120 us -> 114 us
  local copies, waits for them, and re-layouts: 5.66 us -> 2.51 us
    pallas_call x1, Pallas kernels: 59.2 us -> 53.7 us  [on_device(): pl.pallas_call(update_kernel, out_shape=(jax.ShapeDtypeStruct((ROWS, E),...]
    unnamed x24 -> x20, local copies, waits for them, and re-layouts: 3.54 us -> 0.39 us
  transfers between devices with their start and end apart: 4 -> 4, of which waited for: 2 -> 2; matrix products, arithmetic and copies ran while one was open for 4% -> 4% of each run, Pallas kernels for 9% -> 10%
where the time goes in v7:
time: 134 us
  Pallas kernels  114 us (85%)
  starting transfers between devices  5.82 us (4%)
  waiting for transfers between devices  4.84 us (4%)
  other arithmetic  3.92 us (3%)
  local copies, waits for them, and re-layouts  2.51 us (2%)
  between operations  1.72 us (1%)
    pallas_call x1, Pallas kernels, on_device(): pl.pallas_call(update_kernel, out_shape=(jax.ShapeDtypeStruct((ROWS, E),...  53.7 us
    pallas_call x1, Pallas kernels, on_device(): pl.pallas_call(pool_kernel, out_shape=(jax.ShapeDtypeStruct((DEVICES * CA...  41.3 us
    pallas_call x1, Pallas kernels, on_device(): pl.pallas_call(count_kernel, out_shape=jax.ShapeDtypeStruct((C_ROWS, ROWS...  13.3 us
    ppermute x4, starting transfers between devices, from_partner(): return lax.ppermute(block, 'gy', [(y, y ^ flip) for y in range(4)])  5.82 us
    ppermute x4, waiting for transfers between devices, from_partner(): return lax.ppermute(block, 'gy', [(y, y ^ flip) for y in range(4)])  4.84 us
    pallas_call x1, Pallas kernels, on_device(): pl.pallas_call(place_kernel, out_shape=jax.ShapeDtypeStruct((BAGS, E), f3...  4.15 us
    another operation x6, other arithmetic  2.75 us
  transfers between devices with their start and end apart: 4, of which 2 were waited for; matrix products, arithmetic and copies ran while one was open for 4% of the time, Pallas kernels for 10%

profile of v7, /device:TPU:1, one launch (start us, length us, event | category | flops | bytes accessed | tf_op | source)
XLA Modules:
  0.0 133.9 jit_solution(607176220423593041)
XLA Ops:
  0.7 1.3 fusion.31
  1.9 2.1 %collective-permute-start = (f32[1024,128]{1,0:T(8,128)S(1)}, f32[1024,128]{1,0:T(8,128)S(1)}, u32[]{:S(2)}, u32[]{:S(2)}) collective-permute-start(f32[1024,128]{1,0:T(8,128)S(1)} %get-tuple-element.43), channel_id=1, source_target_pairs={{0,1},{1,0},{2,3},{3,2},{4,5},{5,4},{6,7},{7,6},{8,9},{9,8},{10,11... | collective-permute-start | bytes 1572872 | tf_op jit(solution)/shard_map/ppermute | solution.py:521
  4.0 1.8 %collective-permute-start.1 = (f32[1024,128]{1,0:T(8,128)S(1)}, f32[1024,128]{1,0:T(8,128)S(1)}, u32[]{:S(2)}, u32[]{:S(2)}) collective-permute-start(f32[1024,128]{1,0:T(8,128)S(1)} %get-tuple-element.42), channel_id=1, source_target_pairs={{0,3},{1,2},{2,1},{3,0},{4,7},{5,6},{6,5},{7,4},{8,11},{9,10},{10,... | collective-permute-start | bytes 1572872 | tf_op jit(solution)/shard_map/ppermute | solution.py:521
  6.6 0.3 reduce-window.19
  6.8 0.1 slice.47
  7.0 0.1 slice_reduce_fusion
  7.1 0.1 copy.22
  7.2 0.3 fusion.2
  7.6 0.1 broadcast_add_fusion
  7.6 0.0 copy-start.8
  7.7 0.3 copy.23
  8.0 0.3 copy-done.8
  8.4 0.6 fusion.1
  9.0 2.0 %select_convert_fusion.3 = (bf16[2048,32]{1,0:T(8,128)(2,1)S(1)}, bf16[2048,32]{1,0:T(8,128)(2,1)S(1)}, bf16[2048,32]{1,0:T(8,128)(2,1)S(1)}, bf16[2048,32]{1,0:T(8,128)(2,1)S(1)}) fusion(bf16[2048]{0:T(1024)(128)(2,1)S(1)} %get-tuple-element.50, s32[2048]{0:T(1024)S(1)} %fusion.1, bf16[2048]{0:T(1024)(128)(2,1)S(1)} %fusion.24, ...), kind=kLoop, calls=%fused_computation.8 | loop fusion | flops 327680 | bytes 548864 | tf_op jit(solution)/shard_map/convert
  11.0 0.0 copy-start.9
  11.0 1.3 convolution_convert_fusion
  12.3 0.1 fusion.13
  12.4 0.1 reshape.114.bag_in
  12.5 0.1 copy.25.label_ref
  12.6 0.1 fusion.30
  12.7 0.2 convert_reduce_fusion
  12.9 2.3 %collective-permute-done = f32[1024,128]{1,0:T(8,128)S(1)} collective-permute-done((f32[1024,128]{1,0:T(8,128)S(1)}, f32[1024,128]{1,0:T(8,128)S(1)}, u32[]{:S(2)}, u32[]{:S(2)}) %collective-permute-start) | collective-permute-done | bytes 524320 | tf_op jit(solution)/shard_map/ppermute | solution.py:521
  15.3 2.5 %collective-permute-done.1 = f32[1024,128]{1,0:T(8,128)S(1)} collective-permute-done((f32[1024,128]{1,0:T(8,128)S(1)}, f32[1024,128]{1,0:T(8,128)S(1)}, u32[]{:S(2)}, u32[]{:S(2)}) %collective-permute-start.1) | collective-permute-done | bytes 524320 | tf_op jit(solution)/shard_map/ppermute | solution.py:521
  17.8 0.1 broadcast_select_fusion
  17.9 1.9 %collective-permute-start.2 = (f32[1024,128]{1,0:T(8,128)S(1)}, f32[1024,128]{1,0:T(8,128)S(1)}, u32[]{:S(2)}, u32[]{:S(2)}) collective-permute-start(f32[1024,128]{1,0:T(8,128)S(1)} %get-tuple-element.25.a_ref), channel_id=1, source_target_pairs={{0,3},{1,2},{2,1},{3,0},{4,7},{5,6},{6,5},{7,4},{8,11},{9,10},{10,... | collective-permute-start | bytes 1572872 | tf_op jit(solution)/shard_map/ppermute | solution.py:521
  19.8 13.3 %count.1.c_ref = bf16[2304,2048]{1,0:T(8,128)(2,1)S(1)} custom-call(s32[24]{0:T(128)S(1)} %fusion.28.first_ref, s32[48,128]{1,0:T(8,128)S(1)} %bitcast.32, s32[18,128]{1,0:T(8,128)S(1)} %get-tuple-element.23.start_ref, s32[18,128]{1,0:T(8,128)S(1)} %get-tuple-element.24.end_ref), custom_call_target="tpu_custom_call" | custom-call | flops 6845104128 | bytes 10485760 | tf_op jit(solution)/shard_map/count/pallas_call | solution.py:570
  33.1 41.3 %pool.1 = (f32[4096,128]{1,0:T(8,128)S(1)}, s32[128,1,128]{2,1,0:T(1,128)S(1)}, f32[2048,128]{1,0:T(8,128)S(1)}) custom-call(s32[1]{0:T(128)S(6)} %copy.27.mask_ref, s32[4096]{0:T(1024)S(1)} %reshape.114.bag_in, s32[128,1,128]{2,1,0:T(1,128)S(1)} %bitcast.29, bf16[2304,2048]{1,0:T(8,128)(2,1)S(1)} %count.1.c_ref, f32[1024,128]{1,0:T(8,128)S(1)} %get-tuple-element.25.a_ref, ...), custom_call_target="tpu_custom_call" | custom-call | tf_op jit(solution)/shard_map/pool/pallas_call | solution.py:582
  74.4 0.0 copy-start
  74.5 0.0 copy-start.3
  74.5 4.2 %place.1.sums_ref = f32[2048,128]{1,0:T(8,128)S(1)} custom-call(s32[16384]{0:T(1024)S(1)} %bitcast.27, f32[4096,128]{1,0:T(8,128)S(1)} %get-tuple-element.28.got_ref), custom_call_target="tpu_custom_call" | custom-call | tf_op jit(solution)/shard_map/place/pallas_call | solution.py:607
  78.7 53.7 %update.1 = (f32[2048,128]{1,0:T(8,128)S(1)}, f32[1,2048]{1,0:T(1,128)S(1)}, f32[264,1024]{1,0:T(8,128)S(1)}, f32[1,1024]{1,0:T(1,128)S(1)}) custom-call(s32[1]{0:T(128)S(6)} %copy.27.mask_ref, s32[16384]{0:T(1024)S(1)} %bitcast.28, s32[2048]{0:T(1024)S(1)} %multiply_add_fusion.where_in, f32[2048,128]{1,0:T(8,128)S(1)} %place.1.sums_ref, ...), custom_call_target="tpu_custom_call" | custom-call | tf_op jit(solution)/shard_map/update/pallas_call | solution.py:617
  132.4 1.4 %finish.1 = (f32[2048,128]{1,0:T(8,128)}, f32[1,2048]{1,0:T(1,128)}, f32[264,1024]{1,0:T(8,128)}, f32[1,1024]{1,0:T(1,128)}) custom-call(f32[2048,128]{1,0:T(8,128)S(1)} %get-tuple-element.30.a, f32[1,2048]{1,0:T(1,128)S(1)} %get-tuple-element.31.b, f32[264,1024]{1,0:T(8,128)S(1)} %get-tuple-element.32.c, f32[1,1024]{1,0:T(1,128)S(1)} %get-tuple-element.33.d), custom_call_target="tpu_custom_call" | custom-call | tf_op jit(solution)/shard_map/finish/pallas_call | solution.py:675
  (29 shorter events, 0.2 us)
Async XLA Ops:
  0.6 5.9 %copy-start.7 = (s32[1,2048]{1,0:T(1,128)S(1)}, s32[1,2048]{1,0:T(1,128)}, u32[]{:S(2)}) copy-start(s32[1,2048]{1,0:T(1,128)} %param.15) | copy-start | bytes 24580
  0.6 6.4 %copy-start.6 = (s32[2048,1]{0,1:T(1,128)S(1)}, s32[2048,1]{0,1:T(1,128)}, u32[]{:S(2)}) copy-start(s32[2048,1]{0,1:T(1,128)} %param.16) | copy-start | bytes 24580
  1.9 13.3 %collective-permute-start = (f32[1024,128]{1,0:T(8,128)S(1)}, f32[1024,128]{1,0:T(8,128)S(1)}, u32[]{:S(2)}, u32[]{:S(2)}) collective-permute-start(f32[1024,128]{1,0:T(8,128)S(1)} %get-tuple-element.43), channel_id=1, source_target_pairs={{0,1},{1,0},{2,3},{3,2},{4,5},{5,4},{6,7},{7,6},{8,9},{9,8},{10,11... | collective-permute-start | bytes 1572872 | tf_op jit(solution)/shard_map/ppermute | solution.py:521
  4.0 13.7 %collective-permute-start.1 = (f32[1024,128]{1,0:T(8,128)S(1)}, f32[1024,128]{1,0:T(8,128)S(1)}, u32[]{:S(2)}, u32[]{:S(2)}) collective-permute-start(f32[1024,128]{1,0:T(8,128)S(1)} %get-tuple-element.42), channel_id=1, source_target_pairs={{0,3},{1,2},{2,1},{3,0},{4,7},{5,6},{6,5},{7,4},{8,11},{9,10},{10,... | collective-permute-start | bytes 1572872 | tf_op jit(solution)/shard_map/ppermute | solution.py:521
  7.6 0.7 copy-start.8
  11.0 1.5 %copy-start.9 = (f32[128]{0:T(128)S(1)}, f32[128]{0:T(128)}, u32[]{:S(2)}) copy-start(f32[128]{0:T(128)} %param.19) | copy-start | bytes 1540
  11.0 6.8 %copy-start.5 = (f32[2048,128]{1,0:T(8,128)S(1)}, f32[2048,128]{1,0:T(8,128)}, u32[]{:S(2)}) copy-start(f32[2048,128]{1,0:T(8,128)} %param.11) | copy-start | bytes 3145732
  17.8 2.0 %copy-start.4 = (s32[6144]{0:T(1024)S(1)}, s32[6144]{0:T(1024)}, u32[]{:S(2)}) copy-start(s32[6144]{0:T(1024)} %param.14) | copy-start | bytes 73732
  17.9 15.2 %collective-permute-start.2 = (f32[1024,128]{1,0:T(8,128)S(1)}, f32[1024,128]{1,0:T(8,128)S(1)}, u32[]{:S(2)}, u32[]{:S(2)}) collective-permute-start(f32[1024,128]{1,0:T(8,128)S(1)} %get-tuple-element.25.a_ref), channel_id=1, source_target_pairs={{0,3},{1,2},{2,1},{3,0},{4,7},{5,6},{6,5},{7,4},{8,11},{9,10},{10,... | collective-permute-start | bytes 1572872 | tf_op jit(solution)/shard_map/ppermute | solution.py:521
  19.8 13.4 %collective-permute-start.3 = (f32[1024,128]{1,0:T(8,128)S(1)}, f32[1024,128]{1,0:T(8,128)S(1)}, u32[]{:S(2)}, u32[]{:S(2)}) collective-permute-start(f32[1024,128]{1,0:T(8,128)S(1)} %get-tuple-element.26.b_ref), channel_id=1, source_target_pairs={{0,1},{1,0},{2,3},{3,2},{4,5},{5,4},{6,7},{7,6},{8,9},{9,8},{10,11... | collective-permute-start | bytes 1572872 | tf_op jit(solution)/shard_map/ppermute | solution.py:521
  74.4 4.2 %copy-start = (f32[264,1024]{1,0:T(8,128)S(1)}, f32[264,1024]{1,0:T(8,128)}, u32[]{:S(2)}) copy-start(f32[264,1024]{1,0:T(8,128)} %w_ref.1) | copy-start | bytes 3244036
  74.4 4.2 %copy-start.1 = (f32[128,128]{1,0:T(8,128)S(1)}, f32[128,128]{1,0:T(8,128)}, u32[]{:S(2)}) copy-start(f32[128,128]{1,0:T(8,128)} %dense_ref.1) | copy-start | bytes 196612
  74.4 4.2 %copy-start.2 = (f32[2048]{0:T(1024)S(1)}, f32[2048]{0:T(1024)}, u32[]{:S(2)}) copy-start(f32[2048]{0:T(1024)} %param.12) | copy-start | bytes 24580
  74.5 4.2 %copy-start.3 = (f32[1024]{0:T(1024)S(1)}, f32[1024]{0:T(1024)}, u32[]{:S(2)}) copy-start(f32[1024]{0:T(1024)} %param.21) | copy-start | bytes 12292

commit v8 on v7

--- a/solution.py
+++ b/solution.py
@@ -22,7 +22,7 @@
 HALF = G_ROWS // 2
 SEG = HALF // 48
 STRIDE = 37
-CUTS = (1, 24, 44, 64, 128)
+CUTS = (0, 4, 7, 9, 27)
 PAIRS = [(i, j) for i in range(F + 1) for j in range(i + 1, F + 1)]
 PAIR_ROW = {pair: 128 + n for n, pair in enumerate(PAIRS)}
 
@@ -114,6 +114,51 @@
     return pltpu.make_async_remote_copy(
         src_ref=src, dst_ref=dst, send_sem=send, recv_sem=recv, device_id=device, device_id_type=MESH
     )
+
+
+def distance(kind):
+    return sum(kind)
+
+
+KINDS = sorted(
+    ((dx, dy, dz) for dx in (2, 1, 0) for dy in (2, 1, 0) for dz in (2, 1, 0)),
+    key=lambda kind: -distance(kind),
+)
+
+
+def steps_of(kind):
+    return 2 * 2 ** kind.count(1) if distance(kind) else 1
+
+
+def peer_in(kind, j):
+    gx = lax.axis_index("gx")
+    at = [lax.axis_index("gy"), gx // 8, gx // 2 % 4]
+    core, rest = (1, 0) if distance(kind) == 0 else (j % 2, j // 2)
+    there = []
+    for here, far in zip(at, kind):
+        if far == 1:
+            far, rest = 1 + 2 * (rest % 2), rest // 2
+        there.append((here + far) % 4)
+    x, y, z = there
+    return ((y * 4 + z) * 2 + (gx + core) % 2) * 4 + x
+
+
+def send_kinds(kinds, ready, start, waiting):
+    for kind in kinds:
+        count = steps_of(kind)
+        ready(peer_in(kind, 0))
+        if waiting is not None:
+            start(waiting)
+
+        def step(j, carry, kind=kind):
+            ready(peer_in(kind, j))
+            start(peer_in(kind, j - 1))
+            return carry
+
+        if count > 1:
+            lax.fori_loop(1, count, step, 0)
+        waiting = peer_in(kind, count - 1)
+    return waiting
 
 
 def chunk_at(n):
@@ -170,26 +215,16 @@
     bag_copy.wait()
     pick_rows(recv_ref, me * CAP, partial_ref, bag_ref, me * CAP)
 
-    def ready(k):
-        at = peer_of(k) * CAP
-        pick_rows(send_ref, at, partial_ref, bag_ref, at)
-
-    def start(k):
-        peer = peer_of(k)
+    def ready(peer):
+        pick_rows(send_ref, peer * CAP, partial_ref, bag_ref, peer * CAP)
+
+    def start(peer):
         to = device_at(peer)
         put(slots_ref.at[peer], got_ref.at[me], slot_send, slot_recv, to).start()
         put(send_ref.at[chunk_at(peer)], recv_ref.at[chunk_at(me)], row_send, row_recv, to).start()
 
-    ready(1)
     pl.semaphore_wait(barrier, DEVICES - 1)
-
-    def step(k, carry):
-        ready(k)
-        start(k - 1)
-        return carry
-
-    lax.fori_loop(2, DEVICES, step, 0)
-    start(DEVICES - 1)
+    start(send_kinds(KINDS, ready, start, None))
     to = device_at(peer_of(1))
     some = pl.ds(0, DEVICES - 1)
     put(slots_ref.at[some], got_ref.at[some], slot_send, slot_recv, to).wait()
@@ -355,26 +390,13 @@
         pooled_grad(j)
     pooled[BAGS:, :] = jnp.zeros((8, E), f32)
 
-    def ready(k):
-        peer = peer_of(k)
+    def ready(peer):
         pick_rows(back, peer * CAP, pooled, slot_ref, peer * 128)
 
-    def start(k):
-        peer = peer_of(k)
+    def start(peer):
         put(
             back.at[chunk_at(peer)], came.at[chunk_at(me)], row_send, row_recv, device_at(peer)
         ).start()
-
-    def send_rows(n):
-        def step(k, carry):
-            ready(k + 1)
-            start(k)
-            return carry
-
-        last = DEVICES - 1 if CUTS[n + 1] == DEVICES else CUTS[n + 1]
-        lax.fori_loop(CUTS[n], last, step, 0)
-        if last < CUTS[n + 1]:
-            start(last)
 
     class Color:
         def __init__(self, n, at, to):
@@ -458,9 +480,11 @@
     phase_on(0)
     tables[0].wait()
     pick_rows(came, me * CAP, pooled, slot_ref, me * 128)
-    ready(1)
+    waiting = None
     for phase in range(4):
-        send_rows(phase)
+        waiting = send_kinds(KINDS[CUTS[phase] : CUTS[phase + 1]], ready, start, waiting)
+        if phase == 3:
+            start(waiting)
         phase_off(phase)
         phase_on(phase + 1)
 

time: 134 us -> 136 us (1.015)
  Pallas kernels: 114 us -> 116 us
where the time goes in v8:
time: 136 us
  Pallas kernels  116 us (85%)
  starting transfers between devices  5.82 us (4%)
  waiting for transfers between devices  4.84 us (4%)
  other arithmetic  3.92 us (3%)
  local copies, waits for them, and re-layouts  2.51 us (2%)
  between operations  1.72 us (1%)
    pallas_call x1, Pallas kernels, on_device(): pl.pallas_call(update_kernel, out_shape=(jax.ShapeDtypeStruct((ROWS, E),...  54.3 us
    pallas_call x1, Pallas kernels, on_device(): pl.pallas_call(pool_kernel, out_shape=(jax.ShapeDtypeStruct((DEVICES * CA...  42.4 us
    pallas_call x1, Pallas kernels, on_device(): pl.pallas_call(count_kernel, out_shape=jax.ShapeDtypeStruct((C_ROWS, ROWS...  13.5 us
    ppermute x4, starting transfers between devices, from_partner(): return lax.ppermute(block, 'gy', [(y, y ^ flip) for y in range(4)])  5.82 us
    ppermute x4, waiting for transfers between devices, from_partner(): return lax.ppermute(block, 'gy', [(y, y ^ flip) for y in range(4)])  4.84 us
    pallas_call x1, Pallas kernels, on_device(): pl.pallas_call(place_kernel, out_shape=jax.ShapeDtypeStruct((BAGS, E), f3...  4.15 us
    another operation x6, other arithmetic  2.75 us
  transfers between devices with their start and end apart: 4, of which 2 were waited for; matrix products, arithmetic and copies ran while one was open for 4% of the time, Pallas kernels for 10%

profile of v8, /device:TPU:1, one launch (start us, length us, event | category | flops | bytes accessed | tf_op | source)
XLA Modules:
  0.0 135.7 jit_solution(9256477093705974610)
XLA Ops:
  0.7 1.3 fusion.31
  1.9 2.1 %collective-permute-start = (f32[1024,128]{1,0:T(8,128)S(1)}, f32[1024,128]{1,0:T(8,128)S(1)}, u32[]{:S(2)}, u32[]{:S(2)}) collective-permute-start(f32[1024,128]{1,0:T(8,128)S(1)} %get-tuple-element.43), channel_id=1, source_target_pairs={{0,1},{1,0},{2,3},{3,2},{4,5},{5,4},{6,7},{7,6},{8,9},{9,8},{10,11... | collective-permute-start | bytes 1572872 | tf_op jit(solution)/shard_map/ppermute | solution.py:545
  4.0 1.8 %collective-permute-start.1 = (f32[1024,128]{1,0:T(8,128)S(1)}, f32[1024,128]{1,0:T(8,128)S(1)}, u32[]{:S(2)}, u32[]{:S(2)}) collective-permute-start(f32[1024,128]{1,0:T(8,128)S(1)} %get-tuple-element.42), channel_id=1, source_target_pairs={{0,3},{1,2},{2,1},{3,0},{4,7},{5,6},{6,5},{7,4},{8,11},{9,10},{10,... | collective-permute-start | bytes 1572872 | tf_op jit(solution)/shard_map/ppermute | solution.py:545
  6.6 0.3 reduce-window.19
  6.8 0.1 slice.47
  7.0 0.1 slice_reduce_fusion
  7.1 0.1 copy.22
  7.2 0.3 fusion.2
  7.6 0.1 broadcast_add_fusion
  7.6 0.0 copy-start.8
  7.7 0.3 copy.23
  8.0 0.3 copy-done.8
  8.4 0.6 fusion.1
  9.0 2.0 %select_convert_fusion.3 = (bf16[2048,32]{1,0:T(8,128)(2,1)S(1)}, bf16[2048,32]{1,0:T(8,128)(2,1)S(1)}, bf16[2048,32]{1,0:T(8,128)(2,1)S(1)}, bf16[2048,32]{1,0:T(8,128)(2,1)S(1)}) fusion(bf16[2048]{0:T(1024)(128)(2,1)S(1)} %get-tuple-element.50, s32[2048]{0:T(1024)S(1)} %fusion.1, bf16[2048]{0:T(1024)(128)(2,1)S(1)} %fusion.24, ...), kind=kLoop, calls=%fused_computation.8 | loop fusion | flops 327680 | bytes 548864 | tf_op jit(solution)/shard_map/convert
  11.0 0.0 copy-start.5
  11.0 1.3 convolution_convert_fusion
  12.3 0.1 fusion.13
  12.4 0.1 reshape.114.bag_in
  12.5 0.1 copy.25.label_ref
  12.6 0.1 fusion.30
  12.7 0.2 convert_reduce_fusion
  12.9 2.3 %collective-permute-done = f32[1024,128]{1,0:T(8,128)S(1)} collective-permute-done((f32[1024,128]{1,0:T(8,128)S(1)}, f32[1024,128]{1,0:T(8,128)S(1)}, u32[]{:S(2)}, u32[]{:S(2)}) %collective-permute-start) | collective-permute-done | bytes 524320 | tf_op jit(solution)/shard_map/ppermute | solution.py:545
  15.3 2.5 %collective-permute-done.1 = f32[1024,128]{1,0:T(8,128)S(1)} collective-permute-done((f32[1024,128]{1,0:T(8,128)S(1)}, f32[1024,128]{1,0:T(8,128)S(1)}, u32[]{:S(2)}, u32[]{:S(2)}) %collective-permute-start.1) | collective-permute-done | bytes 524320 | tf_op jit(solution)/shard_map/ppermute | solution.py:545
  17.8 0.1 broadcast_select_fusion
  17.9 1.9 %collective-permute-start.2 = (f32[1024,128]{1,0:T(8,128)S(1)}, f32[1024,128]{1,0:T(8,128)S(1)}, u32[]{:S(2)}, u32[]{:S(2)}) collective-permute-start(f32[1024,128]{1,0:T(8,128)S(1)} %get-tuple-element.25.a_ref), channel_id=1, source_target_pairs={{0,3},{1,2},{2,1},{3,0},{4,7},{5,6},{6,5},{7,4},{8,11},{9,10},{10,... | collective-permute-start | bytes 1572872 | tf_op jit(solution)/shard_map/ppermute | solution.py:545
  19.8 13.5 %count.1.c_ref = bf16[2304,2048]{1,0:T(8,128)(2,1)S(1)} custom-call(s32[24]{0:T(128)S(1)} %fusion.28.first_ref, s32[48,128]{1,0:T(8,128)S(1)} %bitcast.32, s32[18,128]{1,0:T(8,128)S(1)} %get-tuple-element.23.start_ref, s32[18,128]{1,0:T(8,128)S(1)} %get-tuple-element.24.end_ref), custom_call_target="tpu_custom_call" | custom-call | flops 6845104128 | bytes 10485760 | tf_op jit(solution)/shard_map/count/pallas_call | solution.py:594
  33.3 42.4 %pool.1 = (f32[4096,128]{1,0:T(8,128)S(1)}, s32[128,1,128]{2,1,0:T(1,128)S(1)}, f32[2048,128]{1,0:T(8,128)S(1)}) custom-call(s32[1]{0:T(128)S(6)} %copy.27.mask_ref, s32[4096]{0:T(1024)S(1)} %reshape.114.bag_in, s32[128,1,128]{2,1,0:T(1,128)S(1)} %bitcast.29, bf16[2304,2048]{1,0:T(8,128)(2,1)S(1)} %count.1.c_ref, f32[1024,128]{1,0:T(8,128)S(1)} %get-tuple-element.25.a_ref, ...), custom_call_target="tpu_custom_call" | custom-call | tf_op jit(solution)/shard_map/pool/pallas_call | solution.py:606
  75.7 0.0 copy-start
  75.7 0.0 copy-start.1
  75.7 4.2 %place.1.sums_ref = f32[2048,128]{1,0:T(8,128)S(1)} custom-call(s32[16384]{0:T(1024)S(1)} %bitcast.27, f32[4096,128]{1,0:T(8,128)S(1)} %get-tuple-element.28.got_ref), custom_call_target="tpu_custom_call" | custom-call | tf_op jit(solution)/shard_map/place/pallas_call | solution.py:631
  79.9 54.3 %update.1 = (f32[2048,128]{1,0:T(8,128)S(1)}, f32[1,2048]{1,0:T(1,128)S(1)}, f32[264,1024]{1,0:T(8,128)S(1)}, f32[1,1024]{1,0:T(1,128)S(1)}) custom-call(s32[1]{0:T(128)S(6)} %copy.27.mask_ref, s32[16384]{0:T(1024)S(1)} %bitcast.28, s32[2048]{0:T(1024)S(1)} %multiply_add_fusion.where_in, f32[2048,128]{1,0:T(8,128)S(1)} %place.1.sums_ref, ...), custom_call_target="tpu_custom_call" | custom-call | tf_op jit(solution)/shard_map/update/pallas_call | solution.py:641
  134.2 1.4 %finish.1 = (f32[2048,128]{1,0:T(8,128)}, f32[1,2048]{1,0:T(1,128)}, f32[264,1024]{1,0:T(8,128)}, f32[1,1024]{1,0:T(1,128)}) custom-call(f32[2048,128]{1,0:T(8,128)S(1)} %get-tuple-element.30.a, f32[1,2048]{1,0:T(1,128)S(1)} %get-tuple-element.31.b, f32[264,1024]{1,0:T(8,128)S(1)} %get-tuple-element.32.c, f32[1,1024]{1,0:T(1,128)S(1)} %get-tuple-element.33.d), custom_call_target="tpu_custom_call" | custom-call | tf_op jit(solution)/shard_map/finish/pallas_call | solution.py:699
  (29 shorter events, 0.2 us)
Async XLA Ops:
  0.6 5.9 %copy-start.7 = (s32[1,2048]{1,0:T(1,128)S(1)}, s32[1,2048]{1,0:T(1,128)}, u32[]{:S(2)}) copy-start(s32[1,2048]{1,0:T(1,128)} %param.15) | copy-start | bytes 24580
  0.6 6.4 %copy-start.6 = (s32[2048,1]{0,1:T(1,128)S(1)}, s32[2048,1]{0,1:T(1,128)}, u32[]{:S(2)}) copy-start(s32[2048,1]{0,1:T(1,128)} %param.16) | copy-start | bytes 24580
  1.9 13.3 %collective-permute-start = (f32[1024,128]{1,0:T(8,128)S(1)}, f32[1024,128]{1,0:T(8,128)S(1)}, u32[]{:S(2)}, u32[]{:S(2)}) collective-permute-start(f32[1024,128]{1,0:T(8,128)S(1)} %get-tuple-element.43), channel_id=1, source_target_pairs={{0,1},{1,0},{2,3},{3,2},{4,5},{5,4},{6,7},{7,6},{8,9},{9,8},{10,11... | collective-permute-start | bytes 1572872 | tf_op jit(solution)/shard_map/ppermute | solution.py:545
  4.0 13.7 %collective-permute-start.1 = (f32[1024,128]{1,0:T(8,128)S(1)}, f32[1024,128]{1,0:T(8,128)S(1)}, u32[]{:S(2)}, u32[]{:S(2)}) collective-permute-start(f32[1024,128]{1,0:T(8,128)S(1)} %get-tuple-element.42), channel_id=1, source_target_pairs={{0,3},{1,2},{2,1},{3,0},{4,7},{5,6},{6,5},{7,4},{8,11},{9,10},{10,... | collective-permute-start | bytes 1572872 | tf_op jit(solution)/shard_map/ppermute | solution.py:545
  7.6 0.7 copy-start.8
  11.0 1.5 %copy-start.9 = (f32[128]{0:T(128)S(1)}, f32[128]{0:T(128)}, u32[]{:S(2)}) copy-start(f32[128]{0:T(128)} %param.19) | copy-start | bytes 1540
  11.0 6.8 %copy-start.5 = (f32[2048,128]{1,0:T(8,128)S(1)}, f32[2048,128]{1,0:T(8,128)}, u32[]{:S(2)}) copy-start(f32[2048,128]{1,0:T(8,128)} %param.11) | copy-start | bytes 3145732
  17.8 2.0 %copy-start.4 = (s32[6144]{0:T(1024)S(1)}, s32[6144]{0:T(1024)}, u32[]{:S(2)}) copy-start(s32[6144]{0:T(1024)} %param.14) | copy-start | bytes 73732
  17.9 15.4 %collective-permute-start.2 = (f32[1024,128]{1,0:T(8,128)S(1)}, f32[1024,128]{1,0:T(8,128)S(1)}, u32[]{:S(2)}, u32[]{:S(2)}) collective-permute-start(f32[1024,128]{1,0:T(8,128)S(1)} %get-tuple-element.25.a_ref), channel_id=1, source_target_pairs={{0,3},{1,2},{2,1},{3,0},{4,7},{5,6},{6,5},{7,4},{8,11},{9,10},{10,... | collective-permute-start | bytes 1572872 | tf_op jit(solution)/shard_map/ppermute | solution.py:545
  19.8 13.5 %collective-permute-start.3 = (f32[1024,128]{1,0:T(8,128)S(1)}, f32[1024,128]{1,0:T(8,128)S(1)}, u32[]{:S(2)}, u32[]{:S(2)}) collective-permute-start(f32[1024,128]{1,0:T(8,128)S(1)} %get-tuple-element.26.b_ref), channel_id=1, source_target_pairs={{0,1},{1,0},{2,3},{3,2},{4,5},{5,4},{6,7},{7,6},{8,9},{9,8},{10,11... | collective-permute-start | bytes 1572872 | tf_op jit(solution)/shard_map/ppermute | solution.py:545
  75.7 4.2 %copy-start = (f32[264,1024]{1,0:T(8,128)S(1)}, f32[264,1024]{1,0:T(8,128)}, u32[]{:S(2)}) copy-start(f32[264,1024]{1,0:T(8,128)} %w_ref.1) | copy-start | bytes 3244036
  75.7 4.2 %copy-start.1 = (f32[128,128]{1,0:T(8,128)S(1)}, f32[128,128]{1,0:T(8,128)}, u32[]{:S(2)}) copy-start(f32[128,128]{1,0:T(8,128)} %dense_ref.1) | copy-start | bytes 196612
  75.7 4.2 %copy-start.2 = (f32[2048]{0:T(1024)S(1)}, f32[2048]{0:T(1024)}, u32[]{:S(2)}) copy-start(f32[2048]{0:T(1024)} %param.12) | copy-start | bytes 24580
  75.7 4.2 %copy-start.3 = (f32[1024]{0:T(1024)S(1)}, f32[1024]{0:T(1024)}, u32[]{:S(2)}) copy-start(f32[1024]{0:T(1024)} %param.21) | copy-start | bytes 12292

commit v9 on v7

--- a/solution.py
+++ b/solution.py
@@ -21,8 +21,8 @@
 G_ROWS = 2304
 HALF = G_ROWS // 2
 SEG = HALF // 48
-STRIDE = 37
-CUTS = (1, 24, 44, 64, 128)
+STRIDE = 91
+CUTS = (1, 32, 64, 96, 128)
 PAIRS = [(i, j) for i in range(F + 1) for j in range(i + 1, F + 1)]
 PAIR_ROW = {pair: 128 + n for n, pair in enumerate(PAIRS)}
 
@@ -476,12 +476,10 @@
     states[0] = held_state
 
     def take(n, carry):
-        for u in range(16):
-            b = n * 16 + u
-            grads[pl.ds(b, 1), :] = came[pl.ds(where_ref[b], 1), :]
+        pick_rows(grads, n * CAP, came, where_ref, n * CAP)
         return carry
 
-    lax.fori_loop(0, BAGS // 16, take, 0)
+    lax.fori_loop(0, BAGS // CAP, take, 0)
     for q in range(BAGS // 128):
         here = slice(q * 128, (q + 1) * 128)
         hi, lo = split(grads[here, :].T)

time: 134 us -> 130 us (0.970)
  Pallas kernels: 114 us -> 109 us
    pallas_call x1, Pallas kernels: 53.7 us -> 50 us  [on_device(): pl.pallas_call(update_kernel, out_shape=(jax.ShapeDtypeStruct((ROWS, E),...]
  transfers between devices with their start and end apart: 4 -> 4, of which waited for: 2 -> 2; matrix products, arithmetic and copies ran while one was open for 4% -> 5% of each run, Pallas kernels for 10% -> 10%
where the time goes in v9:
time: 130 us
  Pallas kernels  109 us (84%)
  starting transfers between devices  5.82 us (4%)
  waiting for transfers between devices  4.84 us (4%)
  other arithmetic  3.92 us (3%)
  local copies, waits for them, and re-layouts  2.51 us (2%)
  between operations  1.72 us (1%)
    pallas_call x1, Pallas kernels, on_device(): pl.pallas_call(update_kernel, out_shape=(jax.ShapeDtypeStruct((ROWS, E),...  50 us
    pallas_call x1, Pallas kernels, on_device(): pl.pallas_call(pool_kernel, out_shape=(jax.ShapeDtypeStruct((DEVICES * CA...  40.6 us
    pallas_call x1, Pallas kernels, on_device(): pl.pallas_call(count_kernel, out_shape=jax.ShapeDtypeStruct((C_ROWS, ROWS...  13.3 us
    ppermute x4, starting transfers between devices, from_partner(): return lax.ppermute(block, 'gy', [(y, y ^ flip) for y in range(4)])  5.82 us
    ppermute x4, waiting for transfers between devices, from_partner(): return lax.ppermute(block, 'gy', [(y, y ^ flip) for y in range(4)])  4.84 us
    pallas_call x1, Pallas kernels, on_device(): pl.pallas_call(place_kernel, out_shape=jax.ShapeDtypeStruct((BAGS, E), f3...  4.15 us
    another operation x6, other arithmetic  2.75 us
  transfers between devices with their start and end apart: 4, of which 2 were waited for; matrix products, arithmetic and copies ran while one was open for 5% of the time, Pallas kernels for 10%

profile of v9, /device:TPU:1, one launch (start us, length us, event | category | flops | bytes accessed | tf_op | source)
XLA Modules:
  0.0 129.5 jit_solution(17713090524772855022)
XLA Ops:
  0.7 1.3 fusion.31
  1.9 2.1 %collective-permute-start = (f32[1024,128]{1,0:T(8,128)S(1)}, f32[1024,128]{1,0:T(8,128)S(1)}, u32[]{:S(2)}, u32[]{:S(2)}) collective-permute-start(f32[1024,128]{1,0:T(8,128)S(1)} %get-tuple-element.43), channel_id=1, source_target_pairs={{0,1},{1,0},{2,3},{3,2},{4,5},{5,4},{6,7},{7,6},{8,9},{9,8},{10,11... | collective-permute-start | bytes 1572872 | tf_op jit(solution)/shard_map/ppermute | solution.py:519
  4.0 1.8 %collective-permute-start.1 = (f32[1024,128]{1,0:T(8,128)S(1)}, f32[1024,128]{1,0:T(8,128)S(1)}, u32[]{:S(2)}, u32[]{:S(2)}) collective-permute-start(f32[1024,128]{1,0:T(8,128)S(1)} %get-tuple-element.42), channel_id=1, source_target_pairs={{0,3},{1,2},{2,1},{3,0},{4,7},{5,6},{6,5},{7,4},{8,11},{9,10},{10,... | collective-permute-start | bytes 1572872 | tf_op jit(solution)/shard_map/ppermute | solution.py:519
  6.6 0.3 reduce-window.19
  6.8 0.1 slice.47
  7.0 0.1 slice_reduce_fusion
  7.1 0.1 copy.22
  7.2 0.3 fusion.2
  7.6 0.1 broadcast_add_fusion
  7.6 0.0 copy-start.8
  7.7 0.3 copy.23
  8.0 0.3 copy-done.8
  8.4 0.6 fusion.1
  9.0 2.0 %select_convert_fusion.3 = (bf16[2048,32]{1,0:T(8,128)(2,1)S(1)}, bf16[2048,32]{1,0:T(8,128)(2,1)S(1)}, bf16[2048,32]{1,0:T(8,128)(2,1)S(1)}, bf16[2048,32]{1,0:T(8,128)(2,1)S(1)}) fusion(bf16[2048]{0:T(1024)(128)(2,1)S(1)} %get-tuple-element.50, s32[2048]{0:T(1024)S(1)} %fusion.1, bf16[2048]{0:T(1024)(128)(2,1)S(1)} %fusion.24, ...), kind=kLoop, calls=%fused_computation.8 | loop fusion | flops 327680 | bytes 548864 | tf_op jit(solution)/shard_map/convert
  11.0 0.0 copy-start.5
  11.0 1.3 convolution_convert_fusion
  12.3 0.1 fusion.13
  12.4 0.1 reshape.114.bag_in
  12.5 0.1 copy.25.label_ref
  12.6 0.1 fusion.30
  12.7 0.2 convert_reduce_fusion
  12.9 2.3 %collective-permute-done = f32[1024,128]{1,0:T(8,128)S(1)} collective-permute-done((f32[1024,128]{1,0:T(8,128)S(1)}, f32[1024,128]{1,0:T(8,128)S(1)}, u32[]{:S(2)}, u32[]{:S(2)}) %collective-permute-start) | collective-permute-done | bytes 524320 | tf_op jit(solution)/shard_map/ppermute | solution.py:519
  15.3 2.5 %collective-permute-done.1 = f32[1024,128]{1,0:T(8,128)S(1)} collective-permute-done((f32[1024,128]{1,0:T(8,128)S(1)}, f32[1024,128]{1,0:T(8,128)S(1)}, u32[]{:S(2)}, u32[]{:S(2)}) %collective-permute-start.1) | collective-permute-done | bytes 524320 | tf_op jit(solution)/shard_map/ppermute | solution.py:519
  17.8 0.1 broadcast_select_fusion
  17.9 1.9 %collective-permute-start.2 = (f32[1024,128]{1,0:T(8,128)S(1)}, f32[1024,128]{1,0:T(8,128)S(1)}, u32[]{:S(2)}, u32[]{:S(2)}) collective-permute-start(f32[1024,128]{1,0:T(8,128)S(1)} %get-tuple-element.25.a_ref), channel_id=1, source_target_pairs={{0,3},{1,2},{2,1},{3,0},{4,7},{5,6},{6,5},{7,4},{8,11},{9,10},{10,... | collective-permute-start | bytes 1572872 | tf_op jit(solution)/shard_map/ppermute | solution.py:519
  19.8 13.3 %count.1.c_ref = bf16[2304,2048]{1,0:T(8,128)(2,1)S(1)} custom-call(s32[24]{0:T(128)S(1)} %fusion.28.first_ref, s32[48,128]{1,0:T(8,128)S(1)} %bitcast.32, s32[18,128]{1,0:T(8,128)S(1)} %get-tuple-element.23.start_ref, s32[18,128]{1,0:T(8,128)S(1)} %get-tuple-element.24.end_ref), custom_call_target="tpu_custom_call" | custom-call | flops 6845104128 | bytes 10485760 | tf_op jit(solution)/shard_map/count/pallas_call | solution.py:568
  33.2 40.6 %pool.1 = (f32[4096,128]{1,0:T(8,128)S(1)}, s32[128,1,128]{2,1,0:T(1,128)S(1)}, f32[2048,128]{1,0:T(8,128)S(1)}) custom-call(s32[1]{0:T(128)S(6)} %copy.27.mask_ref, s32[4096]{0:T(1024)S(1)} %reshape.114.bag_in, s32[128,1,128]{2,1,0:T(1,128)S(1)} %bitcast.29, bf16[2304,2048]{1,0:T(8,128)(2,1)S(1)} %count.1.c_ref, f32[1024,128]{1,0:T(8,128)S(1)} %get-tuple-element.25.a_ref, ...), custom_call_target="tpu_custom_call" | custom-call | tf_op jit(solution)/shard_map/pool/pallas_call | solution.py:580
  73.7 0.0 copy-start
  73.8 0.0 copy-start.1
  73.8 4.2 %place.1.sums_ref = f32[2048,128]{1,0:T(8,128)S(1)} custom-call(s32[16384]{0:T(1024)S(1)} %bitcast.27, f32[4096,128]{1,0:T(8,128)S(1)} %get-tuple-element.28.got_ref), custom_call_target="tpu_custom_call" | custom-call | tf_op jit(solution)/shard_map/place/pallas_call | solution.py:605
  78.0 50.0 %update.1 = (f32[2048,128]{1,0:T(8,128)S(1)}, f32[1,2048]{1,0:T(1,128)S(1)}, f32[264,1024]{1,0:T(8,128)S(1)}, f32[1,1024]{1,0:T(1,128)S(1)}) custom-call(s32[1]{0:T(128)S(6)} %copy.27.mask_ref, s32[16384]{0:T(1024)S(1)} %bitcast.28, s32[2048]{0:T(1024)S(1)} %multiply_add_fusion.where_in, f32[2048,128]{1,0:T(8,128)S(1)} %place.1.sums_ref, ...), custom_call_target="tpu_custom_call" | custom-call | tf_op jit(solution)/shard_map/update/pallas_call | solution.py:615
  128.0 1.4 %finish.1 = (f32[2048,128]{1,0:T(8,128)}, f32[1,2048]{1,0:T(1,128)}, f32[264,1024]{1,0:T(8,128)}, f32[1,1024]{1,0:T(1,128)}) custom-call(f32[2048,128]{1,0:T(8,128)S(1)} %get-tuple-element.30.a, f32[1,2048]{1,0:T(1,128)S(1)} %get-tuple-element.31.b, f32[264,1024]{1,0:T(8,128)S(1)} %get-tuple-element.32.c, f32[1,1024]{1,0:T(1,128)S(1)} %get-tuple-element.33.d), custom_call_target="tpu_custom_call" | custom-call | tf_op jit(solution)/shard_map/finish/pallas_call | solution.py:673
  (29 shorter events, 0.2 us)
Async XLA Ops:
  0.6 5.9 %copy-start.7 = (s32[1,2048]{1,0:T(1,128)S(1)}, s32[1,2048]{1,0:T(1,128)}, u32[]{:S(2)}) copy-start(s32[1,2048]{1,0:T(1,128)} %param.15) | copy-start | bytes 24580
  0.6 6.4 %copy-start.6 = (s32[2048,1]{0,1:T(1,128)S(1)}, s32[2048,1]{0,1:T(1,128)}, u32[]{:S(2)}) copy-start(s32[2048,1]{0,1:T(1,128)} %param.16) | copy-start | bytes 24580
  1.9 13.3 %collective-permute-start = (f32[1024,128]{1,0:T(8,128)S(1)}, f32[1024,128]{1,0:T(8,128)S(1)}, u32[]{:S(2)}, u32[]{:S(2)}) collective-permute-start(f32[1024,128]{1,0:T(8,128)S(1)} %get-tuple-element.43), channel_id=1, source_target_pairs={{0,1},{1,0},{2,3},{3,2},{4,5},{5,4},{6,7},{7,6},{8,9},{9,8},{10,11... | collective-permute-start | bytes 1572872 | tf_op jit(solution)/shard_map/ppermute | solution.py:519
  4.0 13.7 %collective-permute-start.1 = (f32[1024,128]{1,0:T(8,128)S(1)}, f32[1024,128]{1,0:T(8,128)S(1)}, u32[]{:S(2)}, u32[]{:S(2)}) collective-permute-start(f32[1024,128]{1,0:T(8,128)S(1)} %get-tuple-element.42), channel_id=1, source_target_pairs={{0,3},{1,2},{2,1},{3,0},{4,7},{5,6},{6,5},{7,4},{8,11},{9,10},{10,... | collective-permute-start | bytes 1572872 | tf_op jit(solution)/shard_map/ppermute | solution.py:519
  7.6 0.7 copy-start.8
  11.0 1.5 %copy-start.9 = (f32[128]{0:T(128)S(1)}, f32[128]{0:T(128)}, u32[]{:S(2)}) copy-start(f32[128]{0:T(128)} %param.19) | copy-start | bytes 1540
  11.0 6.8 %copy-start.5 = (f32[2048,128]{1,0:T(8,128)S(1)}, f32[2048,128]{1,0:T(8,128)}, u32[]{:S(2)}) copy-start(f32[2048,128]{1,0:T(8,128)} %param.11) | copy-start | bytes 3145732
  17.8 2.0 %copy-start.4 = (s32[6144]{0:T(1024)S(1)}, s32[6144]{0:T(1024)}, u32[]{:S(2)}) copy-start(s32[6144]{0:T(1024)} %param.14) | copy-start | bytes 73732
  17.9 15.3 %collective-permute-start.2 = (f32[1024,128]{1,0:T(8,128)S(1)}, f32[1024,128]{1,0:T(8,128)S(1)}, u32[]{:S(2)}, u32[]{:S(2)}) collective-permute-start(f32[1024,128]{1,0:T(8,128)S(1)} %get-tuple-element.25.a_ref), channel_id=1, source_target_pairs={{0,3},{1,2},{2,1},{3,0},{4,7},{5,6},{6,5},{7,4},{8,11},{9,10},{10,... | collective-permute-start | bytes 1572872 | tf_op jit(solution)/shard_map/ppermute | solution.py:519
  19.8 13.4 %collective-permute-start.3 = (f32[1024,128]{1,0:T(8,128)S(1)}, f32[1024,128]{1,0:T(8,128)S(1)}, u32[]{:S(2)}, u32[]{:S(2)}) collective-permute-start(f32[1024,128]{1,0:T(8,128)S(1)} %get-tuple-element.26.b_ref), channel_id=1, source_target_pairs={{0,1},{1,0},{2,3},{3,2},{4,5},{5,4},{6,7},{7,6},{8,9},{9,8},{10,11... | collective-permute-start | bytes 1572872 | tf_op jit(solution)/shard_map/ppermute | solution.py:519
  73.7 4.2 %copy-start = (f32[264,1024]{1,0:T(8,128)S(1)}, f32[264,1024]{1,0:T(8,128)}, u32[]{:S(2)}) copy-start(f32[264,1024]{1,0:T(8,128)} %w_ref.1) | copy-start | bytes 3244036
  73.8 4.2 %copy-start.1 = (f32[128,128]{1,0:T(8,128)S(1)}, f32[128,128]{1,0:T(8,128)}, u32[]{:S(2)}) copy-start(f32[128,128]{1,0:T(8,128)} %dense_ref.1) | copy-start | bytes 196612
  73.8 4.2 %copy-start.2 = (f32[2048]{0:T(1024)S(1)}, f32[2048]{0:T(1024)}, u32[]{:S(2)}) copy-start(f32[2048]{0:T(1024)} %param.12) | copy-start | bytes 24580
  73.8 4.2 %copy-start.3 = (f32[1024]{0:T(1024)S(1)}, f32[1024]{0:T(1024)}, u32[]{:S(2)}) copy-start(f32[1024]{0:T(1024)} %param.21) | copy-start | bytes 12292

commit v10 on v9

--- a/solution.py
+++ b/solution.py
@@ -22,7 +22,7 @@
 HALF = G_ROWS // 2
 SEG = HALF // 48
 STRIDE = 91
-CUTS = (1, 32, 64, 96, 128)
+CUTS = (1, 12, 40, 70, 100, 128)
 PAIRS = [(i, j) for i in range(F + 1) for j in range(i + 1, F + 1)]
 PAIR_ROW = {pair: 128 + n for n, pair in enumerate(PAIRS)}
 
@@ -107,7 +107,7 @@
         pl.semaphore_signal(barrier, inc=1, device_id=device_at(peer_of(k)), device_id_type=MESH)
         return carry
 
-    lax.fori_loop(1, DEVICES, greet, 0)
+    lax.fori_loop(1, DEVICES, greet, 0, unroll=8)
 
 
 def put(src, dst, send, recv, device):
@@ -453,14 +453,15 @@
         for color in colors:
             color.finish(phase)
 
+    tables[0].wait()
+    pick_rows(came, me * CAP, pooled, slot_ref, me * 128)
+    ready(1)
+    send_rows(0)
     swap.wait()
     acc[...] = grad_ref[pl.ds(my_half, HALF), :] + r1[...]
     phase_on(0)
-    tables[0].wait()
-    pick_rows(came, me * CAP, pooled, slot_ref, me * 128)
-    ready(1)
     for phase in range(4):
-        send_rows(phase)
+        send_rows(phase + 1)
         phase_off(phase)
         phase_on(phase + 1)
 

time: 130 us -> 128 us (0.985)
  no operation moved by 1% of the time
where the time goes in v10:
time: 128 us
  Pallas kernels  108 us (84%)
  starting transfers between devices  5.82 us (5%)
  waiting for transfers between devices  4.84 us (4%)
  other arithmetic  3.92 us (3%)
  local copies, waits for them, and re-layouts  2.51 us (2%)
  between operations  1.72 us (1%)
  matrix products  1.28 us (1%)
    pallas_call x1, Pallas kernels, on_device(): pl.pallas_call(update_kernel, out_shape=(jax.ShapeDtypeStruct((ROWS, E),...  49.5 us
    pallas_call x1, Pallas kernels, on_device(): pl.pallas_call(pool_kernel, out_shape=(jax.ShapeDtypeStruct((DEVICES * CA...  39.3 us
    pallas_call x1, Pallas kernels, on_device(): pl.pallas_call(count_kernel, out_shape=jax.ShapeDtypeStruct((C_ROWS, ROWS...  13.3 us
    ppermute x4, starting transfers between devices, from_partner(): return lax.ppermute(block, 'gy', [(y, y ^ flip) for y in range(4)])  5.82 us
    ppermute x4, waiting for transfers between devices, from_partner(): return lax.ppermute(block, 'gy', [(y, y ^ flip) for y in range(4)])  4.84 us
    pallas_call x1, Pallas kernels, on_device(): pl.pallas_call(place_kernel, out_shape=jax.ShapeDtypeStruct((BAGS, E), f3...  4.15 us
    another operation x6, other arithmetic  2.75 us
  transfers between devices with their start and end apart: 4, of which 2 were waited for; matrix products, arithmetic and copies ran while one was open for 5% of the time, Pallas kernels for 10%

profile of v10, /device:TPU:1, one launch (start us, length us, event | category | flops | bytes accessed | tf_op | source)
XLA Modules:
  0.0 127.7 jit_solution(8819200824754844118)
XLA Ops:
  0.7 1.3 %fusion.31 = (f32[1024,128]{1,0:T(8,128)S(1)}, f32[1024,128]{1,0:T(8,128)S(1)}) fusion(f32[2048,128]{1,0:T(8,128)} %param.11), kind=kLoop, calls=%fused_computation.69 | loop fusion | bytes 2097152 | tf_op jit(solution)/shard_map/slice | solution.py:538
  1.9 2.1 %collective-permute-start = (f32[1024,128]{1,0:T(8,128)S(1)}, f32[1024,128]{1,0:T(8,128)S(1)}, u32[]{:S(2)}, u32[]{:S(2)}) collective-permute-start(f32[1024,128]{1,0:T(8,128)S(1)} %get-tuple-element.43), channel_id=1, source_target_pairs={{0,1},{1,0},{2,3},{3,2},{4,5},{5,4},{6,7},{7,6},{8,9},{9,8},{10,11... | collective-permute-start | bytes 1572872 | tf_op jit(solution)/shard_map/ppermute | solution.py:520
  4.0 1.8 %collective-permute-start.1 = (f32[1024,128]{1,0:T(8,128)S(1)}, f32[1024,128]{1,0:T(8,128)S(1)}, u32[]{:S(2)}, u32[]{:S(2)}) collective-permute-start(f32[1024,128]{1,0:T(8,128)S(1)} %get-tuple-element.42), channel_id=1, source_target_pairs={{0,3},{1,2},{2,1},{3,0},{4,7},{5,6},{6,5},{7,4},{8,11},{9,10},{10,... | collective-permute-start | bytes 1572872 | tf_op jit(solution)/shard_map/ppermute | solution.py:520
  6.6 0.3 reduce-window.19
  6.8 0.1 slice.47
  7.0 0.1 slice_reduce_fusion
  7.1 0.1 copy.22
  7.2 0.3 fusion.2
  7.6 0.1 broadcast_add_fusion
  7.6 0.0 copy-start.8
  7.7 0.3 copy.23
  8.0 0.3 copy-done.8
  8.4 0.6 fusion.1
  9.0 2.0 %select_convert_fusion.3 = (bf16[2048,32]{1,0:T(8,128)(2,1)S(1)}, bf16[2048,32]{1,0:T(8,128)(2,1)S(1)}, bf16[2048,32]{1,0:T(8,128)(2,1)S(1)}, bf16[2048,32]{1,0:T(8,128)(2,1)S(1)}) fusion(bf16[2048]{0:T(1024)(128)(2,1)S(1)} %get-tuple-element.50, s32[2048]{0:T(1024)S(1)} %fusion.1, bf16[2048]{0:T(1024)(128)(2,1)S(1)} %fusion.24, ...), kind=kLoop, calls=%fused_computation.8 | loop fusion | flops 327680 | bytes 548864 | tf_op jit(solution)/shard_map/convert
  11.0 0.0 copy-start.9
  11.0 1.3 %convolution_convert_fusion = s32[128,128]{1,0:T(8,128)S(1)} fusion(bf16[2048,32]{1,0:T(8,128)(2,1)S(1)} %get-tuple-element.47, bf16[2048,32]{1,0:T(8,128)(2,1)S(1)} %get-tuple-element.48, bf16[2048,32]{1,0:T(8,128)(2,1)S(1)} %get-tuple-element.49, bf16[2048,32]{1,0:T(8,128)(2,1)S(1)} %get-tuple-element.46, s32[2048]{0:T(1024)S(1)} %bitcast.35), kind=kOutput, calls=%fused_computation.3 | convolution fusion | flops 70008832 | bytes 598016 | tf_op jit(solution)/shard_map/dot_general | solution.py:45
  12.3 0.1 fusion.13
  12.4 0.1 reshape.114.bag_in
  12.5 0.1 copy.25.label_ref
  12.6 0.1 fusion.30
  12.7 0.2 convert_reduce_fusion
  12.9 2.3 %collective-permute-done = f32[1024,128]{1,0:T(8,128)S(1)} collective-permute-done((f32[1024,128]{1,0:T(8,128)S(1)}, f32[1024,128]{1,0:T(8,128)S(1)}, u32[]{:S(2)}, u32[]{:S(2)}) %collective-permute-start) | collective-permute-done | bytes 524320 | tf_op jit(solution)/shard_map/ppermute | solution.py:520
  15.3 2.5 %collective-permute-done.1 = f32[1024,128]{1,0:T(8,128)S(1)} collective-permute-done((f32[1024,128]{1,0:T(8,128)S(1)}, f32[1024,128]{1,0:T(8,128)S(1)}, u32[]{:S(2)}, u32[]{:S(2)}) %collective-permute-start.1) | collective-permute-done | bytes 524320 | tf_op jit(solution)/shard_map/ppermute | solution.py:520
  17.8 0.1 broadcast_select_fusion
  17.9 1.9 %collective-permute-start.2 = (f32[1024,128]{1,0:T(8,128)S(1)}, f32[1024,128]{1,0:T(8,128)S(1)}, u32[]{:S(2)}, u32[]{:S(2)}) collective-permute-start(f32[1024,128]{1,0:T(8,128)S(1)} %get-tuple-element.25.a_ref), channel_id=1, source_target_pairs={{0,3},{1,2},{2,1},{3,0},{4,7},{5,6},{6,5},{7,4},{8,11},{9,10},{10,... | collective-permute-start | bytes 1572872 | tf_op jit(solution)/shard_map/ppermute | solution.py:520
  19.8 13.3 %count.1.c_ref = bf16[2304,2048]{1,0:T(8,128)(2,1)S(1)} custom-call(s32[24]{0:T(128)S(1)} %fusion.28.first_ref, s32[48,128]{1,0:T(8,128)S(1)} %bitcast.32, s32[18,128]{1,0:T(8,128)S(1)} %get-tuple-element.23.start_ref, s32[18,128]{1,0:T(8,128)S(1)} %get-tuple-element.24.end_ref), custom_call_target="tpu_custom_call" | custom-call | flops 6845104128 | bytes 10485760 | tf_op jit(solution)/shard_map/count/pallas_call | solution.py:569
  33.1 39.3 %pool.1 = (f32[4096,128]{1,0:T(8,128)S(1)}, s32[128,1,128]{2,1,0:T(1,128)S(1)}, f32[2048,128]{1,0:T(8,128)S(1)}) custom-call(s32[1]{0:T(128)S(6)} %copy.27.mask_ref, s32[4096]{0:T(1024)S(1)} %reshape.114.bag_in, s32[128,1,128]{2,1,0:T(1,128)S(1)} %bitcast.29, bf16[2304,2048]{1,0:T(8,128)(2,1)S(1)} %count.1.c_ref, f32[1024,128]{1,0:T(8,128)S(1)} %get-tuple-element.25.a_ref, ...), custom_call_target="tpu_custom_call" | custom-call | tf_op jit(solution)/shard_map/pool/pallas_call | solution.py:581
  72.4 0.0 copy-start
  72.4 0.0 copy-start.1
  72.5 4.2 %place.1.sums_ref = f32[2048,128]{1,0:T(8,128)S(1)} custom-call(s32[16384]{0:T(1024)S(1)} %bitcast.27, f32[4096,128]{1,0:T(8,128)S(1)} %get-tuple-element.28.got_ref), custom_call_target="tpu_custom_call" | custom-call | tf_op jit(solution)/shard_map/place/pallas_call | solution.py:606
  76.7 49.5 %update.1 = (f32[2048,128]{1,0:T(8,128)S(1)}, f32[1,2048]{1,0:T(1,128)S(1)}, f32[264,1024]{1,0:T(8,128)S(1)}, f32[1,1024]{1,0:T(1,128)S(1)}) custom-call(s32[1]{0:T(128)S(6)} %copy.27.mask_ref, s32[16384]{0:T(1024)S(1)} %bitcast.28, s32[2048]{0:T(1024)S(1)} %multiply_add_fusion.where_in, f32[2048,128]{1,0:T(8,128)S(1)} %place.1.sums_ref, ...), custom_call_target="tpu_custom_call" | custom-call | tf_op jit(solution)/shard_map/update/pallas_call | solution.py:616
  126.2 1.4 %finish.1 = (f32[2048,128]{1,0:T(8,128)}, f32[1,2048]{1,0:T(1,128)}, f32[264,1024]{1,0:T(8,128)}, f32[1,1024]{1,0:T(1,128)}) custom-call(f32[2048,128]{1,0:T(8,128)S(1)} %get-tuple-element.30.a, f32[1,2048]{1,0:T(1,128)S(1)} %get-tuple-element.31.b, f32[264,1024]{1,0:T(8,128)S(1)} %get-tuple-element.32.c, f32[1,1024]{1,0:T(1,128)S(1)} %get-tuple-element.33.d), custom_call_target="tpu_custom_call" | custom-call | tf_op jit(solution)/shard_map/finish/pallas_call | solution.py:674
  (29 shorter events, 0.2 us)
Async XLA Ops:
  0.6 5.9 %copy-start.7 = (s32[1,2048]{1,0:T(1,128)S(1)}, s32[1,2048]{1,0:T(1,128)}, u32[]{:S(2)}) copy-start(s32[1,2048]{1,0:T(1,128)} %param.15) | copy-start | bytes 24580
  0.6 6.4 %copy-start.6 = (s32[2048,1]{0,1:T(1,128)S(1)}, s32[2048,1]{0,1:T(1,128)}, u32[]{:S(2)}) copy-start(s32[2048,1]{0,1:T(1,128)} %param.16) | copy-start | bytes 24580
  1.9 13.3 %collective-permute-start = (f32[1024,128]{1,0:T(8,128)S(1)}, f32[1024,128]{1,0:T(8,128)S(1)}, u32[]{:S(2)}, u32[]{:S(2)}) collective-permute-start(f32[1024,128]{1,0:T(8,128)S(1)} %get-tuple-element.43), channel_id=1, source_target_pairs={{0,1},{1,0},{2,3},{3,2},{4,5},{5,4},{6,7},{7,6},{8,9},{9,8},{10,11... | collective-permute-start | bytes 1572872 | tf_op jit(solution)/shard_map/ppermute | solution.py:520
  4.0 13.7 %collective-permute-start.1 = (f32[1024,128]{1,0:T(8,128)S(1)}, f32[1024,128]{1,0:T(8,128)S(1)}, u32[]{:S(2)}, u32[]{:S(2)}) collective-permute-start(f32[1024,128]{1,0:T(8,128)S(1)} %get-tuple-element.42), channel_id=1, source_target_pairs={{0,3},{1,2},{2,1},{3,0},{4,7},{5,6},{6,5},{7,4},{8,11},{9,10},{10,... | collective-permute-start | bytes 1572872 | tf_op jit(solution)/shard_map/ppermute | solution.py:520
  7.6 0.7 copy-start.8
  11.0 1.5 %copy-start.9 = (f32[128]{0:T(128)S(1)}, f32[128]{0:T(128)}, u32[]{:S(2)}) copy-start(f32[128]{0:T(128)} %param.19) | copy-start | bytes 1540
  11.0 6.8 %copy-start.5 = (f32[2048,128]{1,0:T(8,128)S(1)}, f32[2048,128]{1,0:T(8,128)}, u32[]{:S(2)}) copy-start(f32[2048,128]{1,0:T(8,128)} %param.11) | copy-start | bytes 3145732
  17.8 2.0 %copy-start.4 = (s32[6144]{0:T(1024)S(1)}, s32[6144]{0:T(1024)}, u32[]{:S(2)}) copy-start(s32[6144]{0:T(1024)} %param.14) | copy-start | bytes 73732
  17.9 15.2 %collective-permute-start.2 = (f32[1024,128]{1,0:T(8,128)S(1)}, f32[1024,128]{1,0:T(8,128)S(1)}, u32[]{:S(2)}, u32[]{:S(2)}) collective-permute-start(f32[1024,128]{1,0:T(8,128)S(1)} %get-tuple-element.25.a_ref), channel_id=1, source_target_pairs={{0,3},{1,2},{2,1},{3,0},{4,7},{5,6},{6,5},{7,4},{8,11},{9,10},{10,... | collective-permute-start | bytes 1572872 | tf_op jit(solution)/shard_map/ppermute | solution.py:520
  19.8 13.4 %collective-permute-start.3 = (f32[1024,128]{1,0:T(8,128)S(1)}, f32[1024,128]{1,0:T(8,128)S(1)}, u32[]{:S(2)}, u32[]{:S(2)}) collective-permute-start(f32[1024,128]{1,0:T(8,128)S(1)} %get-tuple-element.26.b_ref), channel_id=1, source_target_pairs={{0,1},{1,0},{2,3},{3,2},{4,5},{5,4},{6,7},{7,6},{8,9},{9,8},{10,11... | collective-permute-start | bytes 1572872 | tf_op jit(solution)/shard_map/ppermute | solution.py:520
  72.4 4.2 %copy-start = (f32[264,1024]{1,0:T(8,128)S(1)}, f32[264,1024]{1,0:T(8,128)}, u32[]{:S(2)}) copy-start(f32[264,1024]{1,0:T(8,128)} %w_ref.1) | copy-start | bytes 3244036
  72.4 4.2 %copy-start.1 = (f32[128,128]{1,0:T(8,128)S(1)}, f32[128,128]{1,0:T(8,128)}, u32[]{:S(2)}) copy-start(f32[128,128]{1,0:T(8,128)} %dense_ref.1) | copy-start | bytes 196612
  72.5 4.2 %copy-start.2 = (f32[2048]{0:T(1024)S(1)}, f32[2048]{0:T(1024)}, u32[]{:S(2)}) copy-start(f32[2048]{0:T(1024)} %param.12) | copy-start | bytes 24580
  72.5 4.2 %copy-start.3 = (f32[1024]{0:T(1024)S(1)}, f32[1024]{0:T(1024)}, u32[]{:S(2)}) copy-start(f32[1024]{0:T(1024)} %param.21) | copy-start | bytes 12292

commit v11 on v10

--- a/solution.py
+++ b/solution.py
@@ -107,7 +107,7 @@
         pl.semaphore_signal(barrier, inc=1, device_id=device_at(peer_of(k)), device_id_type=MESH)
         return carry
 
-    lax.fori_loop(1, DEVICES, greet, 0, unroll=8)
+    lax.fori_loop(1, DEVICES, greet, 0, unroll=32)
 
 
 def put(src, dst, send, recv, device):
@@ -188,7 +188,7 @@
         start(k - 1)
         return carry
 
-    lax.fori_loop(2, DEVICES, step, 0)
+    lax.fori_loop(2, DEVICES, step, 0, unroll=2)
     start(DEVICES - 1)
     to = device_at(peer_of(1))
     some = pl.ds(0, DEVICES - 1)
@@ -372,7 +372,7 @@
             return carry
 
         last = DEVICES - 1 if CUTS[n + 1] == DEVICES else CUTS[n + 1]
-        lax.fori_loop(CUTS[n], last, step, 0)
+        lax.fori_loop(CUTS[n], last, step, 0, unroll=2)
         if last < CUTS[n + 1]:
             start(last)
 

time: 128 us -> 128 us (level); the launches traced: 128 us -> 126 us
  Pallas kernels: 108 us -> 106 us
    pallas_call x1, Pallas kernels: 49.5 us -> 48 us  [on_device(): pl.pallas_call(update_kernel, out_shape=(jax.ShapeDtypeStruct((ROWS, E),...]
  transfers between devices with their start and end apart: 4 -> 4, of which waited for: 2 -> 2; matrix products, arithmetic and copies ran while one was open for 5% -> 5% of each run, Pallas kernels for 10% -> 11%
where the time goes in v11:
time: 128 us; the launch traced here: 126 us
  Pallas kernels  106 us (83%)
  starting transfers between devices  5.82 us (5%)
  waiting for transfers between devices  4.84 us (4%)
  other arithmetic  3.92 us (3%)
  local copies, waits for them, and re-layouts  2.51 us (2%)
  between operations  1.72 us (1%)
  matrix products  1.28 us (1%)
    pallas_call x1, Pallas kernels, on_device(): pl.pallas_call(update_kernel, out_shape=(jax.ShapeDtypeStruct((ROWS, E),...  48 us
    pallas_call x1, Pallas kernels, on_device(): pl.pallas_call(pool_kernel, out_shape=(jax.ShapeDtypeStruct((DEVICES * CA...  39.2 us
    pallas_call x1, Pallas kernels, on_device(): pl.pallas_call(count_kernel, out_shape=jax.ShapeDtypeStruct((C_ROWS, ROWS...  13.3 us
    ppermute x4, starting transfers between devices, from_partner(): return lax.ppermute(block, 'gy', [(y, y ^ flip) for y in range(4)])  5.82 us
    ppermute x4, waiting for transfers between devices, from_partner(): return lax.ppermute(block, 'gy', [(y, y ^ flip) for y in range(4)])  4.84 us
    pallas_call x1, Pallas kernels, on_device(): pl.pallas_call(place_kernel, out_shape=jax.ShapeDtypeStruct((BAGS, E), f3...  4.15 us
    another operation x6, other arithmetic  2.75 us
  transfers between devices with their start and end apart: 4, of which 2 were waited for; matrix products, arithmetic and copies ran while one was open for 5% of the time, Pallas kernels for 11%

profile of v11, /device:TPU:1, one launch (start us, length us, event | category | flops | bytes accessed | tf_op | source)
XLA Modules:
  0.0 126.2 jit_solution(17555031722034792796)
XLA Ops:
  0.7 1.3 %fusion.31 = (f32[1024,128]{1,0:T(8,128)S(1)}, f32[1024,128]{1,0:T(8,128)S(1)}) fusion(f32[2048,128]{1,0:T(8,128)} %param.11), kind=kLoop, calls=%fused_computation.69 | loop fusion | bytes 2097152 | tf_op jit(solution)/shard_map/slice | solution.py:538
  1.9 2.1 %collective-permute-start = (f32[1024,128]{1,0:T(8,128)S(1)}, f32[1024,128]{1,0:T(8,128)S(1)}, u32[]{:S(2)}, u32[]{:S(2)}) collective-permute-start(f32[1024,128]{1,0:T(8,128)S(1)} %get-tuple-element.43), channel_id=1, source_target_pairs={{0,1},{1,0},{2,3},{3,2},{4,5},{5,4},{6,7},{7,6},{8,9},{9,8},{10,11... | collective-permute-start | bytes 1572872 | tf_op jit(solution)/shard_map/ppermute | solution.py:520
  4.0 1.8 %collective-permute-start.1 = (f32[1024,128]{1,0:T(8,128)S(1)}, f32[1024,128]{1,0:T(8,128)S(1)}, u32[]{:S(2)}, u32[]{:S(2)}) collective-permute-start(f32[1024,128]{1,0:T(8,128)S(1)} %get-tuple-element.42), channel_id=1, source_target_pairs={{0,3},{1,2},{2,1},{3,0},{4,7},{5,6},{6,5},{7,4},{8,11},{9,10},{10,... | collective-permute-start | bytes 1572872 | tf_op jit(solution)/shard_map/ppermute | solution.py:520
  6.6 0.3 reduce-window.19
  6.8 0.1 slice.47
  7.0 0.1 slice_reduce_fusion
  7.1 0.1 copy.22
  7.2 0.3 fusion.2
  7.6 0.1 broadcast_add_fusion
  7.6 0.0 copy-start.8
  7.7 0.3 copy.23
  8.0 0.3 copy-done.8
  8.4 0.6 fusion.1
  9.0 2.0 %select_convert_fusion.3 = (bf16[2048,32]{1,0:T(8,128)(2,1)S(1)}, bf16[2048,32]{1,0:T(8,128)(2,1)S(1)}, bf16[2048,32]{1,0:T(8,128)(2,1)S(1)}, bf16[2048,32]{1,0:T(8,128)(2,1)S(1)}) fusion(bf16[2048]{0:T(1024)(128)(2,1)S(1)} %get-tuple-element.50, s32[2048]{0:T(1024)S(1)} %fusion.1, bf16[2048]{0:T(1024)(128)(2,1)S(1)} %fusion.24, ...), kind=kLoop, calls=%fused_computation.8 | loop fusion | flops 327680 | bytes 548864 | tf_op jit(solution)/shard_map/convert
  11.0 0.0 copy-start.9
  11.0 0.0 copy-start.5
  11.0 1.3 %convolution_convert_fusion = s32[128,128]{1,0:T(8,128)S(1)} fusion(bf16[2048,32]{1,0:T(8,128)(2,1)S(1)} %get-tuple-element.47, bf16[2048,32]{1,0:T(8,128)(2,1)S(1)} %get-tuple-element.48, bf16[2048,32]{1,0:T(8,128)(2,1)S(1)} %get-tuple-element.49, bf16[2048,32]{1,0:T(8,128)(2,1)S(1)} %get-tuple-element.46, s32[2048]{0:T(1024)S(1)} %bitcast.35), kind=kOutput, calls=%fused_computation.3 | convolution fusion | flops 70008832 | bytes 598016 | tf_op jit(solution)/shard_map/dot_general | solution.py:45
  12.3 0.1 fusion.13
  12.4 0.1 reshape.114.bag_in
  12.5 0.1 copy.25.label_ref
  12.6 0.1 fusion.30
  12.7 0.2 convert_reduce_fusion
  12.9 2.3 %collective-permute-done = f32[1024,128]{1,0:T(8,128)S(1)} collective-permute-done((f32[1024,128]{1,0:T(8,128)S(1)}, f32[1024,128]{1,0:T(8,128)S(1)}, u32[]{:S(2)}, u32[]{:S(2)}) %collective-permute-start) | collective-permute-done | bytes 524320 | tf_op jit(solution)/shard_map/ppermute | solution.py:520
  15.3 2.5 %collective-permute-done.1 = f32[1024,128]{1,0:T(8,128)S(1)} collective-permute-done((f32[1024,128]{1,0:T(8,128)S(1)}, f32[1024,128]{1,0:T(8,128)S(1)}, u32[]{:S(2)}, u32[]{:S(2)}) %collective-permute-start.1) | collective-permute-done | bytes 524320 | tf_op jit(solution)/shard_map/ppermute | solution.py:520
  17.8 0.1 broadcast_select_fusion
  17.9 1.9 %collective-permute-start.2 = (f32[1024,128]{1,0:T(8,128)S(1)}, f32[1024,128]{1,0:T(8,128)S(1)}, u32[]{:S(2)}, u32[]{:S(2)}) collective-permute-start(f32[1024,128]{1,0:T(8,128)S(1)} %get-tuple-element.25.a_ref), channel_id=1, source_target_pairs={{0,3},{1,2},{2,1},{3,0},{4,7},{5,6},{6,5},{7,4},{8,11},{9,10},{10,... | collective-permute-start | bytes 1572872 | tf_op jit(solution)/shard_map/ppermute | solution.py:520
  19.8 13.3 %count.1.c_ref = bf16[2304,2048]{1,0:T(8,128)(2,1)S(1)} custom-call(s32[24]{0:T(128)S(1)} %fusion.28.first_ref, s32[48,128]{1,0:T(8,128)S(1)} %bitcast.32, s32[18,128]{1,0:T(8,128)S(1)} %get-tuple-element.23.start_ref, s32[18,128]{1,0:T(8,128)S(1)} %get-tuple-element.24.end_ref), custom_call_target="tpu_custom_call" | custom-call | flops 6845104128 | bytes 10485760 | tf_op jit(solution)/shard_map/count/pallas_call | solution.py:569
  33.2 39.2 %pool.1 = (f32[4096,128]{1,0:T(8,128)S(1)}, s32[128,1,128]{2,1,0:T(1,128)S(1)}, f32[2048,128]{1,0:T(8,128)S(1)}) custom-call(s32[1]{0:T(128)S(6)} %copy.27.mask_ref, s32[4096]{0:T(1024)S(1)} %reshape.114.bag_in, s32[128,1,128]{2,1,0:T(1,128)S(1)} %bitcast.29, bf16[2304,2048]{1,0:T(8,128)(2,1)S(1)} %count.1.c_ref, f32[1024,128]{1,0:T(8,128)S(1)} %get-tuple-element.25.a_ref, ...), custom_call_target="tpu_custom_call" | custom-call | tf_op jit(solution)/shard_map/pool/pallas_call | solution.py:581
  72.4 0.0 copy-start
  72.4 4.2 %place.1.sums_ref = f32[2048,128]{1,0:T(8,128)S(1)} custom-call(s32[16384]{0:T(1024)S(1)} %bitcast.27, f32[4096,128]{1,0:T(8,128)S(1)} %get-tuple-element.28.got_ref), custom_call_target="tpu_custom_call" | custom-call | tf_op jit(solution)/shard_map/place/pallas_call | solution.py:606
  76.6 48.0 %update.1 = (f32[2048,128]{1,0:T(8,128)S(1)}, f32[1,2048]{1,0:T(1,128)S(1)}, f32[264,1024]{1,0:T(8,128)S(1)}, f32[1,1024]{1,0:T(1,128)S(1)}) custom-call(s32[1]{0:T(128)S(6)} %copy.27.mask_ref, s32[16384]{0:T(1024)S(1)} %bitcast.28, s32[2048]{0:T(1024)S(1)} %multiply_add_fusion.where_in, f32[2048,128]{1,0:T(8,128)S(1)} %place.1.sums_ref, ...), custom_call_target="tpu_custom_call" | custom-call | tf_op jit(solution)/shard_map/update/pallas_call | solution.py:616
  124.6 1.4 %finish.1 = (f32[2048,128]{1,0:T(8,128)}, f32[1,2048]{1,0:T(1,128)}, f32[264,1024]{1,0:T(8,128)}, f32[1,1024]{1,0:T(1,128)}) custom-call(f32[2048,128]{1,0:T(8,128)S(1)} %get-tuple-element.30.a, f32[1,2048]{1,0:T(1,128)S(1)} %get-tuple-element.31.b, f32[264,1024]{1,0:T(8,128)S(1)} %get-tuple-element.32.c, f32[1,1024]{1,0:T(1,128)S(1)} %get-tuple-element.33.d), custom_call_target="tpu_custom_call" | custom-call | tf_op jit(solution)/shard_map/finish/pallas_call | solution.py:674
  (29 shorter events, 0.2 us)
Async XLA Ops:
  0.6 5.9 %copy-start.7 = (s32[1,2048]{1,0:T(1,128)S(1)}, s32[1,2048]{1,0:T(1,128)}, u32[]{:S(2)}) copy-start(s32[1,2048]{1,0:T(1,128)} %param.15) | copy-start | bytes 24580
  0.6 6.4 %copy-start.6 = (s32[2048,1]{0,1:T(1,128)S(1)}, s32[2048,1]{0,1:T(1,128)}, u32[]{:S(2)}) copy-start(s32[2048,1]{0,1:T(1,128)} %param.16) | copy-start | bytes 24580
  1.9 13.3 %collective-permute-start = (f32[1024,128]{1,0:T(8,128)S(1)}, f32[1024,128]{1,0:T(8,128)S(1)}, u32[]{:S(2)}, u32[]{:S(2)}) collective-permute-start(f32[1024,128]{1,0:T(8,128)S(1)} %get-tuple-element.43), channel_id=1, source_target_pairs={{0,1},{1,0},{2,3},{3,2},{4,5},{5,4},{6,7},{7,6},{8,9},{9,8},{10,11... | collective-permute-start | bytes 1572872 | tf_op jit(solution)/shard_map/ppermute | solution.py:520
  4.0 13.7 %collective-permute-start.1 = (f32[1024,128]{1,0:T(8,128)S(1)}, f32[1024,128]{1,0:T(8,128)S(1)}, u32[]{:S(2)}, u32[]{:S(2)}) collective-permute-start(f32[1024,128]{1,0:T(8,128)S(1)} %get-tuple-element.42), channel_id=1, source_target_pairs={{0,3},{1,2},{2,1},{3,0},{4,7},{5,6},{6,5},{7,4},{8,11},{9,10},{10,... | collective-permute-start | bytes 1572872 | tf_op jit(solution)/shard_map/ppermute | solution.py:520
  7.6 0.7 copy-start.8
  11.0 1.5 %copy-start.9 = (f32[128]{0:T(128)S(1)}, f32[128]{0:T(128)}, u32[]{:S(2)}) copy-start(f32[128]{0:T(128)} %param.19) | copy-start | bytes 1540
  11.0 6.8 %copy-start.5 = (f32[2048,128]{1,0:T(8,128)S(1)}, f32[2048,128]{1,0:T(8,128)}, u32[]{:S(2)}) copy-start(f32[2048,128]{1,0:T(8,128)} %param.11) | copy-start | bytes 3145732
  17.8 2.0 %copy-start.4 = (s32[6144]{0:T(1024)S(1)}, s32[6144]{0:T(1024)}, u32[]{:S(2)}) copy-start(s32[6144]{0:T(1024)} %param.14) | copy-start | bytes 73732
  17.9 15.3 %collective-permute-start.2 = (f32[1024,128]{1,0:T(8,128)S(1)}, f32[1024,128]{1,0:T(8,128)S(1)}, u32[]{:S(2)}, u32[]{:S(2)}) collective-permute-start(f32[1024,128]{1,0:T(8,128)S(1)} %get-tuple-element.25.a_ref), channel_id=1, source_target_pairs={{0,3},{1,2},{2,1},{3,0},{4,7},{5,6},{6,5},{7,4},{8,11},{9,10},{10,... | collective-permute-start | bytes 1572872 | tf_op jit(solution)/shard_map/ppermute | solution.py:520
  19.8 13.4 %collective-permute-start.3 = (f32[1024,128]{1,0:T(8,128)S(1)}, f32[1024,128]{1,0:T(8,128)S(1)}, u32[]{:S(2)}, u32[]{:S(2)}) collective-permute-start(f32[1024,128]{1,0:T(8,128)S(1)} %get-tuple-element.26.b_ref), channel_id=1, source_target_pairs={{0,1},{1,0},{2,3},{3,2},{4,5},{5,4},{6,7},{7,6},{8,9},{9,8},{10,11... | collective-permute-start | bytes 1572872 | tf_op jit(solution)/shard_map/ppermute | solution.py:520
  72.4 4.2 %copy-start = (f32[264,1024]{1,0:T(8,128)S(1)}, f32[264,1024]{1,0:T(8,128)}, u32[]{:S(2)}) copy-start(f32[264,1024]{1,0:T(8,128)} %w_ref.1) | copy-start | bytes 3244036
  72.4 4.2 %copy-start.1 = (f32[128,128]{1,0:T(8,128)S(1)}, f32[128,128]{1,0:T(8,128)}, u32[]{:S(2)}) copy-start(f32[128,128]{1,0:T(8,128)} %dense_ref.1) | copy-start | bytes 196612
  72.4 4.2 %copy-start.2 = (f32[2048]{0:T(1024)S(1)}, f32[2048]{0:T(1024)}, u32[]{:S(2)}) copy-start(f32[2048]{0:T(1024)} %param.12) | copy-start | bytes 24580
  72.4 4.2 %copy-start.3 = (f32[1024]{0:T(1024)S(1)}, f32[1024]{0:T(1024)}, u32[]{:S(2)}) copy-start(f32[1024]{0:T(1024)} %param.21) | copy-start | bytes 12292
